TPU v7x, 128 devices: a whole 4x4x4 slice. The times are simulated.
128 devices in a mesh: tm: 16 (over z, y), roll: 8 (over x, core).
Axes of the slice: x: 4, y: 4, z: 4, core: 2. Of those that a mesh axis runs over, the one named last changes fastest.
Arguments:
- inputs: bfloat16 [8, 128, 32, 2048], P('roll', 'tm'), may hold values from -30 to 30
- cotangent: bfloat16 [8, 128, 32, 2048], P('roll', 'tm'), may hold values from -6 to 6
- memory_lists: int32 [8, 128, 8], P('roll', 'tm'), may hold values from -1 to 119, as said below
- w_query: bfloat16 [2048, 1024], replicated, may hold values from -1 to 1
- w_key: bfloat16 [2048, 1024], replicated, may hold values from -1 to 1
- w_value: bfloat16 [2048, 1024], replicated, may hold values from -0.125 to 0.125
- w_output: bfloat16 [1024, 2048], replicated, may hold values from -0.1875 to 0.1875
Outputs:
- attended: bfloat16 [8, 128, 32, 2048], P('roll', 'tm')
- grad_input: bfloat16 [8, 128, 32, 2048], P('roll', 'tm')
- grad_w_query: float32 [2048, 1024], P('tm')
- grad_w_key: float32 [2048, 1024], P('tm')
- grad_w_value: float32 [2048, 1024], P('tm')
- grad_w_output: float32 [1024, 2048], P('tm')
Inputs may be any that keep to these rules, and one draw needn't show every extreme that they name: `memory_lists`: every entry is -1 or a frame of the same rollout that lies in an earlier block of 8 frames and before frame f - 4. The frames named in one list differ, and -1 entries come after them. The frames of one block name at most 3 distinct frames of any other block, and exactly 3 of the block just before theirs.
All inputs are finite; a program needn't handle non-finite values.
Results may differ from a plain program's by a relative error of at most 0.02.
Values may be sent and summed in bfloat16 or wider, within the bound.
No kernel may reach another device: no remote copies, remote signals or barrier semaphores. Data moves between devices by JAX's collectives and lax.ppermute only.
A program may use at most 192 MiB of HBM per device.

v0:
```python
import jax
import jax.numpy as jnp
from jax import lax
from jax.experimental import pallas as pl
from jax.experimental.pallas import tpu as pltpu
from jax.sharding import PartitionSpec as P


HEADS = 8
HEAD = 128
BAND = 4
MEM = 8
CAP = 3
FRAMES = 8
TOK = 32
BLOCKS = 16
ROWS = FRAMES * TOK
SPLIT = (5, 3)
KEYS = (BAND + 1 + MEM) * TOK
CHIPS = 4
SPARE = BLOCKS * CAP
masked_score = -1e30
f32, bf16 = jnp.float32, jnp.bfloat16
VMEM_LIMIT = 60 * 1024 * 1024


def params(n=1):
    return pltpu.CompilerParams(
        dimension_semantics=("arbitrary",) * n, vmem_limit_bytes=VMEM_LIMIT
    )


def dot_last(left, right):
    return lax.dot_general(left, right, (((1,), (1,)), ((), ())), preferred_element_type=f32)


def dot_first(left, right):
    return lax.dot_general(left, right, (((0,), (0,)), ((), ())), preferred_element_type=f32)


def dot(left, right):
    return lax.dot_general(left, right, (((1,), (0,)), ((), ())), preferred_element_type=f32)


def keyval_body(x_ref, wk_ref, wv_ref, out_ref):
    pieces = []
    for h in range(wk_ref.shape[1] // HEAD):
        pieces += [wk_ref[:, h * HEAD : (h + 1) * HEAD], wv_ref[:, h * HEAD : (h + 1) * HEAD]]
    out_ref[...] = dot(x_ref[...], jnp.concatenate(pieces, axis=1)).astype(bf16)


def keyval_rows(x, w_key, w_value):
    rows, width = x.shape
    cols = 256
    return pl.pallas_call(
        keyval_body,
        grid=(w_key.shape[1] // cols,),
        in_specs=[
            pl.BlockSpec((rows, width), lambda j: (0, 0)),
            pl.BlockSpec((width, cols), lambda j: (0, j)),
            pl.BlockSpec((width, cols), lambda j: (0, j)),
        ],
        out_specs=pl.BlockSpec((rows, 2 * cols), lambda j: (0, j)),
        out_shape=jax.ShapeDtypeStruct((rows, 2 * w_key.shape[1]), bf16),
        compiler_params=params(),
        name="keyval",
    )(x, w_key, w_value)


def send_body(pick_ref, kv_ref, out_ref, sem):
    def copy(i):
        at = pl.multiple_of(pick_ref[i] * TOK, TOK)
        return pltpu.make_async_copy(
            kv_ref.at[pl.ds(at, TOK), :], out_ref.at[pl.ds(i * TOK, TOK), :], sem.at[i]
        )

    for i in range(BLOCKS * CAP):
        copy(i).start()
    for i in range(BLOCKS * CAP):
        copy(i).wait()


def named_frames(pick, kv):
    width = kv.shape[1]
    return pl.pallas_call(
        send_body,
        grid_spec=pltpu.PrefetchScalarGridSpec(
            num_scalar_prefetch=1,
            grid=(1,),
            in_specs=[pl.BlockSpec((ROWS, width), lambda i, *_: (0, 0))],
            out_specs=pl.BlockSpec(memory_space=pl.ANY),
            scratch_shapes=[pltpu.SemaphoreType.DMA((BLOCKS * CAP,))],
        ),
        out_shape=jax.ShapeDtypeStruct((BLOCKS * CAP * TOK, width), bf16),
        compiler_params=params(),
        name="send",
    )(pick, kv)


def attend_body(
    read_ref, add_ref, bias_ref, q_ref, g_ref, own_ref, prev_ref, slot_ref, *refs
):
    attend_head(
        read_ref, add_ref, bias_ref, q_ref, g_ref, own_ref, prev_ref, slot_ref, *refs[-13:]
    )


def attend_head(
    read_ref, add_ref, bias_ref, q_ref, g_ref, own_ref, prev_ref, slot_ref,
    o_ref, dq_ref, down_ref, rim_ref, dslot_ref,
    acc_own, acc_prev, acc_slot, kv_scr, s_scr, gp_scr, half_scr, ds_scr,
):
    scale = HEAD ** (-0.5)
    acc_own[...] = jnp.zeros_like(acc_own)
    acc_prev[...] = jnp.zeros_like(acc_prev)
    acc_slot[...] = jnp.zeros_like(acc_slot)
    spans = [slice(f * TOK, (f + 1) * TOK) for f in range(FRAMES)]
    for f, rows in enumerate(spans):
        at = 0
        if f < BAND:
            at = (BAND - f) * TOK
            kv_scr[f, :at, :] = prev_ref[f * TOK : BAND * TOK, :]
        kv_scr[f, at : (BAND + 1) * TOK, :] = own_ref[max(f - BAND, 0) * TOK : (f + 1) * TOK, :]
        for m in range(MEM):
            at = pl.multiple_of(read_ref[f * MEM + m] * TOK, TOK)
            kv_scr[f, (BAND + 1 + m) * TOK : (BAND + 2 + m) * TOK, :] = slot_ref[pl.ds(at, TOK), :]
    for f, rows in enumerate(spans):
        s_scr[rows, :] = dot_last(q_ref[rows, :], kv_scr[f, :, :HEAD]) * scale + bias_ref[f : f + 1, :]
        gp_scr[rows, :] = dot_last(g_ref[rows, :], kv_scr[f, :, HEAD:])
    for rows in spans:
        s = s_scr[rows, :]
        gp = gp_scr[rows, :]
        e = jnp.exp(s - jnp.max(s, axis=1, keepdims=True))
        w = e * (1.0 / jnp.sum(e, axis=1, keepdims=True))
        half_scr[rows, :] = w.astype(bf16)
        ds_scr[rows, :] = (w * (gp - jnp.sum(w * gp, axis=1, keepdims=True))).astype(bf16)
    for f, rows in enumerate(spans):
        o_ref[rows, :] = dot(half_scr[rows, :], kv_scr[f, :, HEAD:]).astype(bf16)
        dq_ref[rows, :] = (dot(ds_scr[rows, :], kv_scr[f, :, :HEAD]) * scale).astype(bf16)
    for f, rows in enumerate(spans):
        dk = dot_first(ds_scr[rows, :], q_ref[rows, :]) * scale
        dv = dot_first(half_scr[rows, :], g_ref[rows, :])
        start = 0
        own = slice(max(f - BAND, 0) * TOK, (f + 1) * TOK)
        if f < BAND:
            start = (BAND - f) * TOK
            prev = slice(f * TOK, BAND * TOK)
            acc_prev[prev, :HEAD] += dk[:start]
            acc_prev[prev, HEAD:] += dv[:start]
        acc_own[own, :HEAD] += dk[start : (BAND + 1) * TOK]
        acc_own[own, HEAD:] += dv[start : (BAND + 1) * TOK]
        spots = [pl.multiple_of(add_ref[f * MEM + m] * TOK, TOK) for m in range(MEM)]
        base = (BAND + 1) * TOK
        for d, cols in ((dk, slice(0, HEAD)), (dv, slice(HEAD, 2 * HEAD))):
            olds = [acc_slot[pl.ds(at, TOK), cols] for at in spots]
            for m, at in enumerate(spots):
                acc_slot[pl.ds(at, TOK), cols] = olds[m] + d[base + m * TOK : base + (m + 1) * TOK]
    down_ref[...] = acc_own[...]
    rim_ref[...] = acc_prev[...].astype(bf16)
    dslot_ref[...] = acc_slot[: SPARE * TOK, :].astype(bf16)


def attend(read, add, bias, q, g, own, prev, slots, first, heads, written):
    col = lambda rows, width: pl.BlockSpec((rows, width), lambda h, *_: (0, h))
    src = lambda rows, width: pl.BlockSpec((rows, width), lambda h, *_: (0, h + first))
    return pl.pallas_call(
        attend_body,
        grid_spec=pltpu.PrefetchScalarGridSpec(
            num_scalar_prefetch=2,
            grid=(heads,),
            in_specs=[
                pl.BlockSpec(bias.shape, lambda h, *_: (0, 0)),
                src(ROWS, HEAD), src(ROWS, HEAD),
                src(ROWS, 2 * HEAD), src(BAND * TOK, 2 * HEAD), src(SPARE * TOK, 2 * HEAD),
            ] + [pl.BlockSpec(memory_space=pl.ANY)] * len(written),
            out_specs=[
                src(ROWS, HEAD), src(ROWS, HEAD),
                col(ROWS, 2 * HEAD), col(BAND * TOK, 2 * HEAD), col(SPARE * TOK, 2 * HEAD),
            ],
            scratch_shapes=[
                pltpu.VMEM((ROWS, 2 * HEAD), f32),
                pltpu.VMEM((BAND * TOK, 2 * HEAD), f32),
                pltpu.VMEM(((SPARE + 1) * TOK, 2 * HEAD), f32),
                pltpu.VMEM((FRAMES, KEYS, 2 * HEAD), bf16),
                pltpu.VMEM((ROWS, KEYS), f32),
                pltpu.VMEM((ROWS, KEYS), f32),
                pltpu.VMEM((ROWS, KEYS), bf16),
                pltpu.VMEM((ROWS, KEYS), bf16),
            ],
        ),
        out_shape=[
            jax.ShapeDtypeStruct(q.shape, bf16),
            jax.ShapeDtypeStruct(q.shape, bf16),
            jax.ShapeDtypeStruct((ROWS, 2 * heads * HEAD), f32),
            jax.ShapeDtypeStruct((BAND * TOK, 2 * heads * HEAD), bf16),
            jax.ShapeDtypeStruct((SPARE * TOK, 2 * heads * HEAD), bf16),
        ],
        input_output_aliases={8 + k: k for k in range(len(written))},
        compiler_params=params(),
        name="attend",
    )(read, add, bias, q, g, own, prev, slots, *written)


def collect_body(pick_ref, own_ref, rim_ref, back_ref, out_ref, acc):
    acc[:ROWS, :] = own_ref[...]
    acc[ROWS:, :] = jnp.zeros_like(acc[ROWS:, :])
    tail = slice((FRAMES - BAND) * TOK, ROWS)
    acc[tail, :] += rim_ref[...].astype(f32)
    for i in range(BLOCKS * CAP):
        at = pl.multiple_of(pick_ref[i] * TOK, TOK)
        acc[pl.ds(at, TOK), :] += back_ref[i * TOK : (i + 1) * TOK, :].astype(f32)
    for h in range(own_ref.shape[1] // (2 * HEAD)):
        for kind in range(2):
            left = (2 * h + kind) * HEAD
            out_ref[kind, :, h * HEAD : (h + 1) * HEAD] = acc[:ROWS, left : left + HEAD].astype(bf16)


def collect(pick, own, rim, back):
    width = own.shape[1]
    cols = 2 * HEAD
    col = lambda rows, w: pl.BlockSpec((rows, w), lambda h, *_: (0, h))
    return pl.pallas_call(
        collect_body,
        grid_spec=pltpu.PrefetchScalarGridSpec(
            num_scalar_prefetch=1,
            grid=(width // cols,),
            in_specs=[col(ROWS, cols), col(BAND * TOK, cols), col(SPARE * TOK, cols)],
            out_specs=pl.BlockSpec((2, ROWS, cols // 2), lambda h, *_: (0, 0, h)),
            scratch_shapes=[pltpu.VMEM((ROWS + TOK, cols), f32)],
        ),
        out_shape=jax.ShapeDtypeStruct((2, ROWS, width // 2), bf16),
        compiler_params=params(),
        name="collect",
    )(pick, own, rim, back)


LANES = HEAD


def taken(right):
    if right.ndim == 3:
        rows, n = right.shape[1:]
        return n, pl.BlockSpec((None, rows, n), lambda i, s, *_: (s[1], 0, 0))
    rows, n = right.shape
    return n // 2, pl.BlockSpec((rows, n // 2), lambda i, s, *_: (0, s[1]))


def packed_rows(rows, n):
    return rows * n // LANES


def packed(part):
    return jnp.concatenate([part[:, at : at + LANES] for at in range(0, part.shape[1], LANES)], axis=0)


def partial_call(pairs, scalars, got=None, by_chip=True, extra=None):
    per = 8
    steps = BLOCKS // per
    chips = CHIPS if by_chip else 1
    cuts = [taken(right) for _, right in pairs]
    across = [left.shape[0] == right.shape[-2] for left, right in pairs]
    shards = [left.shape[1 if a else 0] // BLOCKS for (left, _), a in zip(pairs, across)]
    height = sum(packed_rows(s // chips, n) for (n, _), s in zip(cuts, shards))
    keep = got is not None

    def body(chip_ref, *refs):
        factors, refs = refs[: 2 * len(pairs)], refs[2 * len(pairs) :]
        totals = refs[-len(pairs) :]
        for k, total in enumerate(totals):
            product = dot_first if across[k] else dot
            total[...] = product(factors[2 * k][...], factors[2 * k + 1][...])

        def write(half):
            for t in range(per):
                for d in range(chips):
                    c = lax.rem(chip_ref[0] + d, CHIPS) if keep and by_chip else d
                    parts = []
                    for total, shard in zip(totals, shards):
                        piece = shard // chips
                        first = t * shard + c * piece
                        if keep and by_chip:
                            first = pl.multiple_of(first, piece)
                        parts.append(packed(total[pl.ds(first, piece), :]))
                    part = parts[0] if len(parts) == 1 else jnp.concatenate(parts, axis=0)
                    if not by_chip:
                        if keep:
                            part = part + refs[0][t].astype(f32)
                        out_ref = refs[-1 - len(totals)]
                        if extra is None:
                            out_ref[t] = part.astype(bf16)
                        else:
                            more = extra.shape[1]
                            out_ref[t, :more, :] = refs[1][t]
                            out_ref[t, more:, :] = part.astype(bf16)
                    elif keep:
                        part = part + refs[0][c, t].astype(f32)
                        refs[1 + 2 * d + half][t] = part.astype(bf16)
                    else:
                        refs[0][c, t] = part.astype(bf16)

        if keep and by_chip:
            early = pl.program_id(0) < steps // 2
            pl.when(early)(lambda: write(0))
            pl.when(jnp.logical_not(early))(lambda: write(1))
        else:
            write(0)

    if by_chip:
        whole = pl.BlockSpec((CHIPS, per, height, LANES), lambda i, *_: (0, i, 0, 0))
        shape = (CHIPS, BLOCKS, height, LANES)
    else:
        whole = pl.BlockSpec((per, height, LANES), lambda i, *_: (i, 0, 0))
        shape = (BLOCKS, height, LANES)
    in_specs, operands = [], []
    for (left, right), shard, (_, spec), a in zip(pairs, shards, cuts, across):
        if a:
            in_specs += [pl.BlockSpec((left.shape[0], per * shard), lambda i, *_: (0, i)), spec]
        else:
            in_specs += [pl.BlockSpec((per * shard, left.shape[1]), lambda i, *_: (i, 0)), spec]
        operands += [left, right]
    out_specs, out_shape = whole, jax.ShapeDtypeStruct(shape, bf16)
    if keep:
        in_specs.append(whole)
        operands.append(got)
        if extra is not None:
            more = extra.shape[1]
            in_specs.append(pl.BlockSpec((per, more, LANES), lambda i, *_: (i, 0, 0)))
            operands.append(extra)
            out_specs = pl.BlockSpec((per, more + height, LANES), lambda i, *_: (i, 0, 0))
            out_shape = jax.ShapeDtypeStruct((BLOCKS, more + height, LANES), bf16)
        if by_chip:
            halves = [
                pl.BlockSpec((per, height, LANES), lambda i, *_: (jnp.minimum(i, steps // 2 - 1), 0, 0)),
                pl.BlockSpec((per, height, LANES), lambda i, *_: (jnp.maximum(i - steps // 2, 0), 0, 0)),
            ]
            out_specs = halves * CHIPS
            out_shape = [jax.ShapeDtypeStruct((BLOCKS // 2, height, LANES), bf16)] * (2 * CHIPS)
    return pl.pallas_call(
        body,
        grid_spec=pltpu.PrefetchScalarGridSpec(
            num_scalar_prefetch=1,
            grid=(steps,),
            in_specs=in_specs,
            out_specs=out_specs,
            scratch_shapes=[
                pltpu.VMEM((per * s, n), f32) for (n, _), s in zip(cuts, shards)
            ],
        ),
        out_shape=out_shape,
        compiler_params=params(),
    )(scalars, *operands)


def other_core(x):
    return lax.ppermute(x, "roll", [(i, i ^ 1) for i in range(lax.axis_size("roll"))])


def from_behind(block, distance):
    return lax.ppermute(
        block, "tm", [(i - distance, i) for i in range(BLOCKS) if 0 <= i - distance < BLOCKS]
    )


def exchange(x, axis="tm", groups=None):
    return lax.all_to_all(
        x, axis, split_axis=0, concat_axis=0, tiled=True, axis_index_groups=groups
    )


def summed(parts):
    return jnp.sum(parts.astype(f32), axis=0).astype(bf16)


def along_chips(x, d):
    n = 2 * CHIPS
    return lax.ppermute(x, "roll", [(i, (i + 2 * d) % n) for i in range(n)])


def plus(a, b):
    return (a.astype(f32) + b.astype(f32)).astype(bf16)


def over_chips(pieces):
    own0, own1, next0, next1, far0, far1, last0, last1 = pieces
    up, down = along_chips(far0, 1), along_chips(far1, -1)
    from_next, from_last = along_chips(next1, 1), along_chips(last0, -1)
    came0 = along_chips(plus(next0, up), 1)
    came1 = along_chips(plus(last1, down), -1)
    half0 = own0.astype(f32) + from_last.astype(f32) + came0.astype(f32)
    half1 = own1.astype(f32) + from_next.astype(f32) + came1.astype(f32)
    return jnp.concatenate([half0.astype(bf16), half1.astype(bf16)], axis=0)


def everyone(x, ordered, scalars):
    came = [x] + [along_chips(x, d) for d in range(1, CHIPS)]
    rows = x.shape[0]

    def body(s_ref, *refs):
        out_ref = refs[-1]
        for d in range(CHIPS):
            at = pl.multiple_of(lax.rem(s_ref[0] + CHIPS - d, CHIPS) * ordered, ordered)
            out_ref[pl.ds(at, ordered), :] = refs[d][:ordered, :]
        if ordered < rows:
            total = refs[0][ordered:, :].astype(f32)
            for d in range(1, CHIPS):
                total = total + refs[d][ordered:, :].astype(f32)
            out_ref[CHIPS * ordered :, :] = total.astype(bf16)

    height = CHIPS * ordered + rows - ordered
    whole = lambda n: pl.BlockSpec((n, LANES), lambda i, *_: (0, 0))
    mine = pl.pallas_call(
        body,
        grid_spec=pltpu.PrefetchScalarGridSpec(
            num_scalar_prefetch=1, grid=(1,), in_specs=[whole(rows)] * CHIPS, out_specs=whole(height)
        ),
        out_shape=jax.ShapeDtypeStruct((height, LANES), bf16),
        compiler_params=params(),
        name="gathered",
    )(scalars, *came)
    other = other_core(mine)
    return mine, other


def assembled(mine, other, scalars, shapes, places):
    height = mine.shape[0]

    def body(s_ref, mine_ref, other_ref, *out_refs):
        def write(sources):
            for core, source in enumerate(sources):
                for k, row, column, at, rows in places[core]:
                    out_refs[k][row : row + rows, column : column + LANES] = source[at : at + rows, :].astype(f32)

        pl.when(s_ref[1] == 0)(lambda: write((mine_ref, other_ref)))
        pl.when(s_ref[1] == 1)(lambda: write((other_ref, mine_ref)))

    whole = lambda shape: pl.BlockSpec(shape, lambda i, *_: (0, 0))
    return pl.pallas_call(
        body,
        grid_spec=pltpu.PrefetchScalarGridSpec(
            num_scalar_prefetch=1, grid=(1,),
            in_specs=[whole((height, LANES))] * 2, out_specs=[whole(s) for s in shapes],
        ),
        out_shape=[jax.ShapeDtypeStruct(s, f32) for s in shapes],
        compiler_params=params(),
    )(scalars, mine, other)


def slots_exchange(x):
    return exchange(x.reshape(BLOCKS, CAP * TOK, x.shape[1])).reshape(x.shape)


def step(inputs, cotangent, memory_lists, w_query, w_key, w_value, w_output):
    model_width = inputs.shape[-1]
    inner = w_query.shape[1]
    half = inner // 2
    position = lax.axis_index("tm")
    core = lax.axis_index("roll") % 2
    chip = lax.axis_index("roll") // 2
    keeping = jnp.stack([chip, core]).astype(jnp.int32)
    sending = jnp.stack([chip, 1 - core]).astype(jnp.int32)
    x = inputs.reshape(ROWS, model_width)
    cot = cotangent.reshape(ROWS, model_width)
    x_t = x.T
    recalled = memory_lists[0]
    first_frame = position * FRAMES

    targets = jnp.arange(BLOCKS * FRAMES, dtype=jnp.int32)
    wanted = jnp.any(recalled.reshape(-1, 1) == targets[None, :], axis=0)
    wanted = wanted.astype(jnp.int32).reshape(BLOCKS, FRAMES)
    asked = exchange(wanted)

    x_before = from_behind(x[(FRAMES - BAND) * TOK :], 1)
    keyval = keyval_rows(x, w_key, w_value)
    before = keyval_rows(x_before, w_key, w_value)
    queries = jnp.dot(x, w_query, preferred_element_type=f32).astype(bf16)
    grad_heads = dot_last(cot, w_output).astype(bf16)

    slot_rank = jnp.cumsum(wanted, axis=1) - 1
    slot_table = (jnp.arange(BLOCKS, dtype=jnp.int32)[:, None] * CAP + slot_rank).reshape(-1)
    mem_ok = recalled >= 0
    flat = jnp.where(mem_ok, recalled, 0).reshape(-1)
    hit = flat[:, None] == targets[None, :]
    slot_ids = jnp.sum(jnp.where(hit, slot_table[None, :], 0), axis=1)
    ok_flat = mem_ok.reshape(-1)
    read = jnp.clip(jnp.where(ok_flat, slot_ids, 0), 0, SPARE - 1)
    add = jnp.clip(jnp.where(ok_flat, slot_ids, SPARE), 0, SPARE)
    band_index = (
        jnp.arange(FRAMES, dtype=jnp.int32)[:, None] + jnp.arange(BAND + 1, dtype=jnp.int32)[None, :]
    )
    band_ok = first_frame + band_index - BAND >= 0
    key_valid = jnp.concatenate([band_ok, mem_ok], axis=1)
    bias = jnp.repeat(jnp.where(key_valid, 0.0, masked_score).astype(f32), TOK, axis=1)

    asked_rank = jnp.cumsum(asked, axis=1) - 1
    places = jnp.arange(CAP, dtype=jnp.int32)[None, :, None]
    chosen = (asked[:, None, :] > 0) & (asked_rank[:, None, :] == places)
    frame_no = jnp.arange(FRAMES, dtype=jnp.int32)[None, None, :]
    pick = jnp.sum(jnp.where(chosen, frame_no, 0), axis=2).reshape(-1)
    pick_add = jnp.where(jnp.any(chosen, axis=2).reshape(-1), pick, FRAMES)

    outgoing = named_frames(pick, keyval)
    slots = slots_exchange(outgoing)
    owns, passed, returned = [], [], []
    written, first = (), 0
    for count in SPLIT:
        *written, own_g, rim_g, dslot_g = attend(
            read, add, bias, queries, grad_heads, keyval, before, slots, first, count, written
        )
        passed.append(from_behind(rim_g, -1))
        returned.append(slots_exchange(dslot_g))
        owns.append(own_g)
        first += count

    heads_out, grad_query = written
    sent = partial_call([(x_t, grad_query), (heads_out, cot)], sending)
    got = other_core(sent)
    kept = partial_call([(x_t, grad_query), (heads_out, cot)], keeping, got)
    sum_qo = over_chips(kept)
    share_qo = summed(exchange(sum_qo))
    mine, other = everyone(share_qo, share_qo.shape[0], keeping)
    attended = jnp.dot(heads_out, w_output, preferred_element_type=f32).astype(bf16)
    grad_input = dot_last(grad_query, w_query)
    piece, o_piece = model_width // BLOCKS // CHIPS, inner // BLOCKS // CHIPS
    half_out = model_width // 2
    places = []
    for c in range(2):
        found = []
        for j in range(CHIPS):
            at = j * share_qo.shape[0]
            for k, rows, width in ((0, piece, half), (1, o_piece, half_out)):
                for column in range(c * width, (c + 1) * width, LANES):
                    found.append((k, j * rows, column, at, rows))
                    at += rows
        places.append(found)
    total_q, total_o = assembled(
        mine, other, keeping,
        [(model_width // BLOCKS, inner), (inner // BLOCKS, model_width)], places,
    )

    dks, dvs, sums = [], [], []
    for g, count in enumerate(SPLIT):
        last = g == len(SPLIT) - 1
        dkv = collect(pick_add, owns[g], passed[g], returned[g])
        dks.append(dkv[0])
        dvs.append(dkv[1])
        sent = partial_call([(x_t, dkv)], sending, by_chip=not last)
        got = other_core(sent)
        extra = jnp.concatenate(sums, axis=1) if last else None
        kept = partial_call([(x_t, dkv)], keeping, got, not last, extra)
        if not last:
            sums.append(over_chips(kept))
    late = summed(exchange(kept))
    ordered = sum(packed_rows(piece, count * HEAD) for count in SPLIT[:-1])
    mine, other = everyone(late, ordered, keeping)
    places, shard = [], model_width // BLOCKS
    for c in range(2):
        found, first = [], sum(SPLIT[:-1])
        for j in range(CHIPS):
            for h in range(first):
                found.append((c, j * piece, h * HEAD, j * ordered + h * piece, piece))
        for h in range(first, HEADS):
            found.append((c, 0, h * HEAD, CHIPS * ordered + (h - first) * shard, shard))
        places.append(found)
    total_k, total_v = assembled(mine, other, keeping, [(shard, inner)] * 2, places)
    grad_input = (
        grad_input
        + dot_last(jnp.concatenate(dks, axis=1), w_key)
        + dot_last(jnp.concatenate(dvs, axis=1), w_value)
    )
    shape = (1, FRAMES, TOK, model_width)
    return (
        attended.reshape(shape),
        grad_input.astype(bf16).reshape(shape),
        total_q,
        total_k,
        total_v,
        total_o,
    )


def solution(mesh):
    block = P("roll", "tm", None, None)
    return jax.shard_map(
        step,
        mesh=mesh,
        in_specs=(block, block, P("roll", "tm", None), P(), P(), P(), P()),
        out_specs=(block, block, P("tm", None), P("tm", None), P("tm", None), P("tm", None)),
        check_vma=False,
    )
```

profile of v0, /device:TPU:1, one launch (start us, length us, event | category | flops | bytes accessed | tf_op | source)
XLA Modules:
  0.0 392.4 jit_solution(10518638091357134896)
XLA Ops:
  2.2 8.6 %all-to-all-start = ((s32[16,1,8]{2,1,0:T(1,128)}), s32[16,1,8]{2,1,0:T(1,128)S(1)}, u32[]{:S(2)}, u32[]{:S(2)}) async-start(s32[16,1,8]{2,1,0:T(1,128)} %bitcast.4), calls=%async_computation | async-start | bytes 16384 | tf_op jit(solution)/shard_map/all_to_all | solution.py:365
  10.8 6.6 %keyval.2.kv_ref.own_ref = bf16[256,2048]{1,0:T(8,128)(2,1)} custom-call(bf16[256,2048]{1,0:T(8,128)(2,1)} %bitcast.47, bf16[2048,1024]{1,0:T(8,128)(2,1)} %wk_ref.3, bf16[2048,1024]{1,0:T(8,128)(2,1)} %wv_ref.3), custom_call_target="tpu_custom_call" | custom-call | tf_op jit(solution)/shard_map/keyval/pallas_call | solution.py:55
  18.4 5.0 %send.1 = bf16[1536,2048]{1,0:T(8,128)(2,1)} custom-call(s32[48]{0:T(128)} %reshape.115.pick_ref, bf16[256,2048]{1,0:T(8,128)(2,1)} %keyval.2.kv_ref.own_ref), custom_call_target="tpu_custom_call" | custom-call | tf_op jit(solution)/shard_map/send/pallas_call | solution.py:85
  23.5 6.8 %all-to-all-start.1 = ((bf16[16,96,2048]{2,1,0:T(8,128)(2,1)}), bf16[16,96,2048]{2,1,0:T(8,128)(2,1)}, u32[]{:S(2)}, u32[]{:S(2)}) async-start(bf16[16,96,2048]{2,1,0:T(8,128)(2,1)} %bitcast.45), calls=%async_computation.1 | async-start | bytes 12582912 | tf_op jit(solution)/shard_map/all_to_all | solution.py:365
  35.1 4.2 %convolution_convert_fusion.2.q_ref = bf16[256,1024]{1,0:T(8,128)(2,1)} fusion(bf16[256,2048]{1,0:T(8,128)(2,1)S(1)} %bitcast.48, bf16[2048,1024]{1,0:T(8,128)(2,1)} %param.10), kind=kOutput, calls=%fused_computation.5 | convolution fusion | flops 1074003968 | bytes 5767168 | tf_op jit(solution)/shard_map/dot_general | solution.py:475
  40.1 4.3 %convolution_convert_fusion.1.g_ref = bf16[256,1024]{1,0:T(8,128)(2,1)} fusion(bf16[256,2048]{1,0:T(8,128)(2,1)S(1)} %bitcast.52, bf16[1024,2048]{1,0:T(8,128)(2,1)} %param.13), kind=kOutput, calls=%fused_computation.4 | convolution fusion | flops 1074003968 | bytes 5767168 | tf_op jit(solution)/shard_map/dot_general | solution.py:34
  44.4 78.7 %collective-permute-done.x_ref = bf16[128,2048]{1,0:T(8,128)(2,1)S(1)} collective-permute-done((bf16[128,2048]{1,0:T(8,128)(2,1)S(1)}, bf16[128,2048]{1,0:T(8,128)(2,1)S(1)}, u32[]{:S(2)}, u32[]{:S(2)}) %collective-permute-start) | collective-permute-done | bytes 524320 | tf_op jit(solution)/shard_map/ppermute | solution.py:359
  123.9 5.7 %keyval.3.prev_ref = bf16[128,2048]{1,0:T(8,128)(2,1)} custom-call(bf16[128,2048]{1,0:T(8,128)(2,1)} %copy-done.10, bf16[2048,1024]{1,0:T(8,128)(2,1)} %wk_ref.3, bf16[2048,1024]{1,0:T(8,128)(2,1)} %wv_ref.3), custom_call_target="tpu_custom_call" | custom-call | tf_op jit(solution)/shard_map/keyval/pallas_call | solution.py:55
  129.6 12.6 %attend.2 = (bf16[256,1024]{1,0:T(8,128)(2,1)}, bf16[256,1024]{1,0:T(8,128)(2,1)}, f32[256,1280]{1,0:T(8,128)}, bf16[128,1280]{1,0:T(8,128)(2,1)}, bf16[1536,1280]{1,0:T(8,128)(2,1)}) custom-call(s32[64]{0:T(128)} %get-tuple-element.71.read_ref, s32[64]{0:T(128)} %get-tuple-element.70.add_ref, f32[8,416]{1,0:T(8,128)} %reshape.112.bias_ref, ...), custom_call_target="tpu_custom_call" | custom-call | tf_op jit(solution)/shard_map/attend/pallas_call | solution.py:166
  142.3 13.5 %all-to-all-start.2 = ((bf16[16,96,1280]{2,1,0:T(8,128)(2,1)}), bf16[16,96,1280]{2,1,0:T(8,128)(2,1)}, u32[]{:S(2)}, u32[]{:S(2)}) async-start(bf16[16,96,1280]{2,1,0:T(8,128)(2,1)} %bitcast.53), calls=%async_computation.2 | async-start | bytes 7864320 | tf_op jit(solution)/shard_map/all_to_all | solution.py:365
  157.8 8.8 %attend.3 = (bf16[256,1024]{1,0:T(8,128)(2,1)}, bf16[256,1024]{1,0:T(8,128)(2,1)}, f32[256,768]{1,0:T(8,128)}, bf16[128,768]{1,0:T(8,128)(2,1)}, bf16[1536,768]{1,0:T(8,128)(2,1)}) custom-call(s32[64]{0:T(128)} %get-tuple-element.71.read_ref, s32[64]{0:T(128)} %get-tuple-element.70.add_ref, ...), custom_call_target="tpu_custom_call", output_to_operand_aliasing={{0}: (8, {}), {1}: (9, {})} | custom-call | tf_op jit(solution)/shard_map/attend/pallas_call | solution.py:166
  166.5 5.0 %shard_map.118 = bf16[4,16,256,128]{3,2,1,0:T(8,128)(2,1)} custom-call(s32[2]{0:T(128)} %pad_add_fusion.1.chip_ref, bf16[2048,256]{1,0:T(8,128)(2,1)} %bitcast.39, bf16[256,1024]{1,0:T(8,128)(2,1)} %get-tuple-element.39.refs_1_, bf16[256,1024]{1,0:T(8,128)(2,1)} %get-tuple-element.38.refs_2_, bf16[256,2048]{1,0:T(8,128)(2,1)} %bitcast.50), custom_call_target="tpu_custom_call" | custom-call | tf_op jit(solution)/shard_map/pallas_call | solution.py:338
  176.2 37.0 %collective-permute-done.1.rim_ref = bf16[128,1280]{1,0:T(8,128)(2,1)S(1)} collective-permute-done((bf16[128,1280]{1,0:T(8,128)(2,1)S(1)}, bf16[128,1280]{1,0:T(8,128)(2,1)S(1)}, u32[]{:S(2)}, u32[]{:S(2)}) %collective-permute-start.1) | collective-permute-done | bytes 327712 | tf_op jit(solution)/shard_map/ppermute | solution.py:359
  213.9 6.1 %collect.2.refs_1_ = bf16[2,256,640]{2,1,0:T(8,128)(2,1)} custom-call(s32[48]{0:T(128)} %broadcast_select_fusion.pick_ref, f32[256,1280]{1,0:T(8,128)} %get-tuple-element.40.own_ref, bf16[128,1280]{1,0:T(8,128)(2,1)} %copy-done.12, bf16[1536,1280]{1,0:T(8,128)(2,1)} %bitcast.11.back_ref), custom_call_target="tpu_custom_call" | custom-call | tf_op jit(solution)/shard_map/collect/pallas_call | solution.py:222
  220.0 4.1 %shard_map.122 = bf16[4,16,160,128]{3,2,1,0:T(8,128)(2,1)} custom-call(s32[2]{0:T(128)} %pad_add_fusion.1.chip_ref, bf16[2048,256]{1,0:T(8,128)(2,1)} %bitcast.40, bf16[2,256,640]{2,1,0:T(8,128)(2,1)} %collect.2.refs_1_), custom_call_target="tpu_custom_call" | custom-call | tf_op jit(solution)/shard_map/pallas_call | solution.py:338
  227.4 4.1 %all-to-all-start.3 = ((bf16[16,96,768]{2,1,0:T(8,128)(2,1)}), bf16[16,96,768]{2,1,0:T(8,128)(2,1)S(1)}, u32[]{:S(2)}, u32[]{:S(2)}) async-start(bf16[16,96,768]{2,1,0:T(8,128)(2,1)} %bitcast.54), calls=%async_computation.3 | async-start | bytes 4718592 | tf_op jit(solution)/shard_map/all_to_all | solution.py:365
  232.1 7.0 %shard_map.119 = (bf16[8,256,128]{2,1,0:T(8,128)(2,1)}, bf16[8,256,128]{2,1,0:T(8,128)(2,1)}, bf16[8,256,128]{2,1,0:T(8,128)(2,1)}, bf16[8,256,128]{2,1,0:T(8,12...) custom-call(s32[2]{0:T(128)} %pad_add_fusion.chip_ref.s_ref, ...), custom_call_target="tpu_custom_call" | custom-call | tf_op jit(solution)/shard_map/pallas_call | solution.py:338
  243.2 10.7 %collective-permute-done.5 = bf16[8,256,128]{2,1,0:T(8,128)(2,1)S(1)} collective-permute-done((bf16[8,256,128]{2,1,0:T(8,128)(2,1)}, bf16[8,256,128]{2,1,0:T(8,128)(2,1)S(1)}, u32[]{:S(2)}, u32[]{:S(2)}) %collective-permute-start.5) | collective-permute-done | bytes 524320 | tf_op jit(solution)/shard_map/ppermute | solution.py:376
  258.9 11.6 %collective-permute-done.2.rim_ref = bf16[128,768]{1,0:T(8,128)(2,1)S(1)} collective-permute-done((bf16[128,768]{1,0:T(8,128)(2,1)S(1)}, bf16[128,768]{1,0:T(8,128)(2,1)S(1)}, u32[]{:S(2)}, u32[]{:S(2)}) %collective-permute-start.2) | collective-permute-done | bytes 196640 | tf_op jit(solution)/shard_map/ppermute | solution.py:359
  275.0 4.5 %collect.3.refs_1_ = bf16[2,256,384]{2,1,0:T(8,128)(2,1)} custom-call(s32[48]{0:T(128)} %broadcast_select_fusion.pick_ref, f32[256,768]{1,0:T(8,128)} %get-tuple-element.43.own_ref, bf16[128,768]{1,0:T(8,128)(2,1)} %copy-done.20, bf16[1536,768]{1,0:T(8,128)(2,1)} %bitcast.46), custom_call_target="tpu_custom_call" | custom-call | tf_op jit(solution)/shard_map/collect/pallas_call | solution.py:222
  286.1 5.4 %shard_map.123 = (bf16[8,160,128]{2,1,0:T(8,128)(2,1)}, bf16[8,160,128]{2,1,0:T(8,128)(2,1)}, bf16[8,160,128]{2,1,0:T(8,128)(2,1)}, bf16[8,160,128]{2,1,0:T(8,12...) custom-call(s32[2]{0:T(128)} %pad_add_fusion.chip_ref.s_ref, ...), custom_call_target="tpu_custom_call" | custom-call | tf_op jit(solution)/shard_map/pallas_call | solution.py:338
  296.8 4.5 %all-to-all-start.4 = ((bf16[16,256,128]{2,1,0:T(8,128)(2,1)}), bf16[16,256,128]{2,1,0:T(8,128)(2,1)S(1)}, u32[]{:S(2)}, u32[]{:S(2)}) async-start(bf16[16,256,128]{2,1,0:T(8,128)(2,1)} %pad_maximum_fusion), calls=%async_computation.4 | async-start | bytes 2097152 | tf_op jit(solution)/shard_map/all_to_all | solution.py:365
  306.3 3.7 collective-permute-done.16
  312.2 6.9 %collective-permute-done.19 = bf16[8,160,128]{2,1,0:T(8,128)(2,1)S(1)} collective-permute-done((bf16[8,160,128]{2,1,0:T(8,128)(2,1)S(1)}, bf16[8,160,128]{2,1,0:T(8,128)(2,1)S(1)}, u32[]{:S(2)}, u32[]{:S(2)}) %collective-permute-start.19) | collective-permute-done | bytes 327712 | tf_op jit(solution)/shard_map/ppermute | solution.py:376
  320.1 4.4 %shard_map.124 = bf16[16,544,128]{2,1,0:T(8,128)(2,1)} custom-call(s32[2]{0:T(128)} %pad_add_fusion.chip_ref.s_ref, bf16[2048,256]{1,0:T(8,128)(2,1)} %bitcast.44, bf16[2,256,384]{2,1,0:T(8,128)(2,1)} %collect.3.refs_1_, bf16[16,384,128]{2,1,0:T(8,128)(2,1)} %collective-permute-done.14.refs_2_, bf16[16,160,128]{2,1,0:T(8,128)(2,1)} %pad_maximum_fusion.1.refs_3_), custom_call_target="tpu_custom_call" | custom-call | tf_op jit(solution)/shard_map/pallas_call | solution.py:338
  325.4 5.5 %all-to-all-start.5 = ((bf16[16,544,128]{2,1,0:T(8,128)(2,1)}), bf16[16,544,128]{2,1,0:T(8,128)(2,1)S(1)}, u32[]{:S(2)}, u32[]{:S(2)}) async-start(bf16[16,544,128]{2,1,0:T(8,128)(2,1)} %shard_map.124), calls=%async_computation.5 | async-start | bytes 4456448 | tf_op jit(solution)/shard_map/all_to_all | solution.py:365
  331.0 4.5 %convolution_convert_fusion = bf16[256,2048]{1,0:T(8,128)(2,1)} fusion(bf16[256,1024]{1,0:T(8,128)(2,1)S(1)} %copy-done.5, bf16[1024,2048]{1,0:T(8,128)(2,1)} %param.13), kind=kOutput, calls=%fused_computation.3 | convolution fusion | flops 1074266112 | bytes 5767168 | tf_op jit(solution)/shard_map/dot_general | solution.py:521
  337.3 4.9 %fusion.2 = f32[256,2048]{1,0:T(8,128)} fusion(bf16[2048,1024]{1,0:T(8,128)(2,1)} %wk_ref.3, bf16[256,384]{1,0:T(8,128)(2,1)S(1)} %get-tuple-element.68, bf16[256,640]{1,0:T(8,128)(2,1)S(1)} %get-tuple-element.66), kind=kOutput, calls=%fused_computation.16 | convolution fusion | flops 1074790400 | bytes 6815744 | tf_op jit(solution)/shard_map/dot_general | solution.py:34
  344.8 14.6 %all-to-all-done.5 = bf16[16,544,128]{2,1,0:T(8,128)(2,1)S(1)} async-done(((bf16[16,544,128]{2,1,0:T(8,128)(2,1)}), bf16[16,544,128]{2,1,0:T(8,128)(2,1)S(1)}, u32[]{:S(2)}, u32[]{:S(2)}) %all-to-all-start.5) | async-done | bytes 2228256 | tf_op jit(solution)/shard_map/all_to_all | solution.py:365
  362.6 4.9 %fusion.6 = f32[256,2048]{1,0:T(8,128)} fusion(bf16[2048,1024]{1,0:T(8,128)(2,1)} %wv_ref.3, bf16[256,384]{1,0:T(8,128)(2,1)S(1)} %get-tuple-element.69, bf16[256,640]{1,0:T(8,128)(2,1)S(1)} %get-tuple-element.67), kind=kOutput, calls=%fused_computation.20 | convolution fusion | flops 1074790400 | bytes 6815744 | tf_op jit(solution)/shard_map/dot_general | solution.py:34
  371.0 5.4 %collective-permute-start.13 = (bf16[1024,128]{1,0:T(8,128)(2,1)}, bf16[1024,128]{1,0:T(8,128)(2,1)S(1)}, u32[]{:S(2)}, u32[]{:S(2)}) collective-permute-start(bf16[1024,128]{1,0:T(8,128)(2,1)} %gathered.2.mine_ref), channel_id=1, source_target_pairs={{0,1},{1,0},{2,3},{3,2},{4,5},{5,4},{6,7},{7,6},{8,9},{9,8},{10,11... | collective-permute-start | bytes 786440 | tf_op jit(solution)/shard_map/ppermute | solution.py:355
  380.4 5.1 %fusion.1 = bf16[256,2048]{1,0:T(8,128)(2,1)} fusion(f32[256,2048]{1,0:T(8,128)} %fusion.6, f32[256,2048]{1,0:T(8,128)S(1)} %copy-done.8, bf16[256,1024]{1,0:T(8,128)(2,1)S(1)} %copy-done.2, bf16[2048,1024]{1,0:T(8,128)(2,1)} %param.10), kind=kOutput, calls=%fused_computation.2 | convolution fusion | flops 1075314688 | bytes 9961472 | tf_op jit(solution)/shard_map/dot_general | solution.py:34
  (166 shorter events, 76.5 us)
Async XLA Ops:
  2.2 15.2 %all-to-all-start = ((s32[16,1,8]{2,1,0:T(1,128)}), s32[16,1,8]{2,1,0:T(1,128)S(1)}, u32[]{:S(2)}, u32[]{:S(2)}) async-start(s32[16,1,8]{2,1,0:T(1,128)} %bitcast.4), calls=%async_computation | async-start | bytes 16384 | tf_op jit(solution)/shard_map/all_to_all | solution.py:365
  23.5 106.1 %all-to-all-start.1 = ((bf16[16,96,2048]{2,1,0:T(8,128)(2,1)}), bf16[16,96,2048]{2,1,0:T(8,128)(2,1)}, u32[]{:S(2)}, u32[]{:S(2)}) async-start(bf16[16,96,2048]{2,1,0:T(8,128)(2,1)} %bitcast.45), calls=%async_computation.1 | async-start | bytes 12582912 | tf_op jit(solution)/shard_map/all_to_all | solution.py:365
  30.4 92.7 %collective-permute-start = (bf16[128,2048]{1,0:T(8,128)(2,1)S(1)}, bf16[128,2048]{1,0:T(8,128)(2,1)S(1)}, u32[]{:S(2)}, u32[]{:S(2)}) collective-permute-start(bf16[128,2048]{1,0:T(8,128)(2,1)S(1)} %bitcast.56), channel_id=1, source_target_pairs={{0,8},{8,16},{16,24},{24,32},{32,40},{40,48},{48,56},{56,64},{64,7... | collective-permute-start | bytes 1572872 | tf_op jit(solution)/shard_map/ppermute | solution.py:359
  142.3 70.9 %all-to-all-start.2 = ((bf16[16,96,1280]{2,1,0:T(8,128)(2,1)}), bf16[16,96,1280]{2,1,0:T(8,128)(2,1)}, u32[]{:S(2)}, u32[]{:S(2)}) async-start(bf16[16,96,1280]{2,1,0:T(8,128)(2,1)} %bitcast.53), calls=%async_computation.2 | async-start | bytes 7864320 | tf_op jit(solution)/shard_map/all_to_all | solution.py:365
  171.5 60.6 %collective-permute-start.3 = (bf16[4,16,256,128]{3,2,1,0:T(8,128)(2,1)}, bf16[4,16,256,128]{3,2,1,0:T(8,128)(2,1)}, u32[]{:S(2)}, u32[]{:S(2)}) collective-permute-start(bf16[4,16,256,128]{3,2,1,0:T(8,128)(2,1)} %shard_map.118), channel_id=1, source_target_pairs={{0,1},{1,0},{2,3},{3,2},{4,5},{5,4},{6,7},{7,6},{8,9},{9,8},{10,11... | collective-permute-start | bytes 12582920 | tf_op jit(solution)/shard_map/ppermute | solution.py:355
  174.1 39.1 %collective-permute-start.1 = (bf16[128,1280]{1,0:T(8,128)(2,1)S(1)}, bf16[128,1280]{1,0:T(8,128)(2,1)S(1)}, u32[]{:S(2)}, u32[]{:S(2)}) collective-permute-start(bf16[128,1280]{1,0:T(8,128)(2,1)S(1)} %copy-done.29), channel_id=1, source_target_pairs={{8,0},{16,8},{24,16},{32,24},{40,32},{48,40},{56,48},{64,56},{72,6... | collective-permute-start | bytes 983048 | tf_op jit(solution)/shard_map/ppermute | solution.py:359
  224.1 62.0 %collective-permute-start.15 = (bf16[4,16,160,128]{3,2,1,0:T(8,128)(2,1)}, bf16[4,16,160,128]{3,2,1,0:T(8,128)(2,1)}, u32[]{:S(2)}, u32[]{:S(2)}) collective-permute-start(bf16[4,16,160,128]{3,2,1,0:T(8,128)(2,1)} %shard_map.122), channel_id=1, source_target_pairs={{0,1},{1,0},{2,3},{3,2},{4,5},{5,4},{6,7},{7,6},{8,9},{9,8},{10,11... | collective-permute-start | bytes 7864328 | tf_op jit(solution)/shard_map/ppermute | solution.py:355
  227.4 46.3 %all-to-all-start.3 = ((bf16[16,96,768]{2,1,0:T(8,128)(2,1)}), bf16[16,96,768]{2,1,0:T(8,128)(2,1)S(1)}, u32[]{:S(2)}, u32[]{:S(2)}) async-start(bf16[16,96,768]{2,1,0:T(8,128)(2,1)} %bitcast.54), calls=%async_computation.3 | async-start | bytes 4718592 | tf_op jit(solution)/shard_map/all_to_all | solution.py:365
  239.2 14.7 %collective-permute-start.5 = (bf16[8,256,128]{2,1,0:T(8,128)(2,1)}, bf16[8,256,128]{2,1,0:T(8,128)(2,1)S(1)}, u32[]{:S(2)}, u32[]{:S(2)}) collective-permute-start(bf16[8,256,128]{2,1,0:T(8,128)(2,1)} %get-tuple-element.49), channel_id=1, source_target_pairs={{0,2},{1,3},{2,4},{3,5},{4,6},{5,7},{6,0},{7,1},{8,10},{9,11},{10,... | collective-permute-start | bytes 1572872 | tf_op jit(solution)/shard_map/ppermute | solution.py:376
  240.4 16.0 %collective-permute-start.8 = (bf16[8,256,128]{2,1,0:T(8,128)(2,1)}, bf16[8,256,128]{2,1,0:T(8,128)(2,1)S(1)}, u32[]{:S(2)}, u32[]{:S(2)}) collective-permute-start(bf16[8,256,128]{2,1,0:T(8,128)(2,1)} %get-tuple-element.53), channel_id=1, source_target_pairs={{0,6},{1,7},{2,0},{3,1},{4,2},{5,3},{6,4},{7,5},{8,14},{9,15},{10,... | collective-permute-start | bytes 1572872 | tf_op jit(solution)/shard_map/ppermute | solution.py:376
  241.9 41.3 %collective-permute-start.4 = (bf16[8,256,128]{2,1,0:T(8,128)(2,1)}, bf16[8,256,128]{2,1,0:T(8,128)(2,1)}, u32[]{:S(2)}, u32[]{:S(2)}) collective-permute-start(bf16[8,256,128]{2,1,0:T(8,128)(2,1)} %get-tuple-element.47), channel_id=1, source_target_pairs={{0,6},{1,7},{2,0},{3,1},{4,2},{5,3},{6,4},{7,5},{8,14},{9,15},{10,... | collective-permute-start | bytes 1572872 | tf_op jit(solution)/shard_map/ppermute | solution.py:376
  255.0 29.5 %collective-permute-start.6 = (bf16[8,256,128]{2,1,0:T(8,128)(2,1)S(1)}, bf16[8,256,128]{2,1,0:T(8,128)(2,1)}, u32[]{:S(2)}, u32[]{:S(2)}) collective-permute-start(bf16[8,256,128]{2,1,0:T(8,128)(2,1)S(1)} %add_convert_fusion.3), channel_id=1, source_target_pairs={{0,2},{1,3},{2,4},{3,5},{4,6},{5,7},{6,0},{7,1},{8,10},{9,11},{10,... | collective-permute-start | bytes 1572872 | tf_op jit(solution)/shard_map/ppermute | solution.py:376
  255.1 15.4 %collective-permute-start.2 = (bf16[128,768]{1,0:T(8,128)(2,1)S(1)}, bf16[128,768]{1,0:T(8,128)(2,1)S(1)}, u32[]{:S(2)}, u32[]{:S(2)}) collective-permute-start(bf16[128,768]{1,0:T(8,128)(2,1)S(1)} %copy-done.31), channel_id=1, source_target_pairs={{8,0},{16,8},{24,16},{32,24},{40,32},{48,40},{56,48},{64,56},{72,6... | collective-permute-start | bytes 589832 | tf_op jit(solution)/shard_map/ppermute | solution.py:359
  256.4 35.2 %collective-permute-start.7 = (bf16[8,256,128]{2,1,0:T(8,128)(2,1)}, bf16[8,256,128]{2,1,0:T(8,128)(2,1)}, u32[]{:S(2)}, u32[]{:S(2)}) collective-permute-start(bf16[8,256,128]{2,1,0:T(8,128)(2,1)} %get-tuple-element.51), channel_id=1, source_target_pairs={{0,2},{1,3},{2,4},{3,5},{4,6},{5,7},{6,0},{7,1},{8,10},{9,11},{10,... | collective-permute-start | bytes 1572872 | tf_op jit(solution)/shard_map/ppermute | solution.py:376
  271.2 20.4 %collective-permute-start.9 = (bf16[8,256,128]{2,1,0:T(8,128)(2,1)S(1)}, bf16[8,256,128]{2,1,0:T(8,128)(2,1)}, u32[]{:S(2)}, u32[]{:S(2)}) collective-permute-start(bf16[8,256,128]{2,1,0:T(8,128)(2,1)S(1)} %add_convert_fusion.1), channel_id=1, source_target_pairs={{0,6},{1,7},{2,0},{3,1},{4,2},{5,3},{6,4},{7,5},{8,14},{9,15},{10,... | collective-permute-start | bytes 1572872 | tf_op jit(solution)/shard_map/ppermute | solution.py:376
  283.2 36.9 %collective-permute-start.14 = (bf16[16,384,128]{2,1,0:T(8,128)(2,1)}, bf16[16,384,128]{2,1,0:T(8,128)(2,1)}, u32[]{:S(2)}, u32[]{:S(2)}) collective-permute-start(bf16[16,384,128]{2,1,0:T(8,128)(2,1)} %shard_map.121), channel_id=1, source_target_pairs={{0,1},{1,0},{2,3},{3,2},{4,5},{5,4},{6,7},{7,6},{8,9},{9,8},{10,11... | collective-permute-start | bytes 4718600 | tf_op jit(solution)/shard_map/ppermute | solution.py:355
  291.5 10.7 %collective-permute-start.17 = (bf16[8,160,128]{2,1,0:T(8,128)(2,1)}, bf16[8,160,128]{2,1,0:T(8,128)(2,1)S(1)}, u32[]{:S(2)}, u32[]{:S(2)}) collective-permute-start(bf16[8,160,128]{2,1,0:T(8,128)(2,1)} %get-tuple-element.58), channel_id=1, source_target_pairs={{0,2},{1,3},{2,4},{3,5},{4,6},{5,7},{6,0},{7,1},{8,10},{9,11},{10,... | collective-permute-start | bytes 983048 | tf_op jit(solution)/shard_map/ppermute | solution.py:376
  293.1 10.0 %collective-permute-start.20 = (bf16[8,160,128]{2,1,0:T(8,128)(2,1)}, bf16[8,160,128]{2,1,0:T(8,128)(2,1)S(1)}, u32[]{:S(2)}, u32[]{:S(2)}) collective-permute-start(bf16[8,160,128]{2,1,0:T(8,128)(2,1)} %get-tuple-element.62), channel_id=1, source_target_pairs={{0,6},{1,7},{2,0},{3,1},{4,2},{5,3},{6,4},{7,5},{8,14},{9,15},{10,... | collective-permute-start | bytes 983048 | tf_op jit(solution)/shard_map/ppermute | solution.py:376
  296.8 27.6 %all-to-all-start.4 = ((bf16[16,256,128]{2,1,0:T(8,128)(2,1)}), bf16[16,256,128]{2,1,0:T(8,128)(2,1)S(1)}, u32[]{:S(2)}, u32[]{:S(2)}) async-start(bf16[16,256,128]{2,1,0:T(8,128)(2,1)} %pad_maximum_fusion), calls=%async_computation.4 | async-start | bytes 2097152 | tf_op jit(solution)/shard_map/all_to_all | solution.py:365
  301.3 8.7 %collective-permute-start.16 = (bf16[8,160,128]{2,1,0:T(8,128)(2,1)}, bf16[8,160,128]{2,1,0:T(8,128)(2,1)S(1)}, u32[]{:S(2)}, u32[]{:S(2)}) collective-permute-start(bf16[8,160,128]{2,1,0:T(8,128)(2,1)} %get-tuple-element.56), channel_id=1, source_target_pairs={{0,6},{1,7},{2,0},{3,1},{4,2},{5,3},{6,4},{7,5},{8,14},{9,15},{10,... | collective-permute-start | bytes 983048 | tf_op jit(solution)/shard_map/ppermute | solution.py:376
  302.4 9.7 %collective-permute-start.18 = (bf16[8,160,128]{2,1,0:T(8,128)(2,1)S(1)}, bf16[8,160,128]{2,1,0:T(8,128)(2,1)S(1)}, u32[]{:S(2)}, u32[]{:S(2)}) collective-permute-start(bf16[8,160,128]{2,1,0:T(8,128)(2,1)S(1)} %add_convert_fusion.7), channel_id=1, source_target_pairs={{0,2},{1,3},{2,4},{3,5},{4,6},{5,7},{6,0},{7,1},{8,10},{9,11},{10,... | collective-permute-start | bytes 983048 | tf_op jit(solution)/shard_map/ppermute | solution.py:376
  303.0 16.0 %collective-permute-start.19 = (bf16[8,160,128]{2,1,0:T(8,128)(2,1)S(1)}, bf16[8,160,128]{2,1,0:T(8,128)(2,1)S(1)}, u32[]{:S(2)}, u32[]{:S(2)}) collective-permute-start(bf16[8,160,128]{2,1,0:T(8,128)(2,1)S(1)} %copy-done.30), channel_id=1, source_target_pairs={{0,2},{1,3},{2,4},{3,5},{4,6},{5,7},{6,0},{7,1},{8,10},{9,11},{10,... | collective-permute-start | bytes 983048 | tf_op jit(solution)/shard_map/ppermute | solution.py:376
  303.2 15.8 %collective-permute-start.21 = (bf16[8,160,128]{2,1,0:T(8,128)(2,1)S(1)}, bf16[8,160,128]{2,1,0:T(8,128)(2,1)S(1)}, u32[]{:S(2)}, u32[]{:S(2)}) collective-permute-start(bf16[8,160,128]{2,1,0:T(8,128)(2,1)S(1)} %add_convert_fusion.5), channel_id=1, source_target_pairs={{0,6},{1,7},{2,0},{3,1},{4,2},{5,3},{6,4},{7,5},{8,14},{9,15},{10,... | collective-permute-start | bytes 983048 | tf_op jit(solution)/shard_map/ppermute | solution.py:376
  325.4 34.0 %all-to-all-start.5 = ((bf16[16,544,128]{2,1,0:T(8,128)(2,1)}), bf16[16,544,128]{2,1,0:T(8,128)(2,1)S(1)}, u32[]{:S(2)}, u32[]{:S(2)}) async-start(bf16[16,544,128]{2,1,0:T(8,128)(2,1)} %shard_map.124), calls=%async_computation.5 | async-start | bytes 4456448 | tf_op jit(solution)/shard_map/all_to_all | solution.py:365
  337.0 25.3 %collective-permute-start.10 = (bf16[256,128]{1,0:T(8,128)(2,1)S(1)}, bf16[256,128]{1,0:T(8,128)(2,1)S(1)}, u32[]{:S(2)}, u32[]{:S(2)}) collective-permute-start(bf16[256,128]{1,0:T(8,128)(2,1)S(1)} %reduce_sum.44.refs_0_), channel_id=1, source_target_pairs={{0,2},{1,3},{2,4},{3,5},{4,6},{5,7},{6,0},{7,1},{8,10},{9,11},{10,... | collective-permute-start | bytes 196616 | tf_op jit(solution)/shard_map/ppermute | solution.py:376
  342.2 25.3 %collective-permute-start.11 = (bf16[256,128]{1,0:T(8,128)(2,1)S(1)}, bf16[256,128]{1,0:T(8,128)(2,1)S(1)}, u32[]{:S(2)}, u32[]{:S(2)}) collective-permute-start(bf16[256,128]{1,0:T(8,128)(2,1)S(1)} %reduce_sum.44.refs_0_), channel_id=1, source_target_pairs={{0,4},{1,5},{2,6},{3,7},{4,0},{5,1},{6,2},{7,3},{8,12},{9,13},{10,... | collective-permute-start | bytes 196616 | tf_op jit(solution)/shard_map/ppermute | solution.py:376
  343.7 23.8 %collective-permute-start.12 = (bf16[256,128]{1,0:T(8,128)(2,1)S(1)}, bf16[256,128]{1,0:T(8,128)(2,1)S(1)}, u32[]{:S(2)}, u32[]{:S(2)}) collective-permute-start(bf16[256,128]{1,0:T(8,128)(2,1)S(1)} %reduce_sum.44.refs_0_), channel_id=1, source_target_pairs={{0,6},{1,7},{2,0},{3,1},{4,2},{5,3},{6,4},{7,5},{8,14},{9,15},{10,... | collective-permute-start | bytes 196616 | tf_op jit(solution)/shard_map/ppermute | solution.py:376
  359.8 16.7 %collective-permute-start.22 = (bf16[544,128]{1,0:T(8,128)(2,1)S(1)}, bf16[544,128]{1,0:T(8,128)(2,1)S(1)}, u32[]{:S(2)}, u32[]{:S(2)}) collective-permute-start(bf16[544,128]{1,0:T(8,128)(2,1)S(1)} %reduce_sum.45.refs_0_), channel_id=1, source_target_pairs={{0,2},{1,3},{2,4},{3,5},{4,6},{5,7},{6,0},{7,1},{8,10},{9,11},{10,... | collective-permute-start | bytes 417800 | tf_op jit(solution)/shard_map/ppermute | solution.py:376
  359.9 16.6 %collective-permute-start.23 = (bf16[544,128]{1,0:T(8,128)(2,1)S(1)}, bf16[544,128]{1,0:T(8,128)(2,1)S(1)}, u32[]{:S(2)}, u32[]{:S(2)}) collective-permute-start(bf16[544,128]{1,0:T(8,128)(2,1)S(1)} %reduce_sum.45.refs_0_), channel_id=1, source_target_pairs={{0,4},{1,5},{2,6},{3,7},{4,0},{5,1},{6,2},{7,3},{8,12},{9,13},{10,... | collective-permute-start | bytes 417800 | tf_op jit(solution)/shard_map/ppermute | solution.py:376
  362.3 14.2 %collective-permute-start.24 = (bf16[544,128]{1,0:T(8,128)(2,1)S(1)}, bf16[544,128]{1,0:T(8,128)(2,1)S(1)}, u32[]{:S(2)}, u32[]{:S(2)}) collective-permute-start(bf16[544,128]{1,0:T(8,128)(2,1)S(1)} %reduce_sum.45.refs_0_), channel_id=1, source_target_pairs={{0,6},{1,7},{2,0},{3,1},{4,2},{5,3},{6,4},{7,5},{8,14},{9,15},{10,... | collective-permute-start | bytes 417800 | tf_op jit(solution)/shard_map/ppermute | solution.py:376
  371.0 14.5 %collective-permute-start.13 = (bf16[1024,128]{1,0:T(8,128)(2,1)}, bf16[1024,128]{1,0:T(8,128)(2,1)S(1)}, u32[]{:S(2)}, u32[]{:S(2)}) collective-permute-start(bf16[1024,128]{1,0:T(8,128)(2,1)} %gathered.2.mine_ref), channel_id=1, source_target_pairs={{0,1},{1,0},{2,3},{3,2},{4,5},{5,4},{6,7},{7,6},{8,9},{9,8},{10,11... | collective-permute-start | bytes 786440 | tf_op jit(solution)/shard_map/ppermute | solution.py:355
  380.4 8.6 %collective-permute-start.25 = (bf16[1024,128]{1,0:T(8,128)(2,1)}, bf16[1024,128]{1,0:T(8,128)(2,1)S(1)}, u32[]{:S(2)}, u32[]{:S(2)}) collective-permute-start(bf16[1024,128]{1,0:T(8,128)(2,1)} %gathered.3.mine_ref), channel_id=1, source_target_pairs={{0,1},{1,0},{2,3},{3,2},{4,5},{5,4},{6,7},{7,6},{8,9},{9,8},{10,11... | collective-permute-start | bytes 786440 | tf_op jit(solution)/shard_map/ppermute | solution.py:355
  (32 other events, 275.5 us)
where the time goes:
time: 394 us; the launch traced here: 392 us
  waiting for transfers between devices  166 us (42%)
  Pallas kernels  89.1 us (23%)
  starting transfers between devices  81.8 us (21%)
  matrix products  27.9 us (7%)
  local copies, waits for them, and re-layouts  13.5 us (3%)
  other arithmetic  12.8 us (3%)
    ppermute x3, waiting for transfers between devices, from_behind(): lax.ppermute(block, 'tm', [(i - distance, i) for i in range(BLOCKS) if 0...  127 us
    all_to_all x6, starting transfers between devices, exchange(): lax.all_to_all(x, axis, split_axis=0, concat_axis=0, tiled=True, axis_ind...  43 us
    pallas_call x6, Pallas kernels, partial_call(): pl.pallas_call(body, grid_spec=pltpu.PrefetchScalarGridSpec(num_scalar_pr...  29.5 us
    ppermute x18, waiting for transfers between devices, along_chips(): return lax.ppermute(x, 'roll', [(i, (i + 2 * d) % n) for i in range(n)])  24.1 us
    pallas_call x2, Pallas kernels, attend(): pl.pallas_call(attend_body, grid_spec=pltpu.PrefetchScalarGridSpec(num_sc...  21.4 us
    ppermute x18, starting transfers between devices, along_chips(): return lax.ppermute(x, 'roll', [(i, (i + 2 * d) % n) for i in range(n)])  20.2 us
    dot_general x4, matrix products, dot_last(): lax.dot_general(left, right, (((1,), (1,)), ((), ())), preferred_element_...  19.1 us
    all_to_all x6, waiting for transfers between devices, exchange(): lax.all_to_all(x, axis, split_axis=0, concat_axis=0, tiled=True, axis_ind...  14.6 us
  transfers between devices with their start and end apart: 32, of which 9 were waited for; matrix products, arithmetic and copies ran while one was open for 11% of the time, Pallas kernels for 18%

commit v1 on v0

--- a/solution.py
+++ b/solution.py
@@ -1,3 +1,5 @@
+import functools
+
 import jax
 import jax.numpy as jnp
 from jax import lax
@@ -15,7 +17,7 @@
 TOK = 32
 BLOCKS = 16
 ROWS = FRAMES * TOK
-SPLIT = (5, 3)
+SPLIT = (4, 4)
 KEYS = (BAND + 1 + MEM) * TOK
 CHIPS = 4
 SPARE = BLOCKS * CAP
@@ -253,7 +255,7 @@
     return jnp.concatenate([part[:, at : at + LANES] for at in range(0, part.shape[1], LANES)], axis=0)
 
 
-def partial_call(pairs, scalars, got=None, by_chip=True, extra=None):
+def partial_call(pairs, scalars, got=None, by_chip=True, extra=()):
     per = 8
     steps = BLOCKS // per
     chips = CHIPS if by_chip else 1
@@ -286,12 +288,7 @@
                         if keep:
                             part = part + refs[0][t].astype(f32)
                         out_ref = refs[-1 - len(totals)]
-                        if extra is None:
-                            out_ref[t] = part.astype(bf16)
-                        else:
-                            more = extra.shape[1]
-                            out_ref[t, :more, :] = refs[1][t]
-                            out_ref[t, more:, :] = part.astype(bf16)
+                        out_ref[t, out_ref.shape[1] - height :, :] = part.astype(bf16)
                     elif keep:
                         part = part + refs[0][c, t].astype(f32)
                         refs[1 + 2 * d + half][t] = part.astype(bf16)
@@ -304,6 +301,20 @@
             pl.when(jnp.logical_not(early))(lambda: write(1))
         else:
             write(0)
+
+        def add(half):
+            out_ref, at = refs[-1 - len(totals)], 0
+            for u, sums in enumerate(extra):
+                terms = refs[1 + 6 * u + 3 * half : 4 + 6 * u + 3 * half]
+                size = sums[0][0].shape[1]
+                for t in range(per):
+                    total = sum(term[t].astype(f32) for term in terms)
+                    out_ref[t, at : at + size, :] = total.astype(bf16)
+                at += size
+
+        if extra:
+            for half in range(2):
+                pl.when(pl.program_id(0) == half)(functools.partial(add, half))
 
     if by_chip:
         whole = pl.BlockSpec((CHIPS, per, height, LANES), lambda i, *_: (0, i, 0, 0))
@@ -322,10 +333,14 @@
     if keep:
         in_specs.append(whole)
         operands.append(got)
-        if extra is not None:
-            more = extra.shape[1]
-            in_specs.append(pl.BlockSpec((per, more, LANES), lambda i, *_: (i, 0, 0)))
-            operands.append(extra)
+        more = 0
+        for sums in extra:
+            more += sums[0][0].shape[1]
+            for term in (*sums[0], *sums[1]):
+                in_specs.append(pl.BlockSpec(term.shape, lambda i, *_: (0, 0, 0)))
+                operands.append(term)
+        if extra:
+            assert steps == 2
             out_specs = pl.BlockSpec((per, more + height, LANES), lambda i, *_: (i, 0, 0))
             out_shape = jax.ShapeDtypeStruct((BLOCKS, more + height, LANES), bf16)
         if by_chip:
@@ -351,6 +366,34 @@
     )(scalars, *operands)
 
 
+def input_gradient(dq, dkvs, w_query, w_key, w_value):
+    rows, inner = dq.shape
+    width = w_query.shape[0]
+    cut = 512
+
+    def body(dq_ref, wq_ref, wk_ref, wv_ref, *refs):
+        total = dot_last(dq_ref[...], wq_ref[...])
+        at = 0
+        for ref in refs[:-1]:
+            n = ref.shape[2]
+            for kind, weights in enumerate((wk_ref, wv_ref)):
+                total = total + dot_last(ref[kind], weights[:, at : at + n])
+            at += n
+        refs[-1][...] = total.astype(bf16)
+
+    weights = pl.BlockSpec((cut, inner), lambda j: (j, 0))
+    return pl.pallas_call(
+        body,
+        grid=(width // cut,),
+        in_specs=[pl.BlockSpec((rows, inner), lambda j: (0, 0)), weights, weights, weights]
+        + [pl.BlockSpec(d.shape, lambda j: (0, 0, 0)) for d in dkvs],
+        out_specs=pl.BlockSpec((rows, cut), lambda j: (0, j)),
+        out_shape=jax.ShapeDtypeStruct((rows, width), bf16),
+        compiler_params=params(),
+        name="input_gradient",
+    )(dq, w_query, w_key, w_value, *dkvs)
+
+
 def other_core(x):
     return lax.ppermute(x, "roll", [(i, i ^ 1) for i in range(lax.axis_size("roll"))])
 
@@ -386,9 +429,7 @@
     from_next, from_last = along_chips(next1, 1), along_chips(last0, -1)
     came0 = along_chips(plus(next0, up), 1)
     came1 = along_chips(plus(last1, down), -1)
-    half0 = own0.astype(f32) + from_last.astype(f32) + came0.astype(f32)
-    half1 = own1.astype(f32) + from_next.astype(f32) + came1.astype(f32)
-    return jnp.concatenate([half0.astype(bf16), half1.astype(bf16)], axis=0)
+    return (own0, from_last, came0), (own1, from_next, came1)
 
 
 def everyone(x, ordered, scalars):
@@ -516,61 +557,46 @@
     got = other_core(sent)
     kept = partial_call([(x_t, grad_query), (heads_out, cot)], keeping, got)
     sum_qo = over_chips(kept)
-    share_qo = summed(exchange(sum_qo))
-    mine, other = everyone(share_qo, share_qo.shape[0], keeping)
     attended = jnp.dot(heads_out, w_output, preferred_element_type=f32).astype(bf16)
-    grad_input = dot_last(grad_query, w_query)
-    piece, o_piece = model_width // BLOCKS // CHIPS, inner // BLOCKS // CHIPS
-    half_out = model_width // 2
+    dkvs, sums = [], [sum_qo]
+    for g, count in enumerate(SPLIT):
+        last = g == len(SPLIT) - 1
+        dkv = collect(pick_add, owns[g], passed[g], returned[g])
+        dkvs.append(dkv)
+        sent = partial_call([(x_t, dkv)], sending, by_chip=not last)
+        got = other_core(sent)
+        kept = partial_call([(x_t, dkv)], keeping, got, not last, sums if last else ())
+        if not last:
+            sums.append(over_chips(kept))
+    late = summed(exchange(kept))
+    grad_input = input_gradient(grad_query, dkvs, w_query, w_key, w_value)
+    ordered = sum(sums[0][0].shape[1] for sums in sums)
+    mine, other = everyone(late, ordered, keeping)
+    shard, o_shard = model_width // BLOCKS, inner // BLOCKS
+    piece, o_piece = shard // CHIPS, o_shard // CHIPS
     places = []
     for c in range(2):
-        found = []
+        found, first = [], sum(SPLIT[:-1])
         for j in range(CHIPS):
-            at = j * share_qo.shape[0]
-            for k, rows, width in ((0, piece, half), (1, o_piece, half_out)):
+            at = j * ordered
+            for k, rows, width in ((0, piece, half), (1, o_piece, model_width // 2)):
                 for column in range(c * width, (c + 1) * width, LANES):
                     found.append((k, j * rows, column, at, rows))
                     at += rows
+            for h in range(first):
+                found.append((2 + c, j * piece, h * HEAD, at, piece))
+                at += piece
+        for h in range(first, HEADS):
+            found.append((2 + c, 0, h * HEAD, CHIPS * ordered + (h - first) * shard, shard))
         places.append(found)
-    total_q, total_o = assembled(
+    total_q, total_o, total_k, total_v = assembled(
         mine, other, keeping,
-        [(model_width // BLOCKS, inner), (inner // BLOCKS, model_width)], places,
-    )
-
-    dks, dvs, sums = [], [], []
-    for g, count in enumerate(SPLIT):
-        last = g == len(SPLIT) - 1
-        dkv = collect(pick_add, owns[g], passed[g], returned[g])
-        dks.append(dkv[0])
-        dvs.append(dkv[1])
-        sent = partial_call([(x_t, dkv)], sending, by_chip=not last)
-        got = other_core(sent)
-        extra = jnp.concatenate(sums, axis=1) if last else None
-        kept = partial_call([(x_t, dkv)], keeping, got, not last, extra)
-        if not last:
-            sums.append(over_chips(kept))
-    late = summed(exchange(kept))
-    ordered = sum(packed_rows(piece, count * HEAD) for count in SPLIT[:-1])
-    mine, other = everyone(late, ordered, keeping)
-    places, shard = [], model_width // BLOCKS
-    for c in range(2):
-        found, first = [], sum(SPLIT[:-1])
-        for j in range(CHIPS):
-            for h in range(first):
-                found.append((c, j * piece, h * HEAD, j * ordered + h * piece, piece))
-        for h in range(first, HEADS):
-            found.append((c, 0, h * HEAD, CHIPS * ordered + (h - first) * shard, shard))
-        places.append(found)
-    total_k, total_v = assembled(mine, other, keeping, [(shard, inner)] * 2, places)
-    grad_input = (
-        grad_input
-        + dot_last(jnp.concatenate(dks, axis=1), w_key)
-        + dot_last(jnp.concatenate(dvs, axis=1), w_value)
+        [(shard, inner), (o_shard, model_width), (shard, inner), (shard, inner)], places,
     )
     shape = (1, FRAMES, TOK, model_width)
     return (
         attended.reshape(shape),
-        grad_input.astype(bf16).reshape(shape),
+        grad_input.reshape(shape),
         total_q,
         total_k,
         total_v,

time: 394 us -> 445 us (1.13)
  blocking collectives: 0 us -> 48.3 us
  waiting for transfers between devices: 166 us -> 196 us
  matrix products: 27.9 us -> 12.9 us
  starting transfers between devices: 81.8 us -> 69.8 us
  Pallas kernels: 89.1 us -> 93.8 us
    all_to_all x0 -> x1, blocking collectives: none -> 48.3 us  [exchange(): lax.all_to_all(x, axis, split_axis=0, concat_axis=0, tiled=True, axis_ind...]
    ppermute x18 -> x15, waiting for transfers between devices: 24.1 us -> 44.9 us  [along_chips(): return lax.ppermute(x, 'roll', [(i, (i + 2 * d) % n) for i in range(n)])]
    dot_general x4 -> x1, matrix products: 19.1 us -> 4.26 us  [dot_last(): lax.dot_general(left, right, (((1,), (1,)), ((), ())), preferred_element_...]
    pallas_call x0 -> x1, Pallas kernels: none -> 8.58 us  [input_gradient(): pl.pallas_call(body, grid=(width // cut,), in_specs=[pl.BlockSpec((rows,...]
    all_to_all x6 -> x4, starting transfers between devices: 43 us -> 34.7 us  [exchange(): lax.all_to_all(x, axis, split_axis=0, concat_axis=0, tiled=True, axis_ind...]
    all_to_all x6 -> x4, waiting for transfers between devices: 14.6 us -> 20.5 us  [exchange(): lax.all_to_all(x, axis, split_axis=0, concat_axis=0, tiled=True, axis_ind...]
    ppermute x18 -> x15, starting transfers between devices: 20.2 us -> 17.8 us  [along_chips(): return lax.ppermute(x, 'roll', [(i, (i + 2 * d) % n) for i in range(n)])]
    ppermute x5 -> x4, starting transfers between devices: 12.6 us -> 11.4 us  [other_core(): lax.ppermute(x, 'roll', [(i, i ^ 1) for i in range(lax.axis_size('roll'))])]
  transfers between devices with their start and end apart: 32 -> 26, of which waited for: 9 -> 12; matrix products, arithmetic and copies ran while one was open for 11% -> 5% of each run, Pallas kernels for 18% -> 15%
where the time goes in v1:
time: 445 us; the launch traced here: 444 us
  waiting for transfers between devices  196 us (44%)
  Pallas kernels  93.8 us (21%)
  starting transfers between devices  69.8 us (16%)
  blocking collectives  48.3 us (11%)
  matrix products  12.9 us (3%)
  local copies, waits for them, and re-layouts  12 us (3%)
  other arithmetic  10.4 us (2%)
    ppermute x3, waiting for transfers between devices, from_behind(): lax.ppermute(block, 'tm', [(i - distance, i) for i in range(BLOCKS) if 0...  130 us
    all_to_all x1, blocking collectives, exchange(): lax.all_to_all(x, axis, split_axis=0, concat_axis=0, tiled=True, axis_ind...  48.3 us
    ppermute x15, waiting for transfers between devices, along_chips(): return lax.ppermute(x, 'roll', [(i, (i + 2 * d) % n) for i in range(n)])  44.9 us
    all_to_all x4, starting transfers between devices, exchange(): lax.all_to_all(x, axis, split_axis=0, concat_axis=0, tiled=True, axis_ind...  34.7 us
    pallas_call x6, Pallas kernels, partial_call(): pl.pallas_call(body, grid_spec=pltpu.PrefetchScalarGridSpec(num_scalar_pr...  30.1 us
    pallas_call x2, Pallas kernels, attend(): pl.pallas_call(attend_body, grid_spec=pltpu.PrefetchScalarGridSpec(num_sc...  21.4 us
    all_to_all x4, waiting for transfers between devices, exchange(): lax.all_to_all(x, axis, split_axis=0, concat_axis=0, tiled=True, axis_ind...  20.5 us
    ppermute x15, starting transfers between devices, along_chips(): return lax.ppermute(x, 'roll', [(i, (i + 2 * d) % n) for i in range(n)])  17.8 us
  transfers between devices with their start and end apart: 26, of which 12 were waited for; matrix products, arithmetic and copies ran while one was open for 5% of the time, Pallas kernels for 15%

profile of v1, /device:TPU:1, one launch (start us, length us, event | category | flops | bytes accessed | tf_op | source)
XLA Modules:
  0.0 444.0 jit_solution(3012764520275440824)
XLA Ops:
  2.2 8.6 %all-to-all-start = ((s32[16,1,8]{2,1,0:T(1,128)}), s32[16,1,8]{2,1,0:T(1,128)S(1)}, u32[]{:S(2)}, u32[]{:S(2)}) async-start(s32[16,1,8]{2,1,0:T(1,128)} %bitcast.4), calls=%async_computation | async-start | bytes 16384 | tf_op jit(solution)/shard_map/all_to_all | solution.py:408
  10.8 6.6 %keyval.2.kv_ref.own_ref = bf16[256,2048]{1,0:T(8,128)(2,1)} custom-call(bf16[256,2048]{1,0:T(8,128)(2,1)} %bitcast.35, bf16[2048,1024]{1,0:T(8,128)(2,1)} %wk_ref.5, bf16[2048,1024]{1,0:T(8,128)(2,1)} %wv_ref.5), custom_call_target="tpu_custom_call" | custom-call | tf_op jit(solution)/shard_map/keyval/pallas_call | solution.py:57
  18.5 5.0 %send.1 = bf16[1536,2048]{1,0:T(8,128)(2,1)} custom-call(s32[48]{0:T(128)} %reshape.115.pick_ref, bf16[256,2048]{1,0:T(8,128)(2,1)} %keyval.2.kv_ref.own_ref), custom_call_target="tpu_custom_call" | custom-call | tf_op jit(solution)/shard_map/send/pallas_call | solution.py:87
  23.5 6.8 %all-to-all-start.1 = ((bf16[16,96,2048]{2,1,0:T(8,128)(2,1)}), bf16[16,96,2048]{2,1,0:T(8,128)(2,1)}, u32[]{:S(2)}, u32[]{:S(2)}) async-start(bf16[16,96,2048]{2,1,0:T(8,128)(2,1)} %bitcast.33), calls=%async_computation.1 | async-start | bytes 12582912 | tf_op jit(solution)/shard_map/all_to_all | solution.py:408
  35.0 4.2 convolution_convert_fusion.2.q_ref
  40.1 4.3 convolution_convert_fusion.1.g_ref
  44.4 78.7 %collective-permute-done.x_ref = bf16[128,2048]{1,0:T(8,128)(2,1)S(1)} collective-permute-done((bf16[128,2048]{1,0:T(8,128)(2,1)S(1)}, bf16[128,2048]{1,0:T(8,128)(2,1)S(1)}, u32[]{:S(2)}, u32[]{:S(2)}) %collective-permute-start) | collective-permute-done | bytes 524320 | tf_op jit(solution)/shard_map/ppermute | solution.py:402
  123.9 5.7 %keyval.3.prev_ref = bf16[128,2048]{1,0:T(8,128)(2,1)} custom-call(bf16[128,2048]{1,0:T(8,128)(2,1)} %copy-done.11, bf16[2048,1024]{1,0:T(8,128)(2,1)} %wk_ref.5, bf16[2048,1024]{1,0:T(8,128)(2,1)} %wv_ref.5), custom_call_target="tpu_custom_call" | custom-call | tf_op jit(solution)/shard_map/keyval/pallas_call | solution.py:57
  129.6 10.7 %attend.2 = (bf16[256,1024]{1,0:T(8,128)(2,1)}, bf16[256,1024]{1,0:T(8,128)(2,1)}, f32[256,1024]{1,0:T(8,128)}, bf16[128,1024]{1,0:T(8,128)(2,1)}, bf16[1536,1024]{1,0:T(8,128)(2,1)}) custom-call(s32[64]{0:T(128)} %get-tuple-element.67.read_ref, s32[64]{0:T(128)} %get-tuple-element.66.add_ref, f32[8,416]{1,0:T(8,128)} %reshape.112.bias_ref, ...), custom_call_target="tpu_custom_call" | custom-call | tf_op jit(solution)/shard_map/attend/pallas_call | solution.py:168
  140.3 13.5 %all-to-all-start.2 = ((bf16[16,96,1024]{2,1,0:T(8,128)(2,1)}), bf16[16,96,1024]{2,1,0:T(8,128)(2,1)S(1)}, u32[]{:S(2)}, u32[]{:S(2)}) async-start(bf16[16,96,1024]{2,1,0:T(8,128)(2,1)} %bitcast.41), calls=%async_computation.2 | async-start | bytes 6291456 | tf_op jit(solution)/shard_map/all_to_all | solution.py:408
  156.7 10.7 %attend.3 = (bf16[256,1024]{1,0:T(8,128)(2,1)}, bf16[256,1024]{1,0:T(8,128)(2,1)}, f32[256,1024]{1,0:T(8,128)}, bf16[128,1024]{1,0:T(8,128)(2,1)}, bf16[1536,1024]{1,0:T(8,128)(2,1)}) custom-call(s32[64]{0:T(128)} %get-tuple-element.67.read_ref, s32[64]{0:T(128)} %get-tuple-element.66.add_ref, ...), custom_call_target="tpu_custom_call", output_to_operand_aliasing={{0}: (8, {}), {1}: (9, {})} | custom-call | tf_op jit(solution)/shard_map/attend/pallas_call | solution.py:168
  167.4 4.8 %shard_map.119 = bf16[4,16,256,128]{3,2,1,0:T(8,128)(2,1)} custom-call(s32[2]{0:T(128)} %pad_add_fusion.1.chip_ref, bf16[2048,256]{1,0:T(8,128)(2,1)} %bitcast.27, bf16[256,1024]{1,0:T(8,128)(2,1)} %get-tuple-element.39.dq_ref.refs_1_, bf16[256,1024]{1,0:T(8,128)(2,1)} %get-tuple-element.38.refs_2_, bf16[256,2048]{1,0:T(8,128)(2,1)} %bitcast.38), custom_call_target="tpu_custom_call" | custom-call | tf_op jit(solution)/shard_map/pallas_call | solution.py:353
  174.8 20.5 %all-to-all-done.2 = bf16[16,96,1024]{2,1,0:T(8,128)(2,1)S(1)} async-done(((bf16[16,96,1024]{2,1,0:T(8,128)(2,1)}), bf16[16,96,1024]{2,1,0:T(8,128)(2,1)S(1)}, u32[]{:S(2)}, u32[]{:S(2)}) %all-to-all-start.2) | async-done | bytes 3145760 | tf_op jit(solution)/shard_map/all_to_all | solution.py:408
  195.3 5.8 %all-to-all-start.3 = ((bf16[16,96,1024]{2,1,0:T(8,128)(2,1)}), bf16[16,96,1024]{2,1,0:T(8,128)(2,1)}, u32[]{:S(2)}, u32[]{:S(2)}) async-start(bf16[16,96,1024]{2,1,0:T(8,128)(2,1)} %bitcast.42), calls=%async_computation.3 | async-start | bytes 6291456 | tf_op jit(solution)/shard_map/all_to_all | solution.py:408
  203.2 43.2 %collective-permute-done.1.rim_ref = bf16[128,1024]{1,0:T(8,128)(2,1)S(1)} collective-permute-done((bf16[128,1024]{1,0:T(8,128)(2,1)}, bf16[128,1024]{1,0:T(8,128)(2,1)S(1)}, u32[]{:S(2)}, u32[]{:S(2)}) %collective-permute-start.1) | collective-permute-done | bytes 262176 | tf_op jit(solution)/shard_map/ppermute | solution.py:402
  247.1 5.2 %collect.2.refs_0_.refs_1_ = bf16[2,256,512]{2,1,0:T(8,128)(2,1)} custom-call(s32[48]{0:T(128)} %broadcast_select_fusion.pick_ref, f32[256,1024]{1,0:T(8,128)} %get-tuple-element.40.own_ref, bf16[128,1024]{1,0:T(8,128)(2,1)} %copy-done.17, bf16[1536,1024]{1,0:T(8,128)(2,1)} %bitcast.34), custom_call_target="tpu_custom_call" | custom-call | tf_op jit(solution)/shard_map/collect/pallas_call | solution.py:224
  260.2 8.4 %collective-permute-done.2.rim_ref = bf16[128,1024]{1,0:T(8,128)(2,1)S(1)} collective-permute-done((bf16[128,1024]{1,0:T(8,128)(2,1)S(1)}, bf16[128,1024]{1,0:T(8,128)(2,1)S(1)}, u32[]{:S(2)}, u32[]{:S(2)}) %collective-permute-start.2) | collective-permute-done | bytes 262176 | tf_op jit(solution)/shard_map/ppermute | solution.py:402
  269.3 5.1 %collect.3.refs_1_ = bf16[2,256,512]{2,1,0:T(8,128)(2,1)} custom-call(s32[48]{0:T(128)} %broadcast_select_fusion.pick_ref, f32[256,1024]{1,0:T(8,128)} %get-tuple-element.43.own_ref, bf16[128,1024]{1,0:T(8,128)(2,1)} %copy-done.18, bf16[1536,1024]{1,0:T(8,128)(2,1)} %bitcast.13.back_ref), custom_call_target="tpu_custom_call" | custom-call | tf_op jit(solution)/shard_map/collect/pallas_call | solution.py:224
  274.4 3.7 shard_map.118
  279.5 6.9 %shard_map.120 = (bf16[8,256,128]{2,1,0:T(8,128)(2,1)}, bf16[8,256,128]{2,1,0:T(8,128)(2,1)}, bf16[8,256,128]{2,1,0:T(8,128)(2,1)}, bf16[8,256,128]{2,1,0:T(8,12...) custom-call(s32[2]{0:T(128)} %pad_add_fusion.chip_ref.s_ref, ...), custom_call_target="tpu_custom_call" | custom-call | tf_op jit(solution)/shard_map/pallas_call | solution.py:353
  293.0 4.8 %shard_map.122 = (bf16[8,128,128]{2,1,0:T(8,128)(2,1)}, bf16[8,128,128]{2,1,0:T(8,128)(2,1)}, bf16[8,128,128]{2,1,0:T(8,128)(2,1)}, bf16[8,128,128]{2,1,0:T(8,12...) custom-call(s32[2]{0:T(128)} %pad_add_fusion.chip_ref.s_ref, ...), custom_call_target="tpu_custom_call" | custom-call | tf_op jit(solution)/shard_map/pallas_call | solution.py:353
  305.4 12.0 %collective-permute-done.16 = bf16[8,128,128]{2,1,0:T(8,128)(2,1)S(1)} collective-permute-done((bf16[8,128,128]{2,1,0:T(8,128)(2,1)}, bf16[8,128,128]{2,1,0:T(8,128)(2,1)S(1)}, u32[]{:S(2)}, u32[]{:S(2)}) %collective-permute-start.16) | collective-permute-done | bytes 262176 | tf_op jit(solution)/shard_map/ppermute | solution.py:419
  319.4 6.9 %collective-permute-done.13 = bf16[8,128,128]{2,1,0:T(8,128)(2,1)S(1)} collective-permute-done((bf16[8,128,128]{2,1,0:T(8,128)(2,1)}, bf16[8,128,128]{2,1,0:T(8,128)(2,1)S(1)}, u32[]{:S(2)}, u32[]{:S(2)}) %collective-permute-start.13) | collective-permute-done | bytes 262176 | tf_op jit(solution)/shard_map/ppermute | solution.py:419
  333.9 5.2 %collective-permute-done.7.refs_5_ = bf16[8,256,128]{2,1,0:T(8,128)(2,1)S(1)} collective-permute-done((bf16[8,256,128]{2,1,0:T(8,128)(2,1)S(1)}, bf16[8,256,128]{2,1,0:T(8,128)(2,1)S(1)}, u32[]{:S(2)}, u32[]{:S(2)}) %collective-permute-start.7) | collective-permute-done | bytes 524320 | tf_op jit(solution)/shard_map/ppermute | solution.py:419
  339.1 5.6 %collective-permute-done.15.refs_13_ = bf16[8,128,128]{2,1,0:T(8,128)(2,1)S(1)} collective-permute-done((bf16[8,128,128]{2,1,0:T(8,128)(2,1)S(1)}, bf16[8,128,128]{2,1,0:T(8,128)(2,1)S(1)}, u32[]{:S(2)}, u32[]{:S(2)}) %collective-permute-start.15) | collective-permute-done | bytes 262176 | tf_op jit(solution)/shard_map/ppermute | solution.py:419
  344.7 5.6 %collective-permute-done.14.refs_11_ = bf16[8,128,128]{2,1,0:T(8,128)(2,1)S(1)} collective-permute-done((bf16[8,128,128]{2,1,0:T(8,128)(2,1)S(1)}, bf16[8,128,128]{2,1,0:T(8,128)(2,1)S(1)}, u32[]{:S(2)}, u32[]{:S(2)}) %collective-permute-start.14) | collective-permute-done | bytes 262176 | tf_op jit(solution)/shard_map/ppermute | solution.py:419
  351.0 6.3 %shard_map.123 = bf16[16,896,128]{2,1,0:T(8,128)(2,1)} custom-call(s32[2]{0:T(128)} %pad_add_fusion.chip_ref.s_ref, bf16[2048,256]{1,0:T(8,128)(2,1)} %bitcast.32, bf16[2,256,512]{2,1,0:T(8,128)(2,1)} %collect.3.refs_1_, bf16[16,512,128]{2,1,0:T(8,128)(2,1)} %collective-permute-done.3.refs_2_, bf16[8,256,128]{2,1,0:T(8,128)(2,1)} %get-tuple-element.46.refs_3_, ...), custom_call_target="tpu_custom_call" | custom-call | tf_op jit(solution)/shard_map/pallas_call | solution.py:353
  357.3 48.3 %all_to_all.26 = bf16[16,896,128]{2,1,0:T(8,128)(2,1)} all-to-all(bf16[16,896,128]{2,1,0:T(8,128)(2,1)} %shard_map.123), channel_id=1, replica_groups=mesh['tm'=16,'roll'=8] {'tm'}, dimensions={0} | all-to-all | bytes 7340032 | tf_op jit(solution)/shard_map/all_to_all | solution.py:408
  411.1 6.5 %collective-permute-done.18.refs_1_ = bf16[896,128]{1,0:T(8,128)(2,1)S(1)} collective-permute-done((bf16[896,128]{1,0:T(8,128)(2,1)S(1)}, bf16[896,128]{1,0:T(8,128)(2,1)S(1)}, u32[]{:S(2)}, u32[]{:S(2)}) %collective-permute-start.18) | collective-permute-done | bytes 229408 | tf_op jit(solution)/shard_map/ppermute | solution.py:419
  421.8 5.0 %collective-permute-start.21 = (bf16[2048,128]{1,0:T(8,128)(2,1)}, bf16[2048,128]{1,0:T(8,128)(2,1)S(1)}, u32[]{:S(2)}, u32[]{:S(2)}) collective-permute-start(bf16[2048,128]{1,0:T(8,128)(2,1)} %gathered.1.mine_ref), channel_id=1, source_target_pairs={{0,1},{1,0},{2,3},{3,2},{4,5},{5,4},{6,7},{7,6},{8,9},{9,8},{10,11... | collective-permute-start | bytes 1572872 | tf_op jit(solution)/shard_map/ppermute | solution.py:398
  426.8 4.4 convolution_convert_fusion
  431.2 8.6 %input_gradient.1 = bf16[256,2048]{1,0:T(8,128)(2,1)} custom-call(bf16[256,1024]{1,0:T(8,128)(2,1)} %get-tuple-element.39.dq_ref.refs_1_, bf16[2048,1024]{1,0:T(8,128)(2,1)} %wq_ref.1, bf16[2048,1024]{1,0:T(8,128)(2,1)} %wk_ref.5, bf16[2048,1024]{1,0:T(8,128)(2,1)} %wv_ref.5, bf16[2,256,512]{2,1,0:T(8,128)(2,1)} %collect.2.refs_0_.refs_1_, ...), custom_call_target="tpu_custom_call" | custom-call | tf_op jit(solution)/shard_map/input_gradient/pallas_call | solution.py:385
  (132 shorter events, 65.4 us)
Async XLA Ops:
  2.2 15.2 %all-to-all-start = ((s32[16,1,8]{2,1,0:T(1,128)}), s32[16,1,8]{2,1,0:T(1,128)S(1)}, u32[]{:S(2)}, u32[]{:S(2)}) async-start(s32[16,1,8]{2,1,0:T(1,128)} %bitcast.4), calls=%async_computation | async-start | bytes 16384 | tf_op jit(solution)/shard_map/all_to_all | solution.py:408
  23.5 106.1 %all-to-all-start.1 = ((bf16[16,96,2048]{2,1,0:T(8,128)(2,1)}), bf16[16,96,2048]{2,1,0:T(8,128)(2,1)}, u32[]{:S(2)}, u32[]{:S(2)}) async-start(bf16[16,96,2048]{2,1,0:T(8,128)(2,1)} %bitcast.33), calls=%async_computation.1 | async-start | bytes 12582912 | tf_op jit(solution)/shard_map/all_to_all | solution.py:408
  30.4 92.7 %collective-permute-start = (bf16[128,2048]{1,0:T(8,128)(2,1)S(1)}, bf16[128,2048]{1,0:T(8,128)(2,1)S(1)}, u32[]{:S(2)}, u32[]{:S(2)}) collective-permute-start(bf16[128,2048]{1,0:T(8,128)(2,1)S(1)} %bitcast.44), channel_id=1, source_target_pairs={{0,8},{8,16},{16,24},{24,32},{32,40},{40,48},{48,56},{56,64},{64,7... | collective-permute-start | bytes 1572872 | tf_op jit(solution)/shard_map/ppermute | solution.py:402
  140.3 55.0 %all-to-all-start.2 = ((bf16[16,96,1024]{2,1,0:T(8,128)(2,1)}), bf16[16,96,1024]{2,1,0:T(8,128)(2,1)S(1)}, u32[]{:S(2)}, u32[]{:S(2)}) async-start(bf16[16,96,1024]{2,1,0:T(8,128)(2,1)} %bitcast.41), calls=%async_computation.2 | async-start | bytes 6291456 | tf_op jit(solution)/shard_map/all_to_all | solution.py:408
  172.2 30.4 %copy-start.23 = (s32[48]{0:T(128)S(1)}, s32[48]{0:T(128)}, u32[]{:S(2)}) copy-start(s32[48]{0:T(128)} %reshape.115.pick_ref) | copy-start | bytes 580
  172.2 107.3 %collective-permute-start.4 = (bf16[4,16,256,128]{3,2,1,0:T(8,128)(2,1)}, bf16[4,16,256,128]{3,2,1,0:T(8,128)(2,1)}, u32[]{:S(2)}, u32[]{:S(2)}) collective-permute-start(bf16[4,16,256,128]{3,2,1,0:T(8,128)(2,1)} %shard_map.119), channel_id=1, source_target_pairs={{0,1},{1,0},{2,3},{3,2},{4,5},{5,4},{6,7},{7,6},{8,9},{9,8},{10,11... | collective-permute-start | bytes 12582920 | tf_op jit(solution)/shard_map/ppermute | solution.py:398
  195.3 51.1 %copy-start = (bf16[16,96,1024]{2,1,0:T(8,128)(2,1)}, bf16[16,96,1024]{2,1,0:T(8,128)(2,1)S(1)}, u32[]{:S(2)}) copy-start(bf16[16,96,1024]{2,1,0:T(8,128)(2,1)S(1)} %all-to-all-done.2) | copy-start | bytes 9437188
  195.3 73.3 %all-to-all-start.3 = ((bf16[16,96,1024]{2,1,0:T(8,128)(2,1)}), bf16[16,96,1024]{2,1,0:T(8,128)(2,1)}, u32[]{:S(2)}, u32[]{:S(2)}) async-start(bf16[16,96,1024]{2,1,0:T(8,128)(2,1)} %bitcast.42), calls=%async_computation.3 | async-start | bytes 6291456 | tf_op jit(solution)/shard_map/all_to_all | solution.py:408
  201.1 45.3 %collective-permute-start.1 = (bf16[128,1024]{1,0:T(8,128)(2,1)}, bf16[128,1024]{1,0:T(8,128)(2,1)S(1)}, u32[]{:S(2)}, u32[]{:S(2)}) collective-permute-start(bf16[128,1024]{1,0:T(8,128)(2,1)} %get-tuple-element.41), channel_id=1, source_target_pairs={{8,0},{16,8},{24,16},{32,24},{40,32},{48,40},{56,48},{64,56},{72,6... | collective-permute-start | bytes 786440 | tf_op jit(solution)/shard_map/ppermute | solution.py:402
  255.9 35.7 %collective-permute-start.11 = (bf16[4,16,128,128]{3,2,1,0:T(8,128)(2,1)}, bf16[4,16,128,128]{3,2,1,0:T(8,128)(2,1)S(1)}, u32[]{:S(2)}, u32[]{:S(2)}) collective-permute-start(bf16[4,16,128,128]{3,2,1,0:T(8,128)(2,1)} %shard_map.121), channel_id=1, source_target_pairs={{0,1},{1,0},{2,3},{3,2},{4,5},{5,4},{6,7},{7,6},{8,9},{9,8},{10,11... | collective-permute-start | bytes 6291464 | tf_op jit(solution)/shard_map/ppermute | solution.py:398
  258.9 9.7 %collective-permute-start.2 = (bf16[128,1024]{1,0:T(8,128)(2,1)S(1)}, bf16[128,1024]{1,0:T(8,128)(2,1)S(1)}, u32[]{:S(2)}, u32[]{:S(2)}) collective-permute-start(bf16[128,1024]{1,0:T(8,128)(2,1)S(1)} %copy-done.26), channel_id=1, source_target_pairs={{8,0},{16,8},{24,16},{32,24},{40,32},{48,40},{56,48},{64,56},{72,6... | collective-permute-start | bytes 786440 | tf_op jit(solution)/shard_map/ppermute | solution.py:402
  278.1 53.1 %collective-permute-start.3 = (bf16[16,512,128]{2,1,0:T(8,128)(2,1)}, bf16[16,512,128]{2,1,0:T(8,128)(2,1)}, u32[]{:S(2)}, u32[]{:S(2)}) collective-permute-start(bf16[16,512,128]{2,1,0:T(8,128)(2,1)} %shard_map.118), channel_id=1, source_target_pairs={{0,1},{1,0},{2,3},{3,2},{4,5},{5,4},{6,7},{7,6},{8,9},{9,8},{10,11... | collective-permute-start | bytes 6291464 | tf_op jit(solution)/shard_map/ppermute | solution.py:398
  286.4 31.8 %copy-start.10 = (bf16[8,256,128]{2,1,0:T(8,128)(2,1)S(1)}, bf16[8,256,128]{2,1,0:T(8,128)(2,1)}, u32[]{:S(2)}) copy-start(bf16[8,256,128]{2,1,0:T(8,128)(2,1)} %get-tuple-element.48) | copy-start | bytes 1572868
  286.4 14.2 %collective-permute-start.9 = (bf16[8,256,128]{2,1,0:T(8,128)(2,1)}, bf16[8,256,128]{2,1,0:T(8,128)(2,1)}, u32[]{:S(2)}, u32[]{:S(2)}) collective-permute-start(bf16[8,256,128]{2,1,0:T(8,128)(2,1)} %get-tuple-element.53), channel_id=1, source_target_pairs={{0,6},{1,7},{2,0},{3,1},{4,2},{5,3},{6,4},{7,5},{8,14},{9,15},{10,... | collective-permute-start | bytes 1572872 | tf_op jit(solution)/shard_map/ppermute | solution.py:419
  289.0 16.3 %collective-permute-start.6 = (bf16[8,256,128]{2,1,0:T(8,128)(2,1)}, bf16[8,256,128]{2,1,0:T(8,128)(2,1)}, u32[]{:S(2)}, u32[]{:S(2)}) collective-permute-start(bf16[8,256,128]{2,1,0:T(8,128)(2,1)} %get-tuple-element.49), channel_id=1, source_target_pairs={{0,2},{1,3},{2,4},{3,5},{4,6},{5,7},{6,0},{7,1},{8,10},{9,11},{10,... | collective-permute-start | bytes 1572872 | tf_op jit(solution)/shard_map/ppermute | solution.py:419
  289.0 39.4 %collective-permute-start.5 = (bf16[8,256,128]{2,1,0:T(8,128)(2,1)}, bf16[8,256,128]{2,1,0:T(8,128)(2,1)S(1)}, u32[]{:S(2)}, u32[]{:S(2)}) collective-permute-start(bf16[8,256,128]{2,1,0:T(8,128)(2,1)} %get-tuple-element.47), channel_id=1, source_target_pairs={{0,6},{1,7},{2,0},{3,1},{4,2},{5,3},{6,4},{7,5},{8,14},{9,15},{10,... | collective-permute-start | bytes 1572872 | tf_op jit(solution)/shard_map/ppermute | solution.py:419
  291.7 39.5 %collective-permute-start.8 = (bf16[8,256,128]{2,1,0:T(8,128)(2,1)}, bf16[8,256,128]{2,1,0:T(8,128)(2,1)S(1)}, u32[]{:S(2)}, u32[]{:S(2)}) collective-permute-start(bf16[8,256,128]{2,1,0:T(8,128)(2,1)} %get-tuple-element.51), channel_id=1, source_target_pairs={{0,2},{1,3},{2,4},{3,5},{4,6},{5,7},{6,0},{7,1},{8,10},{9,11},{10,... | collective-permute-start | bytes 1572872 | tf_op jit(solution)/shard_map/ppermute | solution.py:419
  297.8 30.6 %copy-start.25 = (bf16[8,128,128]{2,1,0:T(8,128)(2,1)S(1)}, bf16[8,128,128]{2,1,0:T(8,128)(2,1)}, u32[]{:S(2)}) copy-start(bf16[8,128,128]{2,1,0:T(8,128)(2,1)} %get-tuple-element.55) | copy-start | bytes 786436
  297.8 33.3 %copy-start.24 = (bf16[8,128,128]{2,1,0:T(8,128)(2,1)S(1)}, bf16[8,128,128]{2,1,0:T(8,128)(2,1)}, u32[]{:S(2)}) copy-start(bf16[8,128,128]{2,1,0:T(8,128)(2,1)} %get-tuple-element.59) | copy-start | bytes 786436
  300.6 16.9 %collective-permute-start.16 = (bf16[8,128,128]{2,1,0:T(8,128)(2,1)}, bf16[8,128,128]{2,1,0:T(8,128)(2,1)S(1)}, u32[]{:S(2)}, u32[]{:S(2)}) collective-permute-start(bf16[8,128,128]{2,1,0:T(8,128)(2,1)} %get-tuple-element.61), channel_id=1, source_target_pairs={{0,6},{1,7},{2,0},{3,1},{4,2},{5,3},{6,4},{7,5},{8,14},{9,15},{10,... | collective-permute-start | bytes 786440 | tf_op jit(solution)/shard_map/ppermute | solution.py:419
  305.3 28.6 %collective-permute-start.10 = (bf16[8,256,128]{2,1,0:T(8,128)(2,1)S(1)}, bf16[8,256,128]{2,1,0:T(8,128)(2,1)S(1)}, u32[]{:S(2)}, u32[]{:S(2)}) collective-permute-start(bf16[8,256,128]{2,1,0:T(8,128)(2,1)S(1)} %add_convert_fusion), channel_id=1, source_target_pairs={{0,6},{1,7},{2,0},{3,1},{4,2},{5,3},{6,4},{7,5},{8,14},{9,15},{10,... | collective-permute-start | bytes 1572872 | tf_op jit(solution)/shard_map/ppermute | solution.py:419
  317.4 8.9 %collective-permute-start.13 = (bf16[8,128,128]{2,1,0:T(8,128)(2,1)}, bf16[8,128,128]{2,1,0:T(8,128)(2,1)S(1)}, u32[]{:S(2)}, u32[]{:S(2)}) collective-permute-start(bf16[8,128,128]{2,1,0:T(8,128)(2,1)} %get-tuple-element.57), channel_id=1, source_target_pairs={{0,2},{1,3},{2,4},{3,5},{4,6},{5,7},{6,0},{7,1},{8,10},{9,11},{10,... | collective-permute-start | bytes 786440 | tf_op jit(solution)/shard_map/ppermute | solution.py:419
  326.3 12.8 %collective-permute-start.7 = (bf16[8,256,128]{2,1,0:T(8,128)(2,1)S(1)}, bf16[8,256,128]{2,1,0:T(8,128)(2,1)S(1)}, u32[]{:S(2)}, u32[]{:S(2)}) collective-permute-start(bf16[8,256,128]{2,1,0:T(8,128)(2,1)S(1)} %add_convert_fusion.1), channel_id=1, source_target_pairs={{0,2},{1,3},{2,4},{3,5},{4,6},{5,7},{6,0},{7,1},{8,10},{9,11},{10,... | collective-permute-start | bytes 1572872 | tf_op jit(solution)/shard_map/ppermute | solution.py:419
  328.4 22.0 %copy-start.6 = (bf16[8,256,128]{2,1,0:T(8,128)(2,1)}, bf16[8,256,128]{2,1,0:T(8,128)(2,1)S(1)}, u32[]{:S(2)}) copy-start(bf16[8,256,128]{2,1,0:T(8,128)(2,1)S(1)} %collective-permute-done.5.refs_4_) | copy-start | bytes 1572868
  328.4 10.7 %collective-permute-start.12 = (bf16[8,128,128]{2,1,0:T(8,128)(2,1)S(1)}, bf16[8,128,128]{2,1,0:T(8,128)(2,1)S(1)}, u32[]{:S(2)}, u32[]{:S(2)}) collective-permute-start(bf16[8,128,128]{2,1,0:T(8,128)(2,1)S(1)} %copy-done.25), channel_id=1, source_target_pairs={{0,6},{1,7},{2,0},{3,1},{4,2},{5,3},{6,4},{7,5},{8,14},{9,15},{10,... | collective-permute-start | bytes 786440 | tf_op jit(solution)/shard_map/ppermute | solution.py:419
  331.1 13.6 %collective-permute-start.15 = (bf16[8,128,128]{2,1,0:T(8,128)(2,1)S(1)}, bf16[8,128,128]{2,1,0:T(8,128)(2,1)S(1)}, u32[]{:S(2)}, u32[]{:S(2)}) collective-permute-start(bf16[8,128,128]{2,1,0:T(8,128)(2,1)S(1)} %copy-done.24), channel_id=1, source_target_pairs={{0,2},{1,3},{2,4},{3,5},{4,6},{5,7},{6,0},{7,1},{8,10},{9,11},{10,... | collective-permute-start | bytes 786440 | tf_op jit(solution)/shard_map/ppermute | solution.py:419
  331.2 13.5 %collective-permute-start.17 = (bf16[8,128,128]{2,1,0:T(8,128)(2,1)S(1)}, bf16[8,128,128]{2,1,0:T(8,128)(2,1)S(1)}, u32[]{:S(2)}, u32[]{:S(2)}) collective-permute-start(bf16[8,128,128]{2,1,0:T(8,128)(2,1)S(1)} %add_convert_fusion.2), channel_id=1, source_target_pairs={{0,6},{1,7},{2,0},{3,1},{4,2},{5,3},{6,4},{7,5},{8,14},{9,15},{10,... | collective-permute-start | bytes 786440 | tf_op jit(solution)/shard_map/ppermute | solution.py:419
  333.9 16.4 %collective-permute-start.14 = (bf16[8,128,128]{2,1,0:T(8,128)(2,1)S(1)}, bf16[8,128,128]{2,1,0:T(8,128)(2,1)S(1)}, u32[]{:S(2)}, u32[]{:S(2)}) collective-permute-start(bf16[8,128,128]{2,1,0:T(8,128)(2,1)S(1)} %add_convert_fusion.3), channel_id=1, source_target_pairs={{0,2},{1,3},{2,4},{3,5},{4,6},{5,7},{6,0},{7,1},{8,10},{9,11},{10,... | collective-permute-start | bytes 786440 | tf_op jit(solution)/shard_map/ppermute | solution.py:419
  408.3 9.2 %collective-permute-start.18 = (bf16[896,128]{1,0:T(8,128)(2,1)S(1)}, bf16[896,128]{1,0:T(8,128)(2,1)S(1)}, u32[]{:S(2)}, u32[]{:S(2)}) collective-permute-start(bf16[896,128]{1,0:T(8,128)(2,1)S(1)} %reduce_sum.32.refs_0_), channel_id=1, source_target_pairs={{0,2},{1,3},{2,4},{3,5},{4,6},{5,7},{6,0},{7,1},{8,10},{9,11},{10,... | collective-permute-start | bytes 688136 | tf_op jit(solution)/shard_map/ppermute | solution.py:419
  408.4 9.1 %collective-permute-start.19 = (bf16[896,128]{1,0:T(8,128)(2,1)S(1)}, bf16[896,128]{1,0:T(8,128)(2,1)S(1)}, u32[]{:S(2)}, u32[]{:S(2)}) collective-permute-start(bf16[896,128]{1,0:T(8,128)(2,1)S(1)} %reduce_sum.32.refs_0_), channel_id=1, source_target_pairs={{0,4},{1,5},{2,6},{3,7},{4,0},{5,1},{6,2},{7,3},{8,12},{9,13},{10,... | collective-permute-start | bytes 688136 | tf_op jit(solution)/shard_map/ppermute | solution.py:419
  409.0 8.9 %collective-permute-start.20 = (bf16[896,128]{1,0:T(8,128)(2,1)S(1)}, bf16[896,128]{1,0:T(8,128)(2,1)S(1)}, u32[]{:S(2)}, u32[]{:S(2)}) collective-permute-start(bf16[896,128]{1,0:T(8,128)(2,1)S(1)} %reduce_sum.32.refs_0_), channel_id=1, source_target_pairs={{0,6},{1,7},{2,0},{3,1},{4,2},{5,3},{6,4},{7,5},{8,14},{9,15},{10,... | collective-permute-start | bytes 688136 | tf_op jit(solution)/shard_map/ppermute | solution.py:419
  421.8 18.0 %collective-permute-start.21 = (bf16[2048,128]{1,0:T(8,128)(2,1)}, bf16[2048,128]{1,0:T(8,128)(2,1)S(1)}, u32[]{:S(2)}, u32[]{:S(2)}) collective-permute-start(bf16[2048,128]{1,0:T(8,128)(2,1)} %gathered.1.mine_ref), channel_id=1, source_target_pairs={{0,1},{1,0},{2,3},{3,2},{4,5},{5,4},{6,7},{7,6},{8,9},{9,8},{10,11... | collective-permute-start | bytes 1572872 | tf_op jit(solution)/shard_map/ppermute | solution.py:398
  (21 other events, 147.5 us)

commit v2 on v1

--- a/solution.py
+++ b/solution.py
@@ -65,7 +65,6 @@
         out_specs=pl.BlockSpec((rows, 2 * cols), lambda j: (0, j)),
         out_shape=jax.ShapeDtypeStruct((rows, 2 * w_key.shape[1]), bf16),
         compiler_params=params(),
-        name="keyval",
     )(x, w_key, w_value)
 
 
@@ -95,7 +94,6 @@
         ),
         out_shape=jax.ShapeDtypeStruct((BLOCKS * CAP * TOK, width), bf16),
         compiler_params=params(),
-        name="send",
     )(pick, kv)
 
 
@@ -199,18 +197,20 @@
         ],
         input_output_aliases={8 + k: k for k in range(len(written))},
         compiler_params=params(),
-        name="attend",
     )(read, add, bias, q, g, own, prev, slots, *written)
 
 
-def collect_body(pick_ref, own_ref, rim_ref, back_ref, out_ref, acc):
-    acc[:ROWS, :] = own_ref[...]
-    acc[ROWS:, :] = jnp.zeros_like(acc[ROWS:, :])
+def collect_body(pick_ref, own_ref, rim_ref, back_ref, out_ref, *accs):
+    for acc in accs:
+        acc[...] = jnp.zeros_like(acc)
+    for i in range(BLOCKS * CAP):
+        acc = accs[i % len(accs)]
+        at = pl.multiple_of(pick_ref[i] * TOK, TOK)
+        acc[pl.ds(at, TOK), :] += back_ref[i * TOK : (i + 1) * TOK, :].astype(f32)
+    acc = accs[0]
+    acc[:ROWS, :] = own_ref[...] + sum(a[:ROWS, :] for a in accs)
     tail = slice((FRAMES - BAND) * TOK, ROWS)
     acc[tail, :] += rim_ref[...].astype(f32)
-    for i in range(BLOCKS * CAP):
-        at = pl.multiple_of(pick_ref[i] * TOK, TOK)
-        acc[pl.ds(at, TOK), :] += back_ref[i * TOK : (i + 1) * TOK, :].astype(f32)
     for h in range(own_ref.shape[1] // (2 * HEAD)):
         for kind in range(2):
             left = (2 * h + kind) * HEAD
@@ -228,11 +228,10 @@
             grid=(width // cols,),
             in_specs=[col(ROWS, cols), col(BAND * TOK, cols), col(SPARE * TOK, cols)],
             out_specs=pl.BlockSpec((2, ROWS, cols // 2), lambda h, *_: (0, 0, h)),
-            scratch_shapes=[pltpu.VMEM((ROWS + TOK, cols), f32)],
+            scratch_shapes=[pltpu.VMEM((ROWS + TOK, cols), f32)] * 4,
         ),
         out_shape=jax.ShapeDtypeStruct((2, ROWS, width // 2), bf16),
         compiler_params=params(),
-        name="collect",
     )(pick, own, rim, back)
 
 
@@ -390,7 +389,6 @@
         out_specs=pl.BlockSpec((rows, cut), lambda j: (0, j)),
         out_shape=jax.ShapeDtypeStruct((rows, width), bf16),
         compiler_params=params(),
-        name="input_gradient",
     )(dq, w_query, w_key, w_value, *dkvs)
 
 
@@ -430,6 +428,38 @@
     came0 = along_chips(plus(next0, up), 1)
     came1 = along_chips(plus(last1, down), -1)
     return (own0, from_last, came0), (own1, from_next, came1)
+
+
+def over_blocks(x):
+    return summed(exchange(x))
+
+
+def combined(parts):
+    sizes = [halves[0][0].shape[1] for halves in parts]
+    per = BLOCKS // 2
+
+    def body(*refs):
+        out_ref = refs[-1]
+
+        def write(half):
+            at = 0
+            for u, size in enumerate(sizes):
+                terms = refs[6 * u + 3 * half : 6 * u + 3 * half + 3]
+                out_ref[:, at : at + size, :] = sum(term[...].astype(f32) for term in terms).astype(bf16)
+                at += size
+
+        for half in range(2):
+            pl.when(pl.program_id(0) == half)(functools.partial(write, half))
+
+    operands = [term for halves in parts for terms in halves for term in terms]
+    return pl.pallas_call(
+        body,
+        grid=(2,),
+        in_specs=[pl.BlockSpec(term.shape, lambda i: (0, 0, 0)) for term in operands],
+        out_specs=pl.BlockSpec((per, sum(sizes), LANES), lambda i: (i, 0, 0)),
+        out_shape=jax.ShapeDtypeStruct((BLOCKS, sum(sizes), LANES), bf16),
+        compiler_params=params(),
+    )(*operands)
 
 
 def everyone(x, ordered, scalars):
@@ -456,7 +486,6 @@
         ),
         out_shape=jax.ShapeDtypeStruct((height, LANES), bf16),
         compiler_params=params(),
-        name="gathered",
     )(scalars, *came)
     other = other_core(mine)
     return mine, other
@@ -557,8 +586,10 @@
     got = other_core(sent)
     kept = partial_call([(x_t, grad_query), (heads_out, cot)], keeping, got)
     sum_qo = over_chips(kept)
+    share_qo = over_blocks(combined([sum_qo]))
+    mine_qo, other_qo = everyone(share_qo, share_qo.shape[0], keeping)
     attended = jnp.dot(heads_out, w_output, preferred_element_type=f32).astype(bf16)
-    dkvs, sums = [], [sum_qo]
+    dkvs, sums = [], []
     for g, count in enumerate(SPLIT):
         last = g == len(SPLIT) - 1
         dkv = collect(pick_add, owns[g], passed[g], returned[g])
@@ -574,25 +605,26 @@
     mine, other = everyone(late, ordered, keeping)
     shard, o_shard = model_width // BLOCKS, inner // BLOCKS
     piece, o_piece = shard // CHIPS, o_shard // CHIPS
-    places = []
+    qo_places, kv_places = [], []
     for c in range(2):
-        found, first = [], sum(SPLIT[:-1])
+        found = []
         for j in range(CHIPS):
-            at = j * ordered
+            at = j * share_qo.shape[0]
             for k, rows, width in ((0, piece, half), (1, o_piece, model_width // 2)):
                 for column in range(c * width, (c + 1) * width, LANES):
                     found.append((k, j * rows, column, at, rows))
                     at += rows
+        qo_places.append(found)
+        found, first = [], sum(SPLIT[:-1])
+        for j in range(CHIPS):
             for h in range(first):
-                found.append((2 + c, j * piece, h * HEAD, at, piece))
-                at += piece
+                found.append((c, j * piece, h * HEAD, j * ordered + h * piece, piece))
         for h in range(first, HEADS):
-            found.append((2 + c, 0, h * HEAD, CHIPS * ordered + (h - first) * shard, shard))
-        places.append(found)
-    total_q, total_o, total_k, total_v = assembled(
-        mine, other, keeping,
-        [(shard, inner), (o_shard, model_width), (shard, inner), (shard, inner)], places,
-    )
+            found.append((c, 0, h * HEAD, CHIPS * ordered + (h - first) * shard, shard))
+        kv_places.append(found)
+    total_q, total_o = assembled(mine_qo, other_qo, keeping, [(shard, inner), (o_shard, model_width)], qo_places
+    )
+    total_k, total_v = assembled(mine, other, keeping, [(shard, inner)] * 2, kv_places)
     shape = (1, FRAMES, TOK, model_width)
     return (
         attended.reshape(shape),

time: 445 us -> 431 us (0.969)
  blocking collectives: 48.3 us -> 0 us
  starting transfers between devices: 69.8 us -> 84.4 us
  waiting for transfers between devices: 196 us -> 208 us
  Pallas kernels: 93.8 us -> 99.6 us
    all_to_all x1 -> x0, blocking collectives: 48.3 us -> none  [exchange(): lax.all_to_all(x, axis, split_axis=0, concat_axis=0, tiled=True, axis_ind...]
    all_to_all x4 -> x6, waiting for transfers between devices: 20.5 us -> 41.1 us  [exchange(): lax.all_to_all(x, axis, split_axis=0, concat_axis=0, tiled=True, axis_ind...]
    all_to_all x4 -> x6, starting transfers between devices: 34.7 us -> 47 us  [exchange(): lax.all_to_all(x, axis, split_axis=0, concat_axis=0, tiled=True, axis_ind...]
    ppermute x3, waiting for transfers between devices: 130 us -> 120 us  [from_behind(): lax.ppermute(block, 'tm', [(i - distance, i) for i in range(BLOCKS) if 0...]
    ppermute x4 -> x5, starting transfers between devices: 11.4 us -> 13.6 us  [other_core(): lax.ppermute(x, 'roll', [(i, i ^ 1) for i in range(lax.axis_size('roll'))])]
    ppermute x15 -> x18, waiting for transfers between devices: 44.9 us -> 46.9 us  [along_chips(): return lax.ppermute(x, 'roll', [(i, (i + 2 * d) % n) for i in range(n)])]
    ppermute x15 -> x18, starting transfers between devices: 17.8 us -> 17.9 us  [along_chips(): return lax.ppermute(x, 'roll', [(i, (i + 2 * d) % n) for i in range(n)])]
  transfers between devices with their start and end apart: 26 -> 32, of which waited for: 12 -> 18; matrix products, arithmetic and copies ran while one was open for 5% -> 6% of each run, Pallas kernels for 15% -> 19%
where the time goes in v2:
time: 431 us; the launch traced here: 430 us
  waiting for transfers between devices  208 us (48%)
  Pallas kernels  99.6 us (23%)
  starting transfers between devices  84.4 us (20%)
  local copies, waits for them, and re-layouts  14.3 us (3%)
  matrix products  12.9 us (3%)
  other arithmetic  9.36 us (2%)
    ppermute x3, waiting for transfers between devices, from_behind(): lax.ppermute(block, 'tm', [(i - distance, i) for i in range(BLOCKS) if 0...  120 us
    all_to_all x6, starting transfers between devices, exchange(): lax.all_to_all(x, axis, split_axis=0, concat_axis=0, tiled=True, axis_ind...  47 us
    ppermute x18, waiting for transfers between devices, along_chips(): return lax.ppermute(x, 'roll', [(i, (i + 2 * d) % n) for i in range(n)])  46.9 us
    all_to_all x6, waiting for transfers between devices, exchange(): lax.all_to_all(x, axis, split_axis=0, concat_axis=0, tiled=True, axis_ind...  41.1 us
    pallas_call x6, Pallas kernels, partial_call(): pl.pallas_call(body, grid_spec=pltpu.PrefetchScalarGridSpec(num_scalar_pr...  28.5 us
    pallas_call x2, Pallas kernels, attend(): pl.pallas_call(attend_body, grid_spec=pltpu.PrefetchScalarGridSpec(num_sc...  21.4 us
    ppermute x18, starting transfers between devices, along_chips(): return lax.ppermute(x, 'roll', [(i, (i + 2 * d) % n) for i in range(n)])  17.9 us
    ppermute x5, starting transfers between devices, other_core(): lax.ppermute(x, 'roll', [(i, i ^ 1) for i in range(lax.axis_size('roll'))])  13.6 us
  transfers between devices with their start and end apart: 32, of which 18 were waited for; matrix products, arithmetic and copies ran while one was open for 6% of the time, Pallas kernels for 19%

profile of v2, /device:TPU:1, one launch (start us, length us, event | category | flops | bytes accessed | tf_op | source)
XLA Modules:
  0.0 429.8 jit_solution(5308165133268705507)
XLA Ops:
  2.2 8.6 %all-to-all-start = ((s32[16,1,8]{2,1,0:T(1,128)}), s32[16,1,8]{2,1,0:T(1,128)S(1)}, u32[]{:S(2)}, u32[]{:S(2)}) async-start(s32[16,1,8]{2,1,0:T(1,128)} %bitcast.4), calls=%async_computation | async-start | bytes 16384 | tf_op jit(solution)/shard_map/all_to_all | solution.py:406
  10.8 6.6 %shard_map.118.kv_ref.own_ref = bf16[256,2048]{1,0:T(8,128)(2,1)} custom-call(bf16[256,2048]{1,0:T(8,128)(2,1)} %bitcast.35, bf16[2048,1024]{1,0:T(8,128)(2,1)} %wk_ref.5, bf16[2048,1024]{1,0:T(8,128)(2,1)} %wv_ref.5), custom_call_target="tpu_custom_call" | custom-call | tf_op jit(solution)/shard_map/pallas_call | solution.py:57
  18.5 5.0 %shard_map.120 = bf16[1536,2048]{1,0:T(8,128)(2,1)} custom-call(s32[48]{0:T(128)} %reshape.115.pick_ref, bf16[256,2048]{1,0:T(8,128)(2,1)} %shard_map.118.kv_ref.own_ref), custom_call_target="tpu_custom_call" | custom-call | tf_op jit(solution)/shard_map/pallas_call | solution.py:86
  23.5 6.8 %all-to-all-start.1 = ((bf16[16,96,2048]{2,1,0:T(8,128)(2,1)}), bf16[16,96,2048]{2,1,0:T(8,128)(2,1)}, u32[]{:S(2)}, u32[]{:S(2)}) async-start(bf16[16,96,2048]{2,1,0:T(8,128)(2,1)} %bitcast.33), calls=%async_computation.1 | async-start | bytes 12582912 | tf_op jit(solution)/shard_map/all_to_all | solution.py:406
  35.0 4.2 convolution_convert_fusion.2.q_ref
  40.1 4.3 convolution_convert_fusion.1.g_ref
  44.4 78.8 %collective-permute-done.x_ref = bf16[128,2048]{1,0:T(8,128)(2,1)S(1)} collective-permute-done((bf16[128,2048]{1,0:T(8,128)(2,1)S(1)}, bf16[128,2048]{1,0:T(8,128)(2,1)S(1)}, u32[]{:S(2)}, u32[]{:S(2)}) %collective-permute-start) | collective-permute-done | bytes 524320 | tf_op jit(solution)/shard_map/ppermute | solution.py:400
  123.9 5.7 %shard_map.119.prev_ref = bf16[128,2048]{1,0:T(8,128)(2,1)} custom-call(bf16[128,2048]{1,0:T(8,128)(2,1)} %copy-done.6, bf16[2048,1024]{1,0:T(8,128)(2,1)} %wk_ref.5, bf16[2048,1024]{1,0:T(8,128)(2,1)} %wv_ref.5), custom_call_target="tpu_custom_call" | custom-call | tf_op jit(solution)/shard_map/pallas_call | solution.py:57
  129.7 10.7 %shard_map.121 = (bf16[256,1024]{1,0:T(8,128)(2,1)}, bf16[256,1024]{1,0:T(8,128)(2,1)}, f32[256,1024]{1,0:T(8,128)}, bf16[128,1024]{1,0:T(8,128)(2,1)}, bf16[1536,1024]{1,0:T(8,128)(2,1)}) custom-call(s32[64]{0:T(128)} %get-tuple-element.67.read_ref, s32[64]{0:T(128)} %get-tuple-element.66.add_ref, f32[8,416]{1,0:T(8,128)} %reshape.112.bias_ref, ...), custom_call_target="tpu_custom_call" | custom-call | tf_op jit(solution)/shard_map/pallas_call | solution.py:166
  140.3 13.5 %all-to-all-start.2 = ((bf16[16,96,1024]{2,1,0:T(8,128)(2,1)}), bf16[16,96,1024]{2,1,0:T(8,128)(2,1)S(1)}, u32[]{:S(2)}, u32[]{:S(2)}) async-start(bf16[16,96,1024]{2,1,0:T(8,128)(2,1)} %bitcast.42), calls=%async_computation.2 | async-start | bytes 6291456 | tf_op jit(solution)/shard_map/all_to_all | solution.py:406
  153.8 10.7 %shard_map.122 = (bf16[256,1024]{1,0:T(8,128)(2,1)}, bf16[256,1024]{1,0:T(8,128)(2,1)}, f32[256,1024]{1,0:T(8,128)}, bf16[128,1024]{1,0:T(8,128)(2,1)}, bf16[1536,1024]{1,0:T(8,128)(2,1)}) custom-call(s32[64]{0:T(128)} %get-tuple-element.67.read_ref, s32[64]{0:T(128)} %get-tuple-element.66.add_ref, ...), custom_call_target="tpu_custom_call", output_to_operand_aliasing={{0}: (8, {}), {1}: (9, {})} | custom-call | tf_op jit(solution)/shard_map/pallas_call | solution.py:166
  164.5 30.8 %all-to-all-done.2 = bf16[16,96,1024]{2,1,0:T(8,128)(2,1)S(1)} async-done(((bf16[16,96,1024]{2,1,0:T(8,128)(2,1)}), bf16[16,96,1024]{2,1,0:T(8,128)(2,1)S(1)}, u32[]{:S(2)}, u32[]{:S(2)}) %all-to-all-start.2) | async-done | bytes 3145760 | tf_op jit(solution)/shard_map/all_to_all | solution.py:406
  195.3 6.0 %all-to-all-start.3 = ((bf16[16,96,1024]{2,1,0:T(8,128)(2,1)}), bf16[16,96,1024]{2,1,0:T(8,128)(2,1)}, u32[]{:S(2)}, u32[]{:S(2)}) async-start(bf16[16,96,1024]{2,1,0:T(8,128)(2,1)} %bitcast.41), calls=%async_computation.3 | async-start | bytes 6291456 | tf_op jit(solution)/shard_map/all_to_all | solution.py:406
  205.7 4.9 %shard_map.126 = bf16[4,16,256,128]{3,2,1,0:T(8,128)(2,1)} custom-call(s32[2]{0:T(128)} %pad_add_fusion.1.chip_ref, bf16[2048,256]{1,0:T(8,128)(2,1)} %bitcast.27, bf16[256,1024]{1,0:T(8,128)(2,1)} %get-tuple-element.39.dq_ref.refs_1_, bf16[256,1024]{1,0:T(8,128)(2,1)} %get-tuple-element.38.refs_2_, bf16[256,2048]{1,0:T(8,128)(2,1)} %bitcast.38), custom_call_target="tpu_custom_call" | custom-call | tf_op jit(solution)/shard_map/pallas_call | solution.py:352
  213.5 33.1 %collective-permute-done.1.rim_ref = bf16[128,1024]{1,0:T(8,128)(2,1)S(1)} collective-permute-done((bf16[128,1024]{1,0:T(8,128)(2,1)S(1)}, bf16[128,1024]{1,0:T(8,128)(2,1)S(1)}, u32[]{:S(2)}, u32[]{:S(2)}) %collective-permute-start.1) | collective-permute-done | bytes 262176 | tf_op jit(solution)/shard_map/ppermute | solution.py:400
  247.3 5.3 %shard_map.123.refs_0_.refs_1_ = bf16[2,256,512]{2,1,0:T(8,128)(2,1)} custom-call(s32[48]{0:T(128)} %broadcast_select_fusion.pick_ref, f32[256,1024]{1,0:T(8,128)} %get-tuple-element.40.own_ref, bf16[128,1024]{1,0:T(8,128)(2,1)} %copy-done.15, bf16[1536,1024]{1,0:T(8,128)(2,1)} %bitcast.34), custom_call_target="tpu_custom_call" | custom-call | tf_op jit(solution)/shard_map/pallas_call | solution.py:224
  260.4 8.4 %collective-permute-done.2.rim_ref = bf16[128,1024]{1,0:T(8,128)(2,1)S(1)} collective-permute-done((bf16[128,1024]{1,0:T(8,128)(2,1)S(1)}, bf16[128,1024]{1,0:T(8,128)(2,1)S(1)}, u32[]{:S(2)}, u32[]{:S(2)}) %collective-permute-start.2) | collective-permute-done | bytes 262176 | tf_op jit(solution)/shard_map/ppermute | solution.py:400
  269.6 5.2 %shard_map.124.refs_1_ = bf16[2,256,512]{2,1,0:T(8,128)(2,1)} custom-call(s32[48]{0:T(128)} %broadcast_select_fusion.pick_ref, f32[256,1024]{1,0:T(8,128)} %get-tuple-element.43.own_ref, bf16[128,1024]{1,0:T(8,128)(2,1)} %copy-done.16, bf16[1536,1024]{1,0:T(8,128)(2,1)} %bitcast.13.back_ref), custom_call_target="tpu_custom_call" | custom-call | tf_op jit(solution)/shard_map/pallas_call | solution.py:224
  274.7 3.6 shard_map.131
  281.2 4.7 %shard_map.133 = (bf16[8,128,128]{2,1,0:T(8,128)(2,1)}, bf16[8,128,128]{2,1,0:T(8,128)(2,1)}, bf16[8,128,128]{2,1,0:T(8,128)(2,1)}, bf16[8,128,128]{2,1,0:T(8,12...) custom-call(s32[2]{0:T(128)} %pad_add_fusion.chip_ref.s_ref, ...), custom_call_target="tpu_custom_call" | custom-call | tf_op jit(solution)/shard_map/pallas_call | solution.py:352
  305.3 4.0 collective-permute-done.18.refs_5_
  309.9 4.8 %shard_map.134 = bf16[16,640,128]{2,1,0:T(8,128)(2,1)} custom-call(s32[2]{0:T(128)} %pad_add_fusion.chip_ref.s_ref, bf16[2048,256]{1,0:T(8,128)(2,1)} %bitcast.31, bf16[2,256,512]{2,1,0:T(8,128)(2,1)} %shard_map.124.refs_1_, bf16[16,512,128]{2,1,0:T(8,128)(2,1)} %collective-permute-done.14.refs_2_, bf16[8,128,128]{2,1,0:T(8,128)(2,1)} %get-tuple-element.55.refs_3_, ...), custom_call_target="tpu_custom_call" | custom-call | tf_op jit(solution)/shard_map/pallas_call | solution.py:352
  314.7 5.6 %all-to-all-start.5 = ((bf16[16,640,128]{2,1,0:T(8,128)(2,1)}), bf16[16,640,128]{2,1,0:T(8,128)(2,1)S(1)}, u32[]{:S(2)}, u32[]{:S(2)}) async-start(bf16[16,640,128]{2,1,0:T(8,128)(2,1)} %shard_map.134), calls=%async_computation.5 | async-start | bytes 5242880 | tf_op jit(solution)/shard_map/all_to_all | solution.py:406
  320.3 6.9 %shard_map.127 = (bf16[8,256,128]{2,1,0:T(8,128)(2,1)}, bf16[8,256,128]{2,1,0:T(8,128)(2,1)}, bf16[8,256,128]{2,1,0:T(8,128)(2,1)}, bf16[8,256,128]{2,1,0:T(8,12...) custom-call(s32[2]{0:T(128)} %pad_add_fusion.chip_ref.s_ref, ...), custom_call_target="tpu_custom_call" | custom-call | tf_op jit(solution)/shard_map/pallas_call | solution.py:352
  330.7 8.4 %collective-permute-done.8 = bf16[8,256,128]{2,1,0:T(8,128)(2,1)S(1)} collective-permute-done((bf16[8,256,128]{2,1,0:T(8,128)(2,1)}, bf16[8,256,128]{2,1,0:T(8,128)(2,1)S(1)}, u32[]{:S(2)}, u32[]{:S(2)}) %collective-permute-start.8) | collective-permute-done | bytes 524320 | tf_op jit(solution)/shard_map/ppermute | solution.py:417
  343.1 7.3 %collective-permute-done.4.refs_1_ = bf16[8,256,128]{2,1,0:T(8,128)(2,1)S(1)} collective-permute-done((bf16[8,256,128]{2,1,0:T(8,128)(2,1)}, bf16[8,256,128]{2,1,0:T(8,128)(2,1)S(1)}, u32[]{:S(2)}, u32[]{:S(2)}) %collective-permute-start.4) | collective-permute-done | bytes 524320 | tf_op jit(solution)/shard_map/ppermute | solution.py:417
  351.4 10.2 %collective-permute-done.9.refs_5_ = bf16[8,256,128]{2,1,0:T(8,128)(2,1)S(1)} collective-permute-done((bf16[8,256,128]{2,1,0:T(8,128)(2,1)S(1)}, bf16[8,256,128]{2,1,0:T(8,128)(2,1)S(1)}, u32[]{:S(2)}, u32[]{:S(2)}) %collective-permute-start.9) | collective-permute-done | bytes 524320 | tf_op jit(solution)/shard_map/ppermute | solution.py:417
  366.5 6.6 %all-to-all-start.4 = ((bf16[16,256,128]{2,1,0:T(8,128)(2,1)}), bf16[16,256,128]{2,1,0:T(8,128)(2,1)}, u32[]{:S(2)}, u32[]{:S(2)}) async-start(bf16[16,256,128]{2,1,0:T(8,128)(2,1)} %shard_map.128), calls=%async_computation.4 | async-start | bytes 2097152 | tf_op jit(solution)/shard_map/all_to_all | solution.py:406
  376.4 10.3 %all-to-all-done.4 = bf16[16,256,128]{2,1,0:T(8,128)(2,1)} async-done(((bf16[16,256,128]{2,1,0:T(8,128)(2,1)}), bf16[16,256,128]{2,1,0:T(8,128)(2,1)}, u32[]{:S(2)}, u32[]{:S(2)}) %all-to-all-start.4) | async-done | bytes 1048608 | tf_op jit(solution)/shard_map/all_to_all | solution.py:406
  398.5 7.4 %collective-permute-start.13 = (bf16[1024,128]{1,0:T(8,128)(2,1)}, bf16[1024,128]{1,0:T(8,128)(2,1)S(1)}, u32[]{:S(2)}, u32[]{:S(2)}) collective-permute-start(bf16[1024,128]{1,0:T(8,128)(2,1)} %shard_map.129.mine_ref), channel_id=1, source_target_pairs={{0,1},{1,0},{2,3},{3,2},{4,5},{5,4},{6,7},{7,6},{8,9},{9,8},{10,11... | collective-permute-start | bytes 786440 | tf_op jit(solution)/shard_map/ppermute | solution.py:396
  409.9 4.4 %convolution_convert_fusion = bf16[256,2048]{1,0:T(8,128)(2,1)} fusion(bf16[256,1024]{1,0:T(8,128)(2,1)S(1)} %copy-done.2, bf16[1024,2048]{1,0:T(8,128)(2,1)} %param.13), kind=kOutput, calls=%fused_computation | convolution fusion | flops 1074266112 | bytes 5767168 | tf_op jit(solution)/shard_map/dot_general | solution.py:591
  414.3 8.6 %shard_map.125 = bf16[256,2048]{1,0:T(8,128)(2,1)} custom-call(bf16[256,1024]{1,0:T(8,128)(2,1)} %get-tuple-element.39.dq_ref.refs_1_, bf16[2048,1024]{1,0:T(8,128)(2,1)} %wq_ref.1, bf16[2048,1024]{1,0:T(8,128)(2,1)} %wk_ref.5, bf16[2048,1024]{1,0:T(8,128)(2,1)} %wv_ref.5, bf16[2,256,512]{2,1,0:T(8,128)(2,1)} %shard_map.123.refs_0_.refs_1_, ...), custom_call_target="tpu_custom_call" | custom-call | tf_op jit(solution)/shard_map/pallas_call | solution.py:384
  (153 shorter events, 87.8 us)
Async XLA Ops:
  2.2 15.2 %all-to-all-start = ((s32[16,1,8]{2,1,0:T(1,128)}), s32[16,1,8]{2,1,0:T(1,128)S(1)}, u32[]{:S(2)}, u32[]{:S(2)}) async-start(s32[16,1,8]{2,1,0:T(1,128)} %bitcast.4), calls=%async_computation | async-start | bytes 16384 | tf_op jit(solution)/shard_map/all_to_all | solution.py:406
  23.5 106.1 %all-to-all-start.1 = ((bf16[16,96,2048]{2,1,0:T(8,128)(2,1)}), bf16[16,96,2048]{2,1,0:T(8,128)(2,1)}, u32[]{:S(2)}, u32[]{:S(2)}) async-start(bf16[16,96,2048]{2,1,0:T(8,128)(2,1)} %bitcast.33), calls=%async_computation.1 | async-start | bytes 12582912 | tf_op jit(solution)/shard_map/all_to_all | solution.py:406
  30.4 92.7 %collective-permute-start = (bf16[128,2048]{1,0:T(8,128)(2,1)S(1)}, bf16[128,2048]{1,0:T(8,128)(2,1)S(1)}, u32[]{:S(2)}, u32[]{:S(2)}) collective-permute-start(bf16[128,2048]{1,0:T(8,128)(2,1)S(1)} %bitcast.44), channel_id=1, source_target_pairs={{0,8},{8,16},{16,24},{24,32},{32,40},{40,48},{48,56},{56,64},{64,7... | collective-permute-start | bytes 1572872 | tf_op jit(solution)/shard_map/ppermute | solution.py:400
  140.3 55.0 %all-to-all-start.2 = ((bf16[16,96,1024]{2,1,0:T(8,128)(2,1)}), bf16[16,96,1024]{2,1,0:T(8,128)(2,1)S(1)}, u32[]{:S(2)}, u32[]{:S(2)}) async-start(bf16[16,96,1024]{2,1,0:T(8,128)(2,1)} %bitcast.42), calls=%async_computation.2 | async-start | bytes 6291456 | tf_op jit(solution)/shard_map/all_to_all | solution.py:406
  195.3 73.6 %all-to-all-start.3 = ((bf16[16,96,1024]{2,1,0:T(8,128)(2,1)}), bf16[16,96,1024]{2,1,0:T(8,128)(2,1)}, u32[]{:S(2)}, u32[]{:S(2)}) async-start(bf16[16,96,1024]{2,1,0:T(8,128)(2,1)} %bitcast.41), calls=%async_computation.3 | async-start | bytes 6291456 | tf_op jit(solution)/shard_map/all_to_all | solution.py:406
  204.2 42.4 %collective-permute-start.1 = (bf16[128,1024]{1,0:T(8,128)(2,1)S(1)}, bf16[128,1024]{1,0:T(8,128)(2,1)S(1)}, u32[]{:S(2)}, u32[]{:S(2)}) collective-permute-start(bf16[128,1024]{1,0:T(8,128)(2,1)S(1)} %copy-done.29), channel_id=1, source_target_pairs={{8,0},{16,8},{24,16},{32,24},{40,32},{48,40},{56,48},{64,56},{72,6... | collective-permute-start | bytes 786440 | tf_op jit(solution)/shard_map/ppermute | solution.py:400
  210.5 109.7 %collective-permute-start.3 = (bf16[4,16,256,128]{3,2,1,0:T(8,128)(2,1)}, bf16[4,16,256,128]{3,2,1,0:T(8,128)(2,1)}, u32[]{:S(2)}, u32[]{:S(2)}) collective-permute-start(bf16[4,16,256,128]{3,2,1,0:T(8,128)(2,1)} %shard_map.126), channel_id=1, source_target_pairs={{0,1},{1,0},{2,3},{3,2},{4,5},{5,4},{6,7},{7,6},{8,9},{9,8},{10,11... | collective-permute-start | bytes 12582920 | tf_op jit(solution)/shard_map/ppermute | solution.py:396
  256.2 23.7 %collective-permute-start.15 = (bf16[4,16,128,128]{3,2,1,0:T(8,128)(2,1)}, bf16[4,16,128,128]{3,2,1,0:T(8,128)(2,1)S(1)}, u32[]{:S(2)}, u32[]{:S(2)}) collective-permute-start(bf16[4,16,128,128]{3,2,1,0:T(8,128)(2,1)} %shard_map.132), channel_id=1, source_target_pairs={{0,1},{1,0},{2,3},{3,2},{4,5},{5,4},{6,7},{7,6},{8,9},{9,8},{10,11... | collective-permute-start | bytes 6291464 | tf_op jit(solution)/shard_map/ppermute | solution.py:396
  259.1 9.7 %collective-permute-start.2 = (bf16[128,1024]{1,0:T(8,128)(2,1)S(1)}, bf16[128,1024]{1,0:T(8,128)(2,1)S(1)}, u32[]{:S(2)}, u32[]{:S(2)}) collective-permute-start(bf16[128,1024]{1,0:T(8,128)(2,1)S(1)} %copy-done.28), channel_id=1, source_target_pairs={{8,0},{16,8},{24,16},{32,24},{40,32},{48,40},{56,48},{64,56},{72,6... | collective-permute-start | bytes 786440 | tf_op jit(solution)/shard_map/ppermute | solution.py:400
  278.4 21.5 %collective-permute-start.14 = (bf16[16,512,128]{2,1,0:T(8,128)(2,1)}, bf16[16,512,128]{2,1,0:T(8,128)(2,1)}, u32[]{:S(2)}, u32[]{:S(2)}) collective-permute-start(bf16[16,512,128]{2,1,0:T(8,128)(2,1)} %shard_map.131), channel_id=1, source_target_pairs={{0,1},{1,0},{2,3},{3,2},{4,5},{5,4},{6,7},{7,6},{8,9},{9,8},{10,11... | collective-permute-start | bytes 6291464 | tf_op jit(solution)/shard_map/ppermute | solution.py:396
  285.9 8.5 %collective-permute-start.20 = (bf16[8,128,128]{2,1,0:T(8,128)(2,1)}, bf16[8,128,128]{2,1,0:T(8,128)(2,1)S(1)}, u32[]{:S(2)}, u32[]{:S(2)}) collective-permute-start(bf16[8,128,128]{2,1,0:T(8,128)(2,1)} %get-tuple-element.62), channel_id=1, source_target_pairs={{0,6},{1,7},{2,0},{3,1},{4,2},{5,3},{6,4},{7,5},{8,14},{9,15},{10,... | collective-permute-start | bytes 786440 | tf_op jit(solution)/shard_map/ppermute | solution.py:417
  288.4 9.0 %collective-permute-start.17 = (bf16[8,128,128]{2,1,0:T(8,128)(2,1)}, bf16[8,128,128]{2,1,0:T(8,128)(2,1)S(1)}, u32[]{:S(2)}, u32[]{:S(2)}) collective-permute-start(bf16[8,128,128]{2,1,0:T(8,128)(2,1)} %get-tuple-element.58), channel_id=1, source_target_pairs={{0,2},{1,3},{2,4},{3,5},{4,6},{5,7},{6,0},{7,1},{8,10},{9,11},{10,... | collective-permute-start | bytes 786440 | tf_op jit(solution)/shard_map/ppermute | solution.py:417
  288.4 11.6 %collective-permute-start.16 = (bf16[8,128,128]{2,1,0:T(8,128)(2,1)}, bf16[8,128,128]{2,1,0:T(8,128)(2,1)S(1)}, u32[]{:S(2)}, u32[]{:S(2)}) collective-permute-start(bf16[8,128,128]{2,1,0:T(8,128)(2,1)} %get-tuple-element.56), channel_id=1, source_target_pairs={{0,6},{1,7},{2,0},{3,1},{4,2},{5,3},{6,4},{7,5},{8,14},{9,15},{10,... | collective-permute-start | bytes 786440 | tf_op jit(solution)/shard_map/ppermute | solution.py:417
  294.4 8.9 %collective-permute-start.19 = (bf16[8,128,128]{2,1,0:T(8,128)(2,1)}, bf16[8,128,128]{2,1,0:T(8,128)(2,1)S(1)}, u32[]{:S(2)}, u32[]{:S(2)}) collective-permute-start(bf16[8,128,128]{2,1,0:T(8,128)(2,1)} %get-tuple-element.60), channel_id=1, source_target_pairs={{0,2},{1,3},{2,4},{3,5},{4,6},{5,7},{6,0},{7,1},{8,10},{9,11},{10,... | collective-permute-start | bytes 786440 | tf_op jit(solution)/shard_map/ppermute | solution.py:417
  297.4 7.8 %collective-permute-start.21 = (bf16[8,128,128]{2,1,0:T(8,128)(2,1)S(1)}, bf16[8,128,128]{2,1,0:T(8,128)(2,1)S(1)}, u32[]{:S(2)}, u32[]{:S(2)}) collective-permute-start(bf16[8,128,128]{2,1,0:T(8,128)(2,1)S(1)} %add_convert_fusion.2), channel_id=1, source_target_pairs={{0,6},{1,7},{2,0},{3,1},{4,2},{5,3},{6,4},{7,5},{8,14},{9,15},{10,... | collective-permute-start | bytes 786440 | tf_op jit(solution)/shard_map/ppermute | solution.py:417
  299.8 9.4 %collective-permute-start.18 = (bf16[8,128,128]{2,1,0:T(8,128)(2,1)S(1)}, bf16[8,128,128]{2,1,0:T(8,128)(2,1)S(1)}, u32[]{:S(2)}, u32[]{:S(2)}) collective-permute-start(bf16[8,128,128]{2,1,0:T(8,128)(2,1)S(1)} %add_convert_fusion.3), channel_id=1, source_target_pairs={{0,2},{1,3},{2,4},{3,5},{4,6},{5,7},{6,0},{7,1},{8,10},{9,11},{10,... | collective-permute-start | bytes 786440 | tf_op jit(solution)/shard_map/ppermute | solution.py:417
  314.7 51.8 %all-to-all-start.5 = ((bf16[16,640,128]{2,1,0:T(8,128)(2,1)}), bf16[16,640,128]{2,1,0:T(8,128)(2,1)S(1)}, u32[]{:S(2)}, u32[]{:S(2)}) async-start(bf16[16,640,128]{2,1,0:T(8,128)(2,1)} %shard_map.134), calls=%async_computation.5 | async-start | bytes 5242880 | tf_op jit(solution)/shard_map/all_to_all | solution.py:406
  327.2 11.9 %collective-permute-start.8 = (bf16[8,256,128]{2,1,0:T(8,128)(2,1)}, bf16[8,256,128]{2,1,0:T(8,128)(2,1)S(1)}, u32[]{:S(2)}, u32[]{:S(2)}) collective-permute-start(bf16[8,256,128]{2,1,0:T(8,128)(2,1)} %get-tuple-element.53), channel_id=1, source_target_pairs={{0,6},{1,7},{2,0},{3,1},{4,2},{5,3},{6,4},{7,5},{8,14},{9,15},{10,... | collective-permute-start | bytes 1572872 | tf_op jit(solution)/shard_map/ppermute | solution.py:417
  328.1 13.7 %collective-permute-start.5 = (bf16[8,256,128]{2,1,0:T(8,128)(2,1)}, bf16[8,256,128]{2,1,0:T(8,128)(2,1)S(1)}, u32[]{:S(2)}, u32[]{:S(2)}) collective-permute-start(bf16[8,256,128]{2,1,0:T(8,128)(2,1)} %get-tuple-element.49), channel_id=1, source_target_pairs={{0,2},{1,3},{2,4},{3,5},{4,6},{5,7},{6,0},{7,1},{8,10},{9,11},{10,... | collective-permute-start | bytes 1572872 | tf_op jit(solution)/shard_map/ppermute | solution.py:417
  328.7 21.6 %collective-permute-start.4 = (bf16[8,256,128]{2,1,0:T(8,128)(2,1)}, bf16[8,256,128]{2,1,0:T(8,128)(2,1)S(1)}, u32[]{:S(2)}, u32[]{:S(2)}) collective-permute-start(bf16[8,256,128]{2,1,0:T(8,128)(2,1)} %get-tuple-element.47), channel_id=1, source_target_pairs={{0,6},{1,7},{2,0},{3,1},{4,2},{5,3},{6,4},{7,5},{8,14},{9,15},{10,... | collective-permute-start | bytes 1572872 | tf_op jit(solution)/shard_map/ppermute | solution.py:417
  330.7 20.7 %collective-permute-start.7 = (bf16[8,256,128]{2,1,0:T(8,128)(2,1)}, bf16[8,256,128]{2,1,0:T(8,128)(2,1)S(1)}, u32[]{:S(2)}, u32[]{:S(2)}) collective-permute-start(bf16[8,256,128]{2,1,0:T(8,128)(2,1)} %get-tuple-element.51), channel_id=1, source_target_pairs={{0,2},{1,3},{2,4},{3,5},{4,6},{5,7},{6,0},{7,1},{8,10},{9,11},{10,... | collective-permute-start | bytes 1572872 | tf_op jit(solution)/shard_map/ppermute | solution.py:417
  340.3 21.3 %collective-permute-start.9 = (bf16[8,256,128]{2,1,0:T(8,128)(2,1)S(1)}, bf16[8,256,128]{2,1,0:T(8,128)(2,1)S(1)}, u32[]{:S(2)}, u32[]{:S(2)}) collective-permute-start(bf16[8,256,128]{2,1,0:T(8,128)(2,1)S(1)} %add_convert_fusion), channel_id=1, source_target_pairs={{0,6},{1,7},{2,0},{3,1},{4,2},{5,3},{6,4},{7,5},{8,14},{9,15},{10,... | collective-permute-start | bytes 1572872 | tf_op jit(solution)/shard_map/ppermute | solution.py:417
  342.9 19.8 %collective-permute-start.6 = (bf16[8,256,128]{2,1,0:T(8,128)(2,1)S(1)}, bf16[8,256,128]{2,1,0:T(8,128)(2,1)S(1)}, u32[]{:S(2)}, u32[]{:S(2)}) collective-permute-start(bf16[8,256,128]{2,1,0:T(8,128)(2,1)S(1)} %add_convert_fusion.1), channel_id=1, source_target_pairs={{0,2},{1,3},{2,4},{3,5},{4,6},{5,7},{6,0},{7,1},{8,10},{9,11},{10,... | collective-permute-start | bytes 1572872 | tf_op jit(solution)/shard_map/ppermute | solution.py:417
  366.5 20.1 %all-to-all-start.4 = ((bf16[16,256,128]{2,1,0:T(8,128)(2,1)}), bf16[16,256,128]{2,1,0:T(8,128)(2,1)}, u32[]{:S(2)}, u32[]{:S(2)}) async-start(bf16[16,256,128]{2,1,0:T(8,128)(2,1)} %shard_map.128), calls=%async_computation.4 | async-start | bytes 2097152 | tf_op jit(solution)/shard_map/all_to_all | solution.py:406
  373.5 32.4 %collective-permute-start.22 = (bf16[640,128]{1,0:T(8,128)(2,1)S(1)}, bf16[640,128]{1,0:T(8,128)(2,1)S(1)}, u32[]{:S(2)}, u32[]{:S(2)}) collective-permute-start(bf16[640,128]{1,0:T(8,128)(2,1)S(1)} %reduce_sum.45.refs_0_), channel_id=1, source_target_pairs={{0,2},{1,3},{2,4},{3,5},{4,6},{5,7},{6,0},{7,1},{8,10},{9,11},{10,... | collective-permute-start | bytes 491528 | tf_op jit(solution)/shard_map/ppermute | solution.py:417
  373.7 32.2 %collective-permute-start.23 = (bf16[640,128]{1,0:T(8,128)(2,1)S(1)}, bf16[640,128]{1,0:T(8,128)(2,1)S(1)}, u32[]{:S(2)}, u32[]{:S(2)}) collective-permute-start(bf16[640,128]{1,0:T(8,128)(2,1)S(1)} %reduce_sum.45.refs_0_), channel_id=1, source_target_pairs={{0,4},{1,5},{2,6},{3,7},{4,0},{5,1},{6,2},{7,3},{8,12},{9,13},{10,... | collective-permute-start | bytes 491528 | tf_op jit(solution)/shard_map/ppermute | solution.py:417
  375.8 30.1 %collective-permute-start.24 = (bf16[640,128]{1,0:T(8,128)(2,1)S(1)}, bf16[640,128]{1,0:T(8,128)(2,1)S(1)}, u32[]{:S(2)}, u32[]{:S(2)}) collective-permute-start(bf16[640,128]{1,0:T(8,128)(2,1)S(1)} %reduce_sum.45.refs_0_), channel_id=1, source_target_pairs={{0,6},{1,7},{2,0},{3,1},{4,2},{5,3},{6,4},{7,5},{8,14},{9,15},{10,... | collective-permute-start | bytes 491528 | tf_op jit(solution)/shard_map/ppermute | solution.py:417
  388.1 4.4 %collective-permute-start.10 = (bf16[256,128]{1,0:T(8,128)(2,1)S(1)}, bf16[256,128]{1,0:T(8,128)(2,1)S(1)}, u32[]{:S(2)}, u32[]{:S(2)}) collective-permute-start(bf16[256,128]{1,0:T(8,128)(2,1)S(1)} %reduce_sum.44.refs_0_), channel_id=1, source_target_pairs={{0,2},{1,3},{2,4},{3,5},{4,6},{5,7},{6,0},{7,1},{8,10},{9,11},{10,... | collective-permute-start | bytes 196616 | tf_op jit(solution)/shard_map/ppermute | solution.py:417
  388.6 4.6 %collective-permute-start.11 = (bf16[256,128]{1,0:T(8,128)(2,1)S(1)}, bf16[256,128]{1,0:T(8,128)(2,1)S(1)}, u32[]{:S(2)}, u32[]{:S(2)}) collective-permute-start(bf16[256,128]{1,0:T(8,128)(2,1)S(1)} %reduce_sum.44.refs_0_), channel_id=1, source_target_pairs={{0,4},{1,5},{2,6},{3,7},{4,0},{5,1},{6,2},{7,3},{8,12},{9,13},{10,... | collective-permute-start | bytes 196616 | tf_op jit(solution)/shard_map/ppermute | solution.py:417
  392.5 3.1 collective-permute-start.12
  398.5 24.4 %collective-permute-start.13 = (bf16[1024,128]{1,0:T(8,128)(2,1)}, bf16[1024,128]{1,0:T(8,128)(2,1)S(1)}, u32[]{:S(2)}, u32[]{:S(2)}) collective-permute-start(bf16[1024,128]{1,0:T(8,128)(2,1)} %shard_map.129.mine_ref), channel_id=1, source_target_pairs={{0,1},{1,0},{2,3},{3,2},{4,5},{5,4},{6,7},{7,6},{8,9},{9,8},{10,11... | collective-permute-start | bytes 786440 | tf_op jit(solution)/shard_map/ppermute | solution.py:396
  409.9 16.4 %collective-permute-start.25 = (bf16[1024,128]{1,0:T(8,128)(2,1)}, bf16[1024,128]{1,0:T(8,128)(2,1)S(1)}, u32[]{:S(2)}, u32[]{:S(2)}) collective-permute-start(bf16[1024,128]{1,0:T(8,128)(2,1)} %shard_map.135.mine_ref), channel_id=1, source_target_pairs={{0,1},{1,0},{2,3},{3,2},{4,5},{5,4},{6,7},{7,6},{8,9},{9,8},{10,11... | collective-permute-start | bytes 786440 | tf_op jit(solution)/shard_map/ppermute | solution.py:396
  (30 other events, 209.9 us)

commit v3 on v2

--- a/solution.py
+++ b/solution.py
@@ -81,14 +81,13 @@
         copy(i).wait()
 
 
-def named_frames(pick, kv):
-    width = kv.shape[1]
+def named_frames(pick, kv, block, width):
     return pl.pallas_call(
         send_body,
         grid_spec=pltpu.PrefetchScalarGridSpec(
             num_scalar_prefetch=1,
             grid=(1,),
-            in_specs=[pl.BlockSpec((ROWS, width), lambda i, *_: (0, 0))],
+            in_specs=[pl.BlockSpec((ROWS, width), lambda i, *_: (0, block))],
             out_specs=pl.BlockSpec(memory_space=pl.ANY),
             scratch_shapes=[pltpu.SemaphoreType.DMA((BLOCKS * CAP,))],
         ),
@@ -171,7 +170,7 @@
             in_specs=[
                 pl.BlockSpec(bias.shape, lambda h, *_: (0, 0)),
                 src(ROWS, HEAD), src(ROWS, HEAD),
-                src(ROWS, 2 * HEAD), src(BAND * TOK, 2 * HEAD), src(SPARE * TOK, 2 * HEAD),
+                src(ROWS, 2 * HEAD), src(BAND * TOK, 2 * HEAD), col(SPARE * TOK, 2 * HEAD),
             ] + [pl.BlockSpec(memory_space=pl.ANY)] * len(written),
             out_specs=[
                 src(ROWS, HEAD), src(ROWS, HEAD),
@@ -568,13 +567,17 @@
     pick = jnp.sum(jnp.where(chosen, frame_no, 0), axis=2).reshape(-1)
     pick_add = jnp.where(jnp.any(chosen, axis=2).reshape(-1), pick, FRAMES)
 
-    outgoing = named_frames(pick, keyval)
-    slots = slots_exchange(outgoing)
+    slots, first = [], 0
+    for count in SPLIT:
+        assert first % count == 0
+        outgoing = named_frames(pick, keyval, first // count, 2 * HEAD * count)
+        slots.append(slots_exchange(outgoing))
+        first += count
     owns, passed, returned = [], [], []
     written, first = (), 0
-    for count in SPLIT:
+    for g, count in enumerate(SPLIT):
         *written, own_g, rim_g, dslot_g = attend(
-            read, add, bias, queries, grad_heads, keyval, before, slots, first, count, written
+            read, add, bias, queries, grad_heads, keyval, before, slots[g], first, count, written
         )
         passed.append(from_behind(rim_g, -1))
         returned.append(slots_exchange(dslot_g))

time: 431 us -> 435 us (level)
  local copies, waits for them, and re-layouts: 14.3 us -> 19.6 us
  waiting for transfers between devices: 208 us -> 203 us
    ppermute x3, waiting for transfers between devices: 120 us -> 72.3 us  [from_behind(): lax.ppermute(block, 'tm', [(i - distance, i) for i in range(BLOCKS) if 0...]
    all_to_all x6 -> x7, waiting for transfers between devices: 41.1 us -> 83.6 us  [exchange(): lax.all_to_all(x, axis, split_axis=0, concat_axis=0, tiled=True, axis_ind...]
    unnamed x60 -> x58, local copies, waits for them, and re-layouts: 8.43 us -> 11.9 us
    all_to_all x6 -> x7, starting transfers between devices: 47 us -> 47.3 us  [exchange(): lax.all_to_all(x, axis, split_axis=0, concat_axis=0, tiled=True, axis_ind...]
  transfers between devices with their start and end apart: 32 -> 33, of which waited for: 18 -> 17; matrix products, arithmetic and copies ran while one was open for 6% -> 6% of each run, Pallas kernels for 19% -> 22%
where the time goes in v3:
time: 435 us; the launch traced here: 433 us
  waiting for transfers between devices  203 us (47%)
  Pallas kernels  102 us (23%)
  starting transfers between devices  84.6 us (19%)
  local copies, waits for them, and re-layouts  19.6 us (5%)
  matrix products  13.6 us (3%)
  other arithmetic  9.46 us (2%)
    all_to_all x7, waiting for transfers between devices, exchange(): lax.all_to_all(x, axis, split_axis=0, concat_axis=0, tiled=True, axis_ind...  83.6 us
    ppermute x3, waiting for transfers between devices, from_behind(): lax.ppermute(block, 'tm', [(i - distance, i) for i in range(BLOCKS) if 0...  72.3 us
    all_to_all x7, starting transfers between devices, exchange(): lax.all_to_all(x, axis, split_axis=0, concat_axis=0, tiled=True, axis_ind...  47.3 us
    ppermute x18, waiting for transfers between devices, along_chips(): return lax.ppermute(x, 'roll', [(i, (i + 2 * d) % n) for i in range(n)])  46.6 us
    pallas_call x6, Pallas kernels, partial_call(): pl.pallas_call(body, grid_spec=pltpu.PrefetchScalarGridSpec(num_scalar_pr...  28.5 us
    pallas_call x2, Pallas kernels, attend(): pl.pallas_call(attend_body, grid_spec=pltpu.PrefetchScalarGridSpec(num_sc...  21.4 us
    ppermute x18, starting transfers between devices, along_chips(): return lax.ppermute(x, 'roll', [(i, (i + 2 * d) % n) for i in range(n)])  17.6 us
    ppermute x5, starting transfers between devices, other_core(): lax.ppermute(x, 'roll', [(i, i ^ 1) for i in range(lax.axis_size('roll'))])  13 us
  transfers between devices with their start and end apart: 33, of which 17 were waited for; matrix products, arithmetic and copies ran while one was open for 6% of the time, Pallas kernels for 22%

profile of v3, /device:TPU:1, one launch (start us, length us, event | category | flops | bytes accessed | tf_op | source)
XLA Modules:
  0.0 432.9 jit_solution(11447579401790450516)
XLA Ops:
  2.2 8.6 %all-to-all-start = ((s32[16,1,8]{2,1,0:T(1,128)}), s32[16,1,8]{2,1,0:T(1,128)S(1)}, u32[]{:S(2)}, u32[]{:S(2)}) async-start(s32[16,1,8]{2,1,0:T(1,128)} %bitcast.4), calls=%async_computation | async-start | bytes 16384 | tf_op jit(solution)/shard_map/all_to_all | solution.py:405
  10.8 6.6 %shard_map.118.kv_ref.own_ref = bf16[256,2048]{1,0:T(8,128)(2,1)} custom-call(bf16[256,2048]{1,0:T(8,128)(2,1)} %bitcast.40, bf16[2048,1024]{1,0:T(8,128)(2,1)} %wk_ref.5, bf16[2048,1024]{1,0:T(8,128)(2,1)} %wv_ref.5), custom_call_target="tpu_custom_call" | custom-call | tf_op jit(solution)/shard_map/pallas_call | solution.py:57
  22.3 6.7 %all-to-all-start.2 = ((bf16[16,96,1024]{2,1,0:T(8,128)(2,1)}), bf16[16,96,1024]{2,1,0:T(8,128)(2,1)S(1)}, u32[]{:S(2)}, u32[]{:S(2)}) async-start(bf16[16,96,1024]{2,1,0:T(8,128)(2,1)} %bitcast.39), calls=%async_computation.2 | async-start | bytes 6291456 | tf_op jit(solution)/shard_map/all_to_all | solution.py:405
  32.7 41.6 %all-to-all-done.2 = bf16[16,96,1024]{2,1,0:T(8,128)(2,1)S(1)} async-done(((bf16[16,96,1024]{2,1,0:T(8,128)(2,1)}), bf16[16,96,1024]{2,1,0:T(8,128)(2,1)S(1)}, u32[]{:S(2)}, u32[]{:S(2)}) %all-to-all-start.2) | async-done | bytes 3145760 | tf_op jit(solution)/shard_map/all_to_all | solution.py:405
  86.8 4.6 %convolution_convert_fusion.2.q_ref = bf16[256,1024]{1,0:T(8,128)(2,1)} fusion(bf16[256,2048]{1,0:T(8,128)(2,1)} %bitcast.41, bf16[2048,1024]{1,0:T(8,128)(2,1)} %wq_ref.1), kind=kOutput, calls=%fused_computation.2 | convolution fusion | flops 1074003968 | bytes 5767168 | tf_op jit(solution)/shard_map/dot_general | solution.py:544
  92.2 4.6 %convolution_convert_fusion.1.g_ref = bf16[256,1024]{1,0:T(8,128)(2,1)} fusion(bf16[256,2048]{1,0:T(8,128)(2,1)} %bitcast.43, bf16[1024,2048]{1,0:T(8,128)(2,1)} %param.13), kind=kOutput, calls=%fused_computation.1 | convolution fusion | flops 1074003968 | bytes 5767168 | tf_op jit(solution)/shard_map/dot_general | solution.py:36
  96.8 30.9 %collective-permute-done.x_ref = bf16[128,2048]{1,0:T(8,128)(2,1)} collective-permute-done((bf16[128,2048]{1,0:T(8,128)(2,1)}, bf16[128,2048]{1,0:T(8,128)(2,1)}, u32[]{:S(2)}, u32[]{:S(2)}) %collective-permute-start) | collective-permute-done | bytes 524320 | tf_op jit(solution)/shard_map/ppermute | solution.py:399
  127.7 5.7 %shard_map.119.prev_ref = bf16[128,2048]{1,0:T(8,128)(2,1)} custom-call(bf16[128,2048]{1,0:T(8,128)(2,1)} %collective-permute-done.x_ref, bf16[2048,1024]{1,0:T(8,128)(2,1)} %wk_ref.5, bf16[2048,1024]{1,0:T(8,128)(2,1)} %wv_ref.5), custom_call_target="tpu_custom_call" | custom-call | tf_op jit(solution)/shard_map/pallas_call | solution.py:57
  133.4 10.7 %shard_map.122 = (bf16[256,1024]{1,0:T(8,128)(2,1)}, bf16[256,1024]{1,0:T(8,128)(2,1)}, f32[256,1024]{1,0:T(8,128)}, bf16[128,1024]{1,0:T(8,128)(2,1)}, bf16[1536,1024]{1,0:T(8,128)(2,1)}) custom-call(s32[64]{0:T(128)} %get-tuple-element.67.read_ref, s32[64]{0:T(128)} %get-tuple-element.66.add_ref, f32[8,416]{1,0:T(8,128)} %reshape.118.bias_ref, ...), custom_call_target="tpu_custom_call" | custom-call | tf_op jit(solution)/shard_map/pallas_call | solution.py:165
  145.7 10.3 %all-to-all-start.3 = ((bf16[16,96,1024]{2,1,0:T(8,128)(2,1)}), bf16[16,96,1024]{2,1,0:T(8,128)(2,1)S(1)}, u32[]{:S(2)}, u32[]{:S(2)}) async-start(bf16[16,96,1024]{2,1,0:T(8,128)(2,1)} %bitcast.47), calls=%async_computation.3 | async-start | bytes 6291456 | tf_op jit(solution)/shard_map/all_to_all | solution.py:405
  156.0 10.7 %shard_map.123 = (bf16[256,1024]{1,0:T(8,128)(2,1)}, bf16[256,1024]{1,0:T(8,128)(2,1)}, f32[256,1024]{1,0:T(8,128)}, bf16[128,1024]{1,0:T(8,128)(2,1)}, bf16[1536,1024]{1,0:T(8,128)(2,1)}) custom-call(s32[64]{0:T(128)} %get-tuple-element.67.read_ref, s32[64]{0:T(128)} %get-tuple-element.66.add_ref, ...), custom_call_target="tpu_custom_call", output_to_operand_aliasing={{0}: (8, {}), {1}: (9, {})} | custom-call | tf_op jit(solution)/shard_map/pallas_call | solution.py:165
  166.8 30.8 %all-to-all-done.3 = bf16[16,96,1024]{2,1,0:T(8,128)(2,1)S(1)} async-done(((bf16[16,96,1024]{2,1,0:T(8,128)(2,1)}), bf16[16,96,1024]{2,1,0:T(8,128)(2,1)S(1)}, u32[]{:S(2)}, u32[]{:S(2)}) %all-to-all-start.3) | async-done | bytes 3145760 | tf_op jit(solution)/shard_map/all_to_all | solution.py:405
  197.6 6.0 %all-to-all-start.4 = ((bf16[16,96,1024]{2,1,0:T(8,128)(2,1)}), bf16[16,96,1024]{2,1,0:T(8,128)(2,1)}, u32[]{:S(2)}, u32[]{:S(2)}) async-start(bf16[16,96,1024]{2,1,0:T(8,128)(2,1)} %bitcast.46), calls=%async_computation.4 | async-start | bytes 6291456 | tf_op jit(solution)/shard_map/all_to_all | solution.py:405
  208.0 4.8 %shard_map.127 = bf16[4,16,256,128]{3,2,1,0:T(8,128)(2,1)} custom-call(s32[2]{0:T(128)} %pad_add_fusion.1.chip_ref, bf16[2048,256]{1,0:T(8,128)(2,1)} %bitcast.29, bf16[256,1024]{1,0:T(8,128)(2,1)} %get-tuple-element.39.dq_ref.refs_1_, bf16[256,1024]{1,0:T(8,128)(2,1)} %get-tuple-element.38.refs_2_, bf16[256,2048]{1,0:T(8,128)(2,1)} %bitcast.44), custom_call_target="tpu_custom_call" | custom-call | tf_op jit(solution)/shard_map/pallas_call | solution.py:351
  215.7 33.2 %collective-permute-done.1.rim_ref = bf16[128,1024]{1,0:T(8,128)(2,1)S(1)} collective-permute-done((bf16[128,1024]{1,0:T(8,128)(2,1)S(1)}, bf16[128,1024]{1,0:T(8,128)(2,1)S(1)}, u32[]{:S(2)}, u32[]{:S(2)}) %collective-permute-start.1) | collective-permute-done | bytes 262176 | tf_op jit(solution)/shard_map/ppermute | solution.py:399
  249.6 5.3 %shard_map.124.refs_0_.refs_1_ = bf16[2,256,512]{2,1,0:T(8,128)(2,1)} custom-call(s32[48]{0:T(128)} %broadcast_select_fusion.pick_ref, f32[256,1024]{1,0:T(8,128)} %get-tuple-element.40.own_ref, bf16[128,1024]{1,0:T(8,128)(2,1)} %copy-done.14, bf16[1536,1024]{1,0:T(8,128)(2,1)} %bitcast.35), custom_call_target="tpu_custom_call" | custom-call | tf_op jit(solution)/shard_map/pallas_call | solution.py:223
  262.9 8.3 %collective-permute-done.2.rim_ref = bf16[128,1024]{1,0:T(8,128)(2,1)S(1)} collective-permute-done((bf16[128,1024]{1,0:T(8,128)(2,1)S(1)}, bf16[128,1024]{1,0:T(8,128)(2,1)S(1)}, u32[]{:S(2)}, u32[]{:S(2)}) %collective-permute-start.2) | collective-permute-done | bytes 262176 | tf_op jit(solution)/shard_map/ppermute | solution.py:399
  271.9 5.2 %shard_map.125.refs_1_ = bf16[2,256,512]{2,1,0:T(8,128)(2,1)} custom-call(s32[48]{0:T(128)} %broadcast_select_fusion.pick_ref, f32[256,1024]{1,0:T(8,128)} %get-tuple-element.43.own_ref, bf16[128,1024]{1,0:T(8,128)(2,1)} %copy-done.15, bf16[1536,1024]{1,0:T(8,128)(2,1)} %bitcast.15.back_ref), custom_call_target="tpu_custom_call" | custom-call | tf_op jit(solution)/shard_map/pallas_call | solution.py:223
  283.5 4.7 %shard_map.134 = (bf16[8,128,128]{2,1,0:T(8,128)(2,1)}, bf16[8,128,128]{2,1,0:T(8,128)(2,1)}, bf16[8,128,128]{2,1,0:T(8,128)(2,1)}, bf16[8,128,128]{2,1,0:T(8,12...) custom-call(s32[2]{0:T(128)} %pad_add_fusion.chip_ref.s_ref, ...), custom_call_target="tpu_custom_call" | custom-call | tf_op jit(solution)/shard_map/pallas_call | solution.py:351
  292.2 5.4 %collective-permute-done.17 = bf16[8,128,128]{2,1,0:T(8,128)(2,1)S(1)} collective-permute-done((bf16[8,128,128]{2,1,0:T(8,128)(2,1)}, bf16[8,128,128]{2,1,0:T(8,128)(2,1)S(1)}, u32[]{:S(2)}, u32[]{:S(2)}) %collective-permute-start.17) | collective-permute-done | bytes 262176 | tf_op jit(solution)/shard_map/ppermute | solution.py:416
  306.0 5.6 %collective-permute-done.18.refs_5_ = bf16[8,128,128]{2,1,0:T(8,128)(2,1)S(1)} collective-permute-done((bf16[8,128,128]{2,1,0:T(8,128)(2,1)S(1)}, bf16[8,128,128]{2,1,0:T(8,128)(2,1)S(1)}, u32[]{:S(2)}, u32[]{:S(2)}) %collective-permute-start.18) | collective-permute-done | bytes 262176 | tf_op jit(solution)/shard_map/ppermute | solution.py:416
  312.4 4.7 %shard_map.135 = bf16[16,640,128]{2,1,0:T(8,128)(2,1)} custom-call(s32[2]{0:T(128)} %pad_add_fusion.chip_ref.s_ref, bf16[2048,256]{1,0:T(8,128)(2,1)} %bitcast.33, bf16[2,256,512]{2,1,0:T(8,128)(2,1)} %shard_map.125.refs_1_, bf16[16,512,128]{2,1,0:T(8,128)(2,1)} %collective-permute-done.14.refs_2_, bf16[8,128,128]{2,1,0:T(8,128)(2,1)} %get-tuple-element.55.refs_3_, ...), custom_call_target="tpu_custom_call" | custom-call | tf_op jit(solution)/shard_map/pallas_call | solution.py:351
  317.1 5.5 %all-to-all-start.6 = ((bf16[16,640,128]{2,1,0:T(8,128)(2,1)}), bf16[16,640,128]{2,1,0:T(8,128)(2,1)S(1)}, u32[]{:S(2)}, u32[]{:S(2)}) async-start(bf16[16,640,128]{2,1,0:T(8,128)(2,1)} %shard_map.135), calls=%async_computation.6 | async-start | bytes 5242880 | tf_op jit(solution)/shard_map/all_to_all | solution.py:405
  322.7 7.0 %shard_map.128 = (bf16[8,256,128]{2,1,0:T(8,128)(2,1)}, bf16[8,256,128]{2,1,0:T(8,128)(2,1)}, bf16[8,256,128]{2,1,0:T(8,128)(2,1)}, bf16[8,256,128]{2,1,0:T(8,12...) custom-call(s32[2]{0:T(128)} %pad_add_fusion.chip_ref.s_ref, ...), custom_call_target="tpu_custom_call" | custom-call | tf_op jit(solution)/shard_map/pallas_call | solution.py:351
  333.8 8.8 %collective-permute-done.5 = bf16[8,256,128]{2,1,0:T(8,128)(2,1)S(1)} collective-permute-done((bf16[8,256,128]{2,1,0:T(8,128)(2,1)}, bf16[8,256,128]{2,1,0:T(8,128)(2,1)S(1)}, u32[]{:S(2)}, u32[]{:S(2)}) %collective-permute-start.5) | collective-permute-done | bytes 524320 | tf_op jit(solution)/shard_map/ppermute | solution.py:416
  347.8 5.1 %collective-permute-done.4.refs_1_ = bf16[8,256,128]{2,1,0:T(8,128)(2,1)S(1)} collective-permute-done((bf16[8,256,128]{2,1,0:T(8,128)(2,1)}, bf16[8,256,128]{2,1,0:T(8,128)(2,1)S(1)}, u32[]{:S(2)}, u32[]{:S(2)}) %collective-permute-start.4) | collective-permute-done | bytes 524320 | tf_op jit(solution)/shard_map/ppermute | solution.py:416
  353.8 11.2 %collective-permute-done.6.refs_2_ = bf16[8,256,128]{2,1,0:T(8,128)(2,1)S(1)} collective-permute-done((bf16[8,256,128]{2,1,0:T(8,128)(2,1)S(1)}, bf16[8,256,128]{2,1,0:T(8,128)(2,1)S(1)}, u32[]{:S(2)}, u32[]{:S(2)}) %collective-permute-start.6) | collective-permute-done | bytes 524320 | tf_op jit(solution)/shard_map/ppermute | solution.py:416
  369.7 6.6 %all-to-all-start.5 = ((bf16[16,256,128]{2,1,0:T(8,128)(2,1)}), bf16[16,256,128]{2,1,0:T(8,128)(2,1)}, u32[]{:S(2)}, u32[]{:S(2)}) async-start(bf16[16,256,128]{2,1,0:T(8,128)(2,1)} %shard_map.129), calls=%async_computation.5 | async-start | bytes 2097152 | tf_op jit(solution)/shard_map/all_to_all | solution.py:405
  379.0 11.2 %all-to-all-done.5 = bf16[16,256,128]{2,1,0:T(8,128)(2,1)} async-done(((bf16[16,256,128]{2,1,0:T(8,128)(2,1)}), bf16[16,256,128]{2,1,0:T(8,128)(2,1)}, u32[]{:S(2)}, u32[]{:S(2)}) %all-to-all-start.5) | async-done | bytes 1048608 | tf_op jit(solution)/shard_map/all_to_all | solution.py:405
  402.1 6.9 %collective-permute-start.13 = (bf16[1024,128]{1,0:T(8,128)(2,1)}, bf16[1024,128]{1,0:T(8,128)(2,1)S(1)}, u32[]{:S(2)}, u32[]{:S(2)}) collective-permute-start(bf16[1024,128]{1,0:T(8,128)(2,1)} %shard_map.130.mine_ref), channel_id=1, source_target_pairs={{0,1},{1,0},{2,3},{3,2},{4,5},{5,4},{6,7},{7,6},{8,9},{9,8},{10,11... | collective-permute-start | bytes 786440 | tf_op jit(solution)/shard_map/ppermute | solution.py:395
  413.0 4.4 %convolution_convert_fusion = bf16[256,2048]{1,0:T(8,128)(2,1)} fusion(bf16[256,1024]{1,0:T(8,128)(2,1)S(1)} %copy-done.3, bf16[1024,2048]{1,0:T(8,128)(2,1)} %param.13), kind=kOutput, calls=%fused_computation | convolution fusion | flops 1074266112 | bytes 5767168 | tf_op jit(solution)/shard_map/dot_general | solution.py:594
  417.4 8.6 %shard_map.126 = bf16[256,2048]{1,0:T(8,128)(2,1)} custom-call(bf16[256,1024]{1,0:T(8,128)(2,1)} %get-tuple-element.39.dq_ref.refs_1_, bf16[2048,1024]{1,0:T(8,128)(2,1)} %wq_ref.1, bf16[2048,1024]{1,0:T(8,128)(2,1)} %wk_ref.5, bf16[2048,1024]{1,0:T(8,128)(2,1)} %wv_ref.5, bf16[2,256,512]{2,1,0:T(8,128)(2,1)} %shard_map.124.refs_0_.refs_1_, ...), custom_call_target="tpu_custom_call" | custom-call | tf_op jit(solution)/shard_map/pallas_call | solution.py:383
  (154 shorter events, 101.9 us)
Async XLA Ops:
  2.2 15.2 %all-to-all-start = ((s32[16,1,8]{2,1,0:T(1,128)}), s32[16,1,8]{2,1,0:T(1,128)S(1)}, u32[]{:S(2)}, u32[]{:S(2)}) async-start(s32[16,1,8]{2,1,0:T(1,128)} %bitcast.4), calls=%async_computation | async-start | bytes 16384 | tf_op jit(solution)/shard_map/all_to_all | solution.py:405
  22.3 52.0 %all-to-all-start.2 = ((bf16[16,96,1024]{2,1,0:T(8,128)(2,1)}), bf16[16,96,1024]{2,1,0:T(8,128)(2,1)S(1)}, u32[]{:S(2)}, u32[]{:S(2)}) async-start(bf16[16,96,1024]{2,1,0:T(8,128)(2,1)} %bitcast.39), calls=%async_computation.2 | async-start | bytes 6291456 | tf_op jit(solution)/shard_map/all_to_all | solution.py:405
  76.0 68.0 %all-to-all-start.1 = ((bf16[16,96,1024]{2,1,0:T(8,128)(2,1)}), bf16[16,96,1024]{2,1,0:T(8,128)(2,1)S(1)}, u32[]{:S(2)}, u32[]{:S(2)}) async-start(bf16[16,96,1024]{2,1,0:T(8,128)(2,1)} %bitcast.38), calls=%async_computation.1 | async-start | bytes 6291456 | tf_op jit(solution)/shard_map/all_to_all | solution.py:405
  81.7 46.0 %collective-permute-start = (bf16[128,2048]{1,0:T(8,128)(2,1)}, bf16[128,2048]{1,0:T(8,128)(2,1)}, u32[]{:S(2)}, u32[]{:S(2)}) collective-permute-start(bf16[128,2048]{1,0:T(8,128)(2,1)} %bitcast.3), channel_id=1, source_target_pairs={{0,8},{8,16},{16,24},{24,32},{32,40},{40,48},{48,56},{56,64},{64,7... | collective-permute-start | bytes 1572872 | tf_op jit(solution)/shard_map/ppermute | solution.py:399
  145.7 51.8 %all-to-all-start.3 = ((bf16[16,96,1024]{2,1,0:T(8,128)(2,1)}), bf16[16,96,1024]{2,1,0:T(8,128)(2,1)S(1)}, u32[]{:S(2)}, u32[]{:S(2)}) async-start(bf16[16,96,1024]{2,1,0:T(8,128)(2,1)} %bitcast.47), calls=%async_computation.3 | async-start | bytes 6291456 | tf_op jit(solution)/shard_map/all_to_all | solution.py:405
  197.6 73.6 %all-to-all-start.4 = ((bf16[16,96,1024]{2,1,0:T(8,128)(2,1)}), bf16[16,96,1024]{2,1,0:T(8,128)(2,1)}, u32[]{:S(2)}, u32[]{:S(2)}) async-start(bf16[16,96,1024]{2,1,0:T(8,128)(2,1)} %bitcast.46), calls=%async_computation.4 | async-start | bytes 6291456 | tf_op jit(solution)/shard_map/all_to_all | solution.py:405
  206.5 42.4 %collective-permute-start.1 = (bf16[128,1024]{1,0:T(8,128)(2,1)S(1)}, bf16[128,1024]{1,0:T(8,128)(2,1)S(1)}, u32[]{:S(2)}, u32[]{:S(2)}) collective-permute-start(bf16[128,1024]{1,0:T(8,128)(2,1)S(1)} %copy-done.28), channel_id=1, source_target_pairs={{8,0},{16,8},{24,16},{32,24},{40,32},{48,40},{56,48},{64,56},{72,6... | collective-permute-start | bytes 786440 | tf_op jit(solution)/shard_map/ppermute | solution.py:399
  212.8 109.9 %collective-permute-start.3 = (bf16[4,16,256,128]{3,2,1,0:T(8,128)(2,1)}, bf16[4,16,256,128]{3,2,1,0:T(8,128)(2,1)}, u32[]{:S(2)}, u32[]{:S(2)}) collective-permute-start(bf16[4,16,256,128]{3,2,1,0:T(8,128)(2,1)} %shard_map.127), channel_id=1, source_target_pairs={{0,1},{1,0},{2,3},{3,2},{4,5},{5,4},{6,7},{7,6},{8,9},{9,8},{10,11... | collective-permute-start | bytes 12582920 | tf_op jit(solution)/shard_map/ppermute | solution.py:395
  258.5 23.7 %collective-permute-start.15 = (bf16[4,16,128,128]{3,2,1,0:T(8,128)(2,1)}, bf16[4,16,128,128]{3,2,1,0:T(8,128)(2,1)S(1)}, u32[]{:S(2)}, u32[]{:S(2)}) collective-permute-start(bf16[4,16,128,128]{3,2,1,0:T(8,128)(2,1)} %shard_map.133), channel_id=1, source_target_pairs={{0,1},{1,0},{2,3},{3,2},{4,5},{5,4},{6,7},{7,6},{8,9},{9,8},{10,11... | collective-permute-start | bytes 6291464 | tf_op jit(solution)/shard_map/ppermute | solution.py:395
  261.4 9.7 %collective-permute-start.2 = (bf16[128,1024]{1,0:T(8,128)(2,1)S(1)}, bf16[128,1024]{1,0:T(8,128)(2,1)S(1)}, u32[]{:S(2)}, u32[]{:S(2)}) collective-permute-start(bf16[128,1024]{1,0:T(8,128)(2,1)S(1)} %copy-done.27), channel_id=1, source_target_pairs={{8,0},{16,8},{24,16},{32,24},{40,32},{48,40},{56,48},{64,56},{72,6... | collective-permute-start | bytes 786440 | tf_op jit(solution)/shard_map/ppermute | solution.py:399
  280.7 20.2 %collective-permute-start.14 = (bf16[16,512,128]{2,1,0:T(8,128)(2,1)}, bf16[16,512,128]{2,1,0:T(8,128)(2,1)}, u32[]{:S(2)}, u32[]{:S(2)}) collective-permute-start(bf16[16,512,128]{2,1,0:T(8,128)(2,1)} %shard_map.132), channel_id=1, source_target_pairs={{0,1},{1,0},{2,3},{3,2},{4,5},{5,4},{6,7},{7,6},{8,9},{9,8},{10,11... | collective-permute-start | bytes 6291464 | tf_op jit(solution)/shard_map/ppermute | solution.py:395
  288.2 9.3 %collective-permute-start.17 = (bf16[8,128,128]{2,1,0:T(8,128)(2,1)}, bf16[8,128,128]{2,1,0:T(8,128)(2,1)S(1)}, u32[]{:S(2)}, u32[]{:S(2)}) collective-permute-start(bf16[8,128,128]{2,1,0:T(8,128)(2,1)} %get-tuple-element.58), channel_id=1, source_target_pairs={{0,2},{1,3},{2,4},{3,5},{4,6},{5,7},{6,0},{7,1},{8,10},{9,11},{10,... | collective-permute-start | bytes 786440 | tf_op jit(solution)/shard_map/ppermute | solution.py:416
  289.4 9.1 %collective-permute-start.20 = (bf16[8,128,128]{2,1,0:T(8,128)(2,1)}, bf16[8,128,128]{2,1,0:T(8,128)(2,1)S(1)}, u32[]{:S(2)}, u32[]{:S(2)}) collective-permute-start(bf16[8,128,128]{2,1,0:T(8,128)(2,1)} %get-tuple-element.62), channel_id=1, source_target_pairs={{0,6},{1,7},{2,0},{3,1},{4,2},{5,3},{6,4},{7,5},{8,14},{9,15},{10,... | collective-permute-start | bytes 786440 | tf_op jit(solution)/shard_map/ppermute | solution.py:416
  290.9 11.9 %collective-permute-start.16 = (bf16[8,128,128]{2,1,0:T(8,128)(2,1)}, bf16[8,128,128]{2,1,0:T(8,128)(2,1)S(1)}, u32[]{:S(2)}, u32[]{:S(2)}) collective-permute-start(bf16[8,128,128]{2,1,0:T(8,128)(2,1)} %get-tuple-element.56), channel_id=1, source_target_pairs={{0,6},{1,7},{2,0},{3,1},{4,2},{5,3},{6,4},{7,5},{8,14},{9,15},{10,... | collective-permute-start | bytes 786440 | tf_op jit(solution)/shard_map/ppermute | solution.py:416
  297.5 8.4 %collective-permute-start.19 = (bf16[8,128,128]{2,1,0:T(8,128)(2,1)}, bf16[8,128,128]{2,1,0:T(8,128)(2,1)S(1)}, u32[]{:S(2)}, u32[]{:S(2)}) collective-permute-start(bf16[8,128,128]{2,1,0:T(8,128)(2,1)} %get-tuple-element.60), channel_id=1, source_target_pairs={{0,2},{1,3},{2,4},{3,5},{4,6},{5,7},{6,0},{7,1},{8,10},{9,11},{10,... | collective-permute-start | bytes 786440 | tf_op jit(solution)/shard_map/ppermute | solution.py:416
  298.6 13.0 %collective-permute-start.18 = (bf16[8,128,128]{2,1,0:T(8,128)(2,1)S(1)}, bf16[8,128,128]{2,1,0:T(8,128)(2,1)S(1)}, u32[]{:S(2)}, u32[]{:S(2)}) collective-permute-start(bf16[8,128,128]{2,1,0:T(8,128)(2,1)S(1)} %add_convert_fusion.3), channel_id=1, source_target_pairs={{0,2},{1,3},{2,4},{3,5},{4,6},{5,7},{6,0},{7,1},{8,10},{9,11},{10,... | collective-permute-start | bytes 786440 | tf_op jit(solution)/shard_map/ppermute | solution.py:416
  300.9 10.7 %collective-permute-start.21 = (bf16[8,128,128]{2,1,0:T(8,128)(2,1)S(1)}, bf16[8,128,128]{2,1,0:T(8,128)(2,1)S(1)}, u32[]{:S(2)}, u32[]{:S(2)}) collective-permute-start(bf16[8,128,128]{2,1,0:T(8,128)(2,1)S(1)} %add_convert_fusion.2), channel_id=1, source_target_pairs={{0,6},{1,7},{2,0},{3,1},{4,2},{5,3},{6,4},{7,5},{8,14},{9,15},{10,... | collective-permute-start | bytes 786440 | tf_op jit(solution)/shard_map/ppermute | solution.py:416
  317.1 52.6 %all-to-all-start.6 = ((bf16[16,640,128]{2,1,0:T(8,128)(2,1)}), bf16[16,640,128]{2,1,0:T(8,128)(2,1)S(1)}, u32[]{:S(2)}, u32[]{:S(2)}) async-start(bf16[16,640,128]{2,1,0:T(8,128)(2,1)} %shard_map.135), calls=%async_computation.6 | async-start | bytes 5242880 | tf_op jit(solution)/shard_map/all_to_all | solution.py:405
  329.6 13.0 %collective-permute-start.5 = (bf16[8,256,128]{2,1,0:T(8,128)(2,1)}, bf16[8,256,128]{2,1,0:T(8,128)(2,1)S(1)}, u32[]{:S(2)}, u32[]{:S(2)}) collective-permute-start(bf16[8,256,128]{2,1,0:T(8,128)(2,1)} %get-tuple-element.49), channel_id=1, source_target_pairs={{0,2},{1,3},{2,4},{3,5},{4,6},{5,7},{6,0},{7,1},{8,10},{9,11},{10,... | collective-permute-start | bytes 1572872 | tf_op jit(solution)/shard_map/ppermute | solution.py:416
  329.7 14.2 %collective-permute-start.8 = (bf16[8,256,128]{2,1,0:T(8,128)(2,1)}, bf16[8,256,128]{2,1,0:T(8,128)(2,1)S(1)}, u32[]{:S(2)}, u32[]{:S(2)}) collective-permute-start(bf16[8,256,128]{2,1,0:T(8,128)(2,1)} %get-tuple-element.53), channel_id=1, source_target_pairs={{0,6},{1,7},{2,0},{3,1},{4,2},{5,3},{6,4},{7,5},{8,14},{9,15},{10,... | collective-permute-start | bytes 1572872 | tf_op jit(solution)/shard_map/ppermute | solution.py:416
  332.4 20.5 %collective-permute-start.4 = (bf16[8,256,128]{2,1,0:T(8,128)(2,1)}, bf16[8,256,128]{2,1,0:T(8,128)(2,1)S(1)}, u32[]{:S(2)}, u32[]{:S(2)}) collective-permute-start(bf16[8,256,128]{2,1,0:T(8,128)(2,1)} %get-tuple-element.47), channel_id=1, source_target_pairs={{0,6},{1,7},{2,0},{3,1},{4,2},{5,3},{6,4},{7,5},{8,14},{9,15},{10,... | collective-permute-start | bytes 1572872 | tf_op jit(solution)/shard_map/ppermute | solution.py:416
  332.4 21.4 %collective-permute-start.7 = (bf16[8,256,128]{2,1,0:T(8,128)(2,1)}, bf16[8,256,128]{2,1,0:T(8,128)(2,1)S(1)}, u32[]{:S(2)}, u32[]{:S(2)}) collective-permute-start(bf16[8,256,128]{2,1,0:T(8,128)(2,1)} %get-tuple-element.51), channel_id=1, source_target_pairs={{0,2},{1,3},{2,4},{3,5},{4,6},{5,7},{6,0},{7,1},{8,10},{9,11},{10,... | collective-permute-start | bytes 1572872 | tf_op jit(solution)/shard_map/ppermute | solution.py:416
  343.8 21.3 %collective-permute-start.6 = (bf16[8,256,128]{2,1,0:T(8,128)(2,1)S(1)}, bf16[8,256,128]{2,1,0:T(8,128)(2,1)S(1)}, u32[]{:S(2)}, u32[]{:S(2)}) collective-permute-start(bf16[8,256,128]{2,1,0:T(8,128)(2,1)S(1)} %add_convert_fusion.1), channel_id=1, source_target_pairs={{0,2},{1,3},{2,4},{3,5},{4,6},{5,7},{6,0},{7,1},{8,10},{9,11},{10,... | collective-permute-start | bytes 1572872 | tf_op jit(solution)/shard_map/ppermute | solution.py:416
  345.0 20.0 %collective-permute-start.9 = (bf16[8,256,128]{2,1,0:T(8,128)(2,1)S(1)}, bf16[8,256,128]{2,1,0:T(8,128)(2,1)S(1)}, u32[]{:S(2)}, u32[]{:S(2)}) collective-permute-start(bf16[8,256,128]{2,1,0:T(8,128)(2,1)S(1)} %add_convert_fusion), channel_id=1, source_target_pairs={{0,6},{1,7},{2,0},{3,1},{4,2},{5,3},{6,4},{7,5},{8,14},{9,15},{10,... | collective-permute-start | bytes 1572872 | tf_op jit(solution)/shard_map/ppermute | solution.py:416
  369.7 20.5 %all-to-all-start.5 = ((bf16[16,256,128]{2,1,0:T(8,128)(2,1)}), bf16[16,256,128]{2,1,0:T(8,128)(2,1)}, u32[]{:S(2)}, u32[]{:S(2)}) async-start(bf16[16,256,128]{2,1,0:T(8,128)(2,1)} %shard_map.129), calls=%async_computation.5 | async-start | bytes 2097152 | tf_op jit(solution)/shard_map/all_to_all | solution.py:405
  376.7 32.4 %collective-permute-start.24 = (bf16[640,128]{1,0:T(8,128)(2,1)S(1)}, bf16[640,128]{1,0:T(8,128)(2,1)S(1)}, u32[]{:S(2)}, u32[]{:S(2)}) collective-permute-start(bf16[640,128]{1,0:T(8,128)(2,1)S(1)} %reduce_sum.45.refs_0_), channel_id=1, source_target_pairs={{0,6},{1,7},{2,0},{3,1},{4,2},{5,3},{6,4},{7,5},{8,14},{9,15},{10,... | collective-permute-start | bytes 491528 | tf_op jit(solution)/shard_map/ppermute | solution.py:416
  378.4 30.7 %collective-permute-start.23 = (bf16[640,128]{1,0:T(8,128)(2,1)S(1)}, bf16[640,128]{1,0:T(8,128)(2,1)S(1)}, u32[]{:S(2)}, u32[]{:S(2)}) collective-permute-start(bf16[640,128]{1,0:T(8,128)(2,1)S(1)} %reduce_sum.45.refs_0_), channel_id=1, source_target_pairs={{0,4},{1,5},{2,6},{3,7},{4,0},{5,1},{6,2},{7,3},{8,12},{9,13},{10,... | collective-permute-start | bytes 491528 | tf_op jit(solution)/shard_map/ppermute | solution.py:416
  378.4 30.7 %collective-permute-start.22 = (bf16[640,128]{1,0:T(8,128)(2,1)S(1)}, bf16[640,128]{1,0:T(8,128)(2,1)S(1)}, u32[]{:S(2)}, u32[]{:S(2)}) collective-permute-start(bf16[640,128]{1,0:T(8,128)(2,1)S(1)} %reduce_sum.45.refs_0_), channel_id=1, source_target_pairs={{0,2},{1,3},{2,4},{3,5},{4,6},{5,7},{6,0},{7,1},{8,10},{9,11},{10,... | collective-permute-start | bytes 491528 | tf_op jit(solution)/shard_map/ppermute | solution.py:416
  393.1 4.6 %collective-permute-start.11 = (bf16[256,128]{1,0:T(8,128)(2,1)S(1)}, bf16[256,128]{1,0:T(8,128)(2,1)S(1)}, u32[]{:S(2)}, u32[]{:S(2)}) collective-permute-start(bf16[256,128]{1,0:T(8,128)(2,1)S(1)} %reduce_sum.44.refs_0_), channel_id=1, source_target_pairs={{0,4},{1,5},{2,6},{3,7},{4,0},{5,1},{6,2},{7,3},{8,12},{9,13},{10,... | collective-permute-start | bytes 196616 | tf_op jit(solution)/shard_map/ppermute | solution.py:416
  394.8 4.3 collective-permute-start.10
  402.1 23.9 %collective-permute-start.13 = (bf16[1024,128]{1,0:T(8,128)(2,1)}, bf16[1024,128]{1,0:T(8,128)(2,1)S(1)}, u32[]{:S(2)}, u32[]{:S(2)}) collective-permute-start(bf16[1024,128]{1,0:T(8,128)(2,1)} %shard_map.130.mine_ref), channel_id=1, source_target_pairs={{0,1},{1,0},{2,3},{3,2},{4,5},{5,4},{6,7},{7,6},{8,9},{9,8},{10,11... | collective-permute-start | bytes 786440 | tf_op jit(solution)/shard_map/ppermute | solution.py:395
  413.0 16.4 %collective-permute-start.25 = (bf16[1024,128]{1,0:T(8,128)(2,1)}, bf16[1024,128]{1,0:T(8,128)(2,1)S(1)}, u32[]{:S(2)}, u32[]{:S(2)}) collective-permute-start(bf16[1024,128]{1,0:T(8,128)(2,1)} %shard_map.136.mine_ref), channel_id=1, source_target_pairs={{0,1},{1,0},{2,3},{3,2},{4,5},{5,4},{6,7},{7,6},{8,9},{9,8},{10,11... | collective-permute-start | bytes 786440 | tf_op jit(solution)/shard_map/ppermute | solution.py:395
  (30 other events, 238.9 us)
